TPU v7x, 32 devices: a whole 2x2x4 slice. The times are simulated.
32 devices in a mesh: gy: 8 (over z, core), gz: 4 (over y, x).
Axes of the slice: x: 2, y: 2, z: 4, core: 2. Of those that a mesh axis runs over, the one named last changes fastest.
Arguments:
- phase_field: float32 [128, 512, 1024], P('gz', 'gy'), may hold values from 0 to 1
- others: float32 [128, 512, 1024], P('gz', 'gy'), may hold values from 0 to 1
- cond_x: float32 [1023], replicated, may hold values from 256 to 4096
- cond_y: float32 [511], replicated, may hold values from 256 to 4096
- cond_z: float32 [127], replicated, may hold values from 64 to 1024
- inverse_x: float32 [1024, 1024], replicated, as said below
- inverse_y: float32 [512, 512], replicated
- inverse_z: float32 [128, 128], replicated
Outputs:
- grown: float32 [128, 512, 1024], P('gz', 'gy')
Inputs may be any that keep to these rules, and one draw needn't show every extreme that they name: inverse_x is the inverse of the 1024 x 1024 matrix I - 0.5 Lx, where Lx maps a line v to cond_x[i] (v[i+1] - v[i]) - cond_x[i-1] (v[i] - v[i-1]) with the missing edges at the ends left out; inverse_y and inverse_z are built likewise from cond_y and cond_z.
All inputs are finite; a program needn't handle non-finite values.
Results may differ from a plain program's by a relative error of at most 0.0003.
Values sent between devices are 32-bit elements; how exact they have to be, the bound alone decides.
No kernel may reach another device: no remote copies, remote signals or barrier semaphores. Data moves between devices by JAX's collectives and lax.ppermute only.
A program may use at most 128 MiB of HBM per device.

v0:
```python
import jax
import jax.numpy as jnp
from jax import lax
from jax.sharding import PartitionSpec as P

STEPS = 2


reaction_rate = 2.0


def padded_2(array, sides, width):
    for axis, dim in sides:
        size, length = (lax.axis_size(axis), array.shape[dim])
        up = [(i, (i + 1) % size) for i in range(size - 1)]
        down = [(j, i) for i, j in up]
        last = lax.slice_in_dim(array, length - width, length, axis=dim)
        first = lax.slice_in_dim(array, 0, width, axis=dim)
        before = lax.ppermute(last, axis, up)
        after = lax.ppermute(first, axis, down)
        array = jnp.concatenate([before, array, after], axis=dim)
    return array


def along_x(field, inverse):
    return jnp.einsum("zyx,wx->zyw", field, inverse, precision=lax.Precision.HIGHEST)


def along_y(field, inverse):
    return jnp.einsum("zyx,wy->zwx", field, inverse, precision=lax.Precision.HIGHEST)


def along_z(field, inverse):
    return jnp.einsum("zyx,wz->wyx", field, inverse, precision=lax.Precision.HIGHEST)


def stencil(field, cond_x, cond_y, cond_z):
    depth, rows, _ = field.shape
    padded = padded_2(field, (("gy", 1), ("gz", 0)), 1)
    weights_y = lax.dynamic_slice_in_dim(
        jnp.pad(cond_y, (1, 1)), lax.axis_index("gy") * rows, rows + 1
    )
    weights_z = lax.dynamic_slice_in_dim(
        jnp.pad(cond_z, (1, 1)), lax.axis_index("gz") * depth, depth + 1
    )
    core_y = padded[1:-1]
    core_z = padded[:, 1:-1]
    flux_x = jnp.pad(jnp.diff(field, axis=2) * cond_x, ((0, 0), (0, 0), (1, 1)))
    flux_y = (core_y[:, 1:, :] - core_y[:, :-1, :]) * weights_y[None, :, None]
    flux_z = (core_z[1:] - core_z[:-1]) * weights_z[:, None, None]
    total = flux_x[:, :, 1:] - flux_x[:, :, :-1]
    total = total + (flux_y[:, 1:, :] - flux_y[:, :-1, :])
    return total + (flux_z[1:] - flux_z[:-1])


def body(phase_field, others, cond_x, cond_y, cond_z, inverse_x, inverse_y, inverse_z):
    field = phase_field
    for step in range(STEPS):
        lap = stencil(field, cond_x, cond_y, cond_z)
        rhs = lap + reaction_rate * (field - field * field * field - 2.0 * field * others)
        moved = along_x(rhs, inverse_x)
        moved = lax.all_to_all(moved, "gz", split_axis=2, concat_axis=0, tiled=True)
        moved = along_z(moved, inverse_z)
        moved = lax.all_to_all(moved, "gy", split_axis=0, concat_axis=1, tiled=True)
        moved = along_y(moved, inverse_y)
        moved = lax.all_to_all(
            lax.all_to_all(moved, "gy", split_axis=1, concat_axis=0, tiled=True),
            "gz",
            split_axis=0,
            concat_axis=2,
            tiled=True,
        )
        field = field + moved
    return field


def solution(mesh):
    placed = (P("gz", "gy", None), P("gz", "gy", None), P(), P(), P(), P(), P(), P())
    return jax.shard_map(
        body, mesh=mesh, in_specs=placed, out_specs=P("gz", "gy", None), check_vma=False
    )
```

profile of v0, /device:TPU:0, one launch (start us, length us, event | category | flops | bytes accessed | tf_op | source)
XLA Modules:
  0.0 1681.9 jit_solution(9647709565455193330)
XLA Ops:
  0.0 1.8 fusion.46
  1.9 2.4 collective-permute-start.1
  4.3 1.3 collective-permute-start
  5.6 0.0 copy-start.4
  5.6 10.4 subtract_multiply_fusion
  16.0 0.1 pad_dynamic-slice_fusion.1
  16.0 0.1 pad_dynamic-slice_fusion
  16.1 1.1 pad_maximum_fusion.17
  17.2 1.3 collective-permute-start.2
  18.5 0.0 slice-start.2
  18.6 5.1 collective-permute-start.3
  23.7 11.3 fusion
  35.0 5.0 fusion.5
  40.0 39.8 %fusion.10 = f32[32,64,1024]{2,1,0:T(8,128)} fusion(f32[32,64,1023]{2,1,0:T(8,128)} %subtract_multiply_fusion, f32[32,64,1024]{2,1,0:T(8,128)} %param.8, f32[33,64,1024]{2,1,0:T(8,128)} %fusion.5, f32[32,65,1024]{2,1,0:T(8,128)} %fusion, f32[32,64,1024]{2,1,0:T(8,128)} %param.9, f32[1024,1024]{1,0:T(8,128)} %param.13), kind=kOutput, calls=%fused_computation.30 | convolution fusion | flops 25797066752 | bytes 71303168 | tf_op jit(solution)/shard_map/zyx,wx->zyw/dot_general | solution.py:26
  79.9 16.2 copy.61
  96.1 14.6 reshape.6
  110.6 100.8 %all_to_all.144 = f32[4,1,524288]{2,1,0:T(1,128)} all-to-all(f32[4,1,524288]{2,1,0:T(1,128)} %reshape.6), channel_id=1, replica_groups=mesh['gy'=8,'gz'=4] {'gz'}, dimensions={0} | all-to-all | bytes 16777216 | tf_op jit(solution)/shard_map/all_to_all | solution.py:62
  211.4 0.5 broadcast.23
  211.9 28.3 %reduce = f32[4,524288]{1,0:T(4,128)} reduce(f32[4,1,524288]{2,1,0:T(1,128)} %all_to_all.144, f32[]{:T(128)} %broadcast.23), dimensions={1}, to_apply=%all_to_all.104.reduce_sub_computation | reduce | bytes 16777220 | tf_op jit(solution)/shard_map/all_to_all | solution.py:62
  240.2 16.8 reshape.7
  257.0 22.6 %copy.85 = f32[32,64,4,256]{3,2,1,0:T(4,128)} copy(f32[32,64,4,256]{1,0,3,2:T(8,128)} %bitcast.72) | data formatting | bytes 16777216 | tf_op jit(solution)/shard_map/all_to_all | solution.py:62
  279.6 8.3 copy.89
  287.8 15.5 convolution_bitcast_fusion.3
  303.3 9.2 copy.65
  312.5 190.2 %all_to_all.145 = f32[128,64,256]{2,1,0:T(8,128)S(1)} all-to-all(f32[128,64,256]{2,1,0:T(8,128)} %copy.65), channel_id=1, replica_groups=mesh['gy'=8,'gz'=4] {'gy'}, dimensions={0} | all-to-all | bytes 16777216 | tf_op jit(solution)/shard_map/all_to_all | solution.py:64
  502.7 1.1 copy.66
  503.8 29.8 %convolution_bitcast_fusion.1 = f32[16,512,256]{1,2,0:T(8,128)} fusion(f32[16,512,256]{2,1,0:T(8,128)S(1)} %bitcast.75, f32[512,512]{1,0:T(8,128)S(1)} %copy-done), kind=kOutput, calls=%fused_computation.60 | convolution fusion | flops 12884901888 | bytes 17825792 | tf_op jit(solution)/shard_map/zyx,wy->zwx/dot_general | solution.py:30
  533.6 10.3 copy.68
  544.0 187.6 %all_to_all.146 = f32[16,512,256]{2,0,1:T(8,128)S(1)} all-to-all(f32[16,512,256]{2,0,1:T(8,128)} %copy.68), channel_id=1, replica_groups=mesh['gy'=8,'gz'=4] {'gy'}, dimensions={1} | all-to-all | bytes 16777216 | tf_op jit(solution)/shard_map/all_to_all | solution.py:67
  731.6 4.7 copy.70
  736.3 95.4 %all_to_all.147 = f32[128,64,256]{2,1,0:T(8,128)S(1)} all-to-all(f32[128,64,256]{2,1,0:T(8,128)S(1)} %bitcast.83), channel_id=1, replica_groups=mesh['gy'=8,'gz'=4] {'gz'}, dimensions={0} | all-to-all | bytes 16777216 | tf_op jit(solution)/shard_map/all_to_all | solution.py:66
  831.8 4.5 copy.91
  836.3 12.2 add.45
  848.4 1.8 fusion.45
  850.2 1.3 collective-permute-start.5
  851.5 0.0 slice-start.1
  851.5 1.6 collective-permute-start.4
  853.1 10.4 fusion.26
  863.5 0.1 pad_maximum_fusion.14
  863.6 1.3 collective-permute-start.6
  864.9 4.6 collective-permute-start.7
  869.5 5.1 fusion.1
  874.6 0.5 collective-permute-done.6
  875.1 1.7 collective-permute-done.7
  876.8 5.0 fusion.3
  881.9 39.9 %fusion.16 = f32[32,64,1024]{2,1,0:T(8,128)} fusion(f32[32,64,1023]{2,1,0:T(8,128)} %fusion.26, f32[32,64,1024]{2,1,0:T(8,128)} %add.45, f32[33,64,1024]{2,1,0:T(8,128)} %fusion.3, f32[32,65,1024]{2,1,0:T(8,128)} %fusion.1, f32[32,64,1024]{2,1,0:T(8,128)} %param.9, f32[1024,1024]{1,0:T(8,128)} %param.13), kind=kOutput, calls=%fused_computation.35 | convolution fusion | flops 25797066752 | bytes 71303168 | tf_op jit(solution)/shard_map/zyx,wx->zyw/dot_general | solution.py:26
  921.8 16.2 copy.72
  938.0 14.4 reshape.8
  952.3 105.0 %all_to_all.148 = f32[4,1,524288]{2,1,0:T(1,128)} all-to-all(f32[4,1,524288]{2,1,0:T(1,128)} %reshape.8), channel_id=1, replica_groups=mesh['gy'=8,'gz'=4] {'gz'}, dimensions={0} | all-to-all | bytes 16777216 | tf_op jit(solution)/shard_map/all_to_all | solution.py:62
  1057.4 28.1 %reduce.1 = f32[4,524288]{1,0:T(4,128)} reduce(f32[4,1,524288]{2,1,0:T(1,128)} %all_to_all.148, f32[]{:T(128)} %broadcast.23), dimensions={1}, to_apply=%all_to_all.120.reduce_sub_computation | reduce | bytes 16777220 | tf_op jit(solution)/shard_map/all_to_all | solution.py:62
  1085.5 16.8 reshape.9
  1102.3 13.2 copy.87
  1115.5 8.2 copy.90
  1123.7 15.5 convolution_bitcast_fusion.2
  1139.1 9.2 copy.76
  1148.3 187.8 %all_to_all.149 = f32[128,64,256]{2,1,0:T(8,128)S(1)} all-to-all(f32[128,64,256]{2,1,0:T(8,128)} %copy.76), channel_id=1, replica_groups=mesh['gy'=8,'gz'=4] {'gy'}, dimensions={0} | all-to-all | bytes 16777216 | tf_op jit(solution)/shard_map/all_to_all | solution.py:64
  1336.2 1.1 copy.77
  1337.3 29.6 %convolution_bitcast_fusion = f32[16,512,256]{1,2,0:T(8,128)} fusion(f32[16,512,256]{2,1,0:T(8,128)S(1)} %bitcast.76, f32[512,512]{1,0:T(8,128)S(1)} %copy-done), kind=kOutput, calls=%fused_computation.59 | convolution fusion | flops 12884901888 | bytes 17825792 | tf_op jit(solution)/shard_map/zyx,wy->zwx/dot_general | solution.py:30
  1366.9 10.3 copy.79
  1377.2 187.6 %all_to_all.150 = f32[16,512,256]{2,0,1:T(8,128)S(1)} all-to-all(f32[16,512,256]{2,0,1:T(8,128)} %copy.79), channel_id=1, replica_groups=mesh['gy'=8,'gz'=4] {'gy'}, dimensions={1} | all-to-all | bytes 16777216 | tf_op jit(solution)/shard_map/all_to_all | solution.py:67
  1564.8 4.7 copy.81
  1569.6 95.4 %all_to_all.151 = f32[128,64,256]{2,1,0:T(8,128)S(1)} all-to-all(f32[128,64,256]{2,1,0:T(8,128)S(1)} %bitcast.87), channel_id=1, replica_groups=mesh['gy'=8,'gz'=4] {'gz'}, dimensions={0} | all-to-all | bytes 16777216 | tf_op jit(solution)/shard_map/all_to_all | solution.py:66
  1665.0 4.3 copy.92
  1669.3 12.1 add.49
  (23 shorter events, 0.1 us)
Async XLA Ops:
  0.0 503.8 %copy-start = (f32[512,512]{1,0:T(8,128)S(1)}, f32[512,512]{1,0:T(8,128)}, u32[]{:S(2)}) copy-start(f32[512,512]{1,0:T(8,128)} %param.14) | copy-start | bytes 3145732
  1.9 14.3 collective-permute-start.1
  4.3 11.9 collective-permute-start
  5.6 10.4 copy-start.4
  5.6 10.5 copy-start.3
  17.2 17.7 %collective-permute-start.2 = (f32[1,66,1024]{2,1,0:T(8,128)S(1)}, f32[1,66,1024]{2,1,0:T(8,128)S(1)}, u32[]{:S(2)}, u32[]{:S(2)}) collective-permute-start(f32[1,66,1024]{2,1,0:T(8,128)S(1)} %get-tuple-element.7), channel_id=1, source_target_pairs={{1,0},{2,1},{3,2},{5,4},{6,5},{7,6},{9,8},{10,9},{11,10},{13,12},{... | collective-permute-start | bytes 811016 | tf_op jit(solution)/shard_map/ppermute | solution.py:20
  18.5 16.4 slice-start.2
  18.5 16.4 slice-start.3
  18.6 16.4 collective-permute-start.3
  279.6 8.3 copy-start.1
  836.3 16.8 %copy-start.2 = (f32[1023]{0:T(1024)S(1)}, f32[1023]{0:T(1024)}, u32[]{:S(2)}) copy-start(f32[1023]{0:T(1024)} %param.10) | copy-start | bytes 12280
  850.2 13.3 collective-permute-start.5
  851.5 12.0 slice-start
  851.5 12.0 slice-start.1
  851.5 12.0 collective-permute-start.4
  863.6 11.5 collective-permute-start.6
  864.9 11.9 collective-permute-start.7
where the time goes:
time: 1690 us; the launch traced here: 1680 us
  blocking collectives  1150 us (68%)
  local copies, waits for them, and re-layouts  211 us (12%)
  matrix products  170 us (10%)
  other arithmetic  129 us (8%)
  starting transfers between devices  18.8 us (1%)
    all_to_all x2, blocking collectives, body(): moved = lax.all_to_all(moved, 'gy', split_axis=0, concat_axis=1, tiled=True)  378 us
    all_to_all x2, blocking collectives, body(): lax.all_to_all(moved, 'gy', split_axis=1, concat_axis=0, tiled=True)  375 us
    all_to_all x2, blocking collectives, body(): moved = lax.all_to_all(moved, 'gz', split_axis=2, concat_axis=0, tiled=True)  206 us
    all_to_all x2, blocking collectives, body(): lax.all_to_all(lax.all_to_all(moved, 'gy', split_axis=1, concat_axis=0, t...  191 us
    dot_general x2, matrix products, along_x(): jnp.einsum('zyx,wx->zyw', field, inverse, precision=lax.Precision.HIGHEST)  79.8 us
    unnamed x22, local copies, waits for them, and re-layouts  62.5 us
    dot_general x2, matrix products, along_y(): jnp.einsum('zyx,wy->zwx', field, inverse, precision=lax.Precision.HIGHEST)  59.4 us
    all_to_all x2, other arithmetic, body(): moved = lax.all_to_all(moved, 'gz', split_axis=2, concat_axis=0, tiled=True)  56.4 us
  transfers between devices with their start and end apart: 8, of which 2 were waited for; matrix products, arithmetic and copies ran while one was open for 2% of the time, Pallas kernels for 0%

commit v1 on v0

v1 whole, which is shorter than its diff:
```python
import functools

import jax
import jax.numpy as jnp
from jax import lax
from jax.experimental import pallas as pl
from jax.experimental.pallas import tpu as pltpu
from jax.sharding import PartitionSpec as P

STEPS = 2
REACTION = 2.0
LANES = 128
SUB = 8
XB = 256
ZB = 8

f32 = jnp.float32
bf16 = jnp.bfloat16


def halves(a):
    high = lax.reduce_precision(a, 8, 7)
    low = a - high
    return high.astype(bf16), low.astype(bf16)


def split(a):
    high = a.astype(bf16)
    low = (a - high.astype(f32)).astype(bf16)
    return high, low


def wide(column, lanes=LANES):
    return jnp.broadcast_to(column[:, None], (column.shape[0], lanes))


def line_tables(inverse, axis, count):
    total = inverse.shape[0]
    parts = lax.axis_size(axis)
    me = lax.axis_index(axis)
    start = me * count
    before = jnp.maximum(start - 1, 0)
    after = jnp.minimum(start + count, total - 1)
    block = lax.dynamic_slice(inverse, (start, start), (count, count))
    eye = jnp.eye(count, dtype=f32)
    diag = jnp.sum(block * eye, axis=0)
    column = lax.dynamic_slice(inverse, (start, before), (count, 1))[:, 0]
    pivot = lax.dynamic_slice(inverse, (before, before), (1, 1))[0, 0]
    from_low = column / pivot
    column = lax.dynamic_slice(inverse, (start, after), (count, 1))[:, 0]
    pivot = lax.dynamic_slice(inverse, (after, after), (1, 1))[0, 0]
    from_high = column / pivot
    lasts = inverse[count - 1 :: count, count - 1 :: count]
    firsts = inverse[::count, ::count]
    unit = jnp.eye(parts, dtype=f32)
    carry_up = lasts / jnp.sum(lasts * unit, axis=0)[None, :]
    carry_down = firsts / jnp.sum(firsts * unit, axis=0)[None, :]
    return dict(
        block=block,
        diag=diag,
        from_low=from_low,
        from_high=from_high,
        carry_up=carry_up,
        carry_down=carry_down,
    )


def entry(table, i, j):
    n = table.shape[0]
    i = jnp.clip(i, 0, n - 1)
    j = jnp.clip(j, 0, n - 1)
    return lax.dynamic_slice(table, (i, j), (1, 1))[0, 0]


def cyclic(size, k, stride=1):
    groups = size // stride
    return [
        (c * stride + r, ((c + k) % groups) * stride + r)
        for c in range(groups)
        for r in range(stride)
    ]


def carries_direct(up, down, tables, axis):
    parts = lax.axis_size(axis)
    me = lax.axis_index(axis)
    low = jnp.zeros_like(up)
    high = jnp.zeros_like(up)
    got = []
    for k in range(1, parts):
        dest = (me + k) % parts
        got.append(lax.ppermute(jnp.where(dest > me, up, down), axis, cyclic(parts, k)))
    for k in range(1, parts):
        src = (me - k) % parts
        below = src < me
        a = jnp.where(below, entry(tables["carry_up"], me - 1, src), 0.0)
        b = jnp.where(below, 0.0, entry(tables["carry_down"], me + 1, src))
        low = low + a * got[k - 1]
        high = high + b * got[k - 1]
    return low, high


def carries_paired(both, tables, axis):
    parts = lax.axis_size(axis)
    me = lax.axis_index(axis)
    chips = parts // 2
    core = me % 2
    chip = me // 2
    half = both.shape[1] // 2
    up_t, down_t = tables["carry_up"], tables["carry_down"]
    even, odd = 2 * chip, 2 * chip + 1
    first, second = both[:, :half], both[:, half:]
    mine = jnp.where(core == 0, first, second)
    theirs = jnp.where(core == 0, second, first)
    swap = [(i, i ^ 1) for i in range(parts)]
    other = lax.ppermute(theirs, axis, swap)
    of_even = jnp.where(core == 0, mine, other)
    of_odd = jnp.where(core == 0, other, mine)
    up = of_odd[0] + entry(up_t, odd, even) * of_even[0]
    down = of_even[1] + entry(down_t, even, odd) * of_odd[1]
    got = []
    for k in range(1, chips):
        dest = (chip + k) % chips
        got.append(
            lax.ppermute(jnp.where(dest > chip, up, down), axis, cyclic(parts, k, 2))
        )
    low = jnp.zeros_like(up)
    high = jnp.zeros_like(up)
    for k in range(1, chips):
        src = (chip - k) % chips
        below = src < chip
        a = jnp.where(below, entry(up_t, even - 1, 2 * src + 1), 0.0)
        b = jnp.where(below, 0.0, entry(down_t, odd + 1, 2 * src))
        low = low + a * got[k - 1]
        high = high + b * got[k - 1]
    odd_low = of_even[0] + jnp.where(chip > 0, entry(up_t, even, even - 1), 0.0) * low
    even_high = (
        of_odd[1] + jnp.where(chip < chips - 1, entry(down_t, odd, odd + 1), 0.0) * high
    )
    for_even = jnp.stack([low, even_high])
    for_odd = jnp.stack([odd_low, high])
    keep = jnp.where(core == 0, for_even, for_odd)
    give = jnp.where(core == 0, for_odd, for_even)
    back = lax.ppermute(give, axis, swap)
    head = jnp.where(core == 0, keep, back)
    tail = jnp.where(core == 0, back, keep)
    whole = jnp.concatenate([head, tail], axis=1)
    return whole[0], whole[1]


def explicit_kernel(
    u_ref, below_ref, above_ref, o_ref, ylo_ref, yhi_ref, zlo_ref, zhi_ref,
    cx_ref, cup_ref, cdn_ref, cz_ref, wz_ref, ay_ref, axh_ref, axl_ref, xlo_ref, xhi_ref,
    t_ref, sy_ref, sz_ref, rhs_ref, line_ref,
):
    step = pl.program_id(0)
    steps = pl.num_programs(0)
    zb, rows, nx = u_ref.shape
    tiles = rows // SUB
    blocks = nx // XB
    sub = lax.broadcasted_iota(jnp.int32, (SUB, nx), 0)
    cx = cx_ref[...]

    def plane(z, carry):
        zz = step * zb + z
        c_up = cz_ref[zz + 1]
        c_dn = cz_ref[zz]

        def get(r):
            return u_ref[z, r * SUB : (r + 1) * SUB, :]

        low_row = ylo_ref[pl.ds(zz, 1), :]
        high_row = yhi_ref[pl.ds(zz, 1), :]
        before = jnp.broadcast_to(low_row, (SUB, nx))
        current = get(0)
        down_roll = pltpu.roll(current, 1, 0)
        for r in range(tiles):
            lane_rows = slice(r * SUB, (r + 1) * SUB)
            if r + 1 < tiles:
                following = get(r + 1)
                up_next = pltpu.roll(following, SUB - 1, 0)
                down_next = pltpu.roll(following, 1, 0)
            else:
                following = None
                up_next = jnp.broadcast_to(high_row, (SUB, nx))
                down_next = None
            c = current
            down = jnp.where(sub == 0, before, down_roll)
            up = jnp.where(sub == SUB - 1, up_next, pltpu.roll(c, SUB - 1, 0))
            fx = (pltpu.roll(c, nx - 1, 1) - c) * cx
            total = fx - pltpu.roll(fx, 1, 1)
            cup = jnp.concatenate([cup_ref[lane_rows, :]] * (nx // LANES), axis=1)
            cdn = jnp.concatenate([cdn_ref[lane_rows, :]] * (nx // LANES), axis=1)
            total = total + ((up - c) * cup - (c - down) * cdn)
            zdn = lax.select(
                z > 0,
                u_ref[jnp.maximum(z - 1, 0), lane_rows, :],
                lax.select(step > 0, below_ref[0, lane_rows, :], zlo_ref[lane_rows, :]),
            )
            zup = lax.select(
                z < zb - 1,
                u_ref[jnp.minimum(z + 1, zb - 1), lane_rows, :],
                lax.select(
                    step < steps - 1, above_ref[0, lane_rows, :], zhi_ref[lane_rows, :]
                ),
            )
            total = total + ((zup - c) * c_up - (c - zdn) * c_dn)
            o = o_ref[z, lane_rows, :]
            total = total + (REACTION * c) * (1.0 - c * c - 2.0 * o)
            rhs_ref[pl.ds(pl.multiple_of(z * rows + r * SUB, SUB), SUB), :] = total
            before = down_roll
            current = following
            down_roll = down_next
        return carry

    lax.fori_loop(0, zb, plane, 0)

    for e in range(blocks):
        cols = slice(e * XB, (e + 1) * XB)
        high, low = split(rhs_ref[:, cols])
        dot = functools.partial(jnp.dot, preferred_element_type=f32)
        line_ref[:, cols] = (
            dot(high, axh_ref[e]) + dot(low, axh_ref[e]) + dot(high, axl_ref[e])
        )
    lows = []
    w = None
    for e in range(blocks):
        end = line_ref[:, (e + 1) * XB - 1 : (e + 1) * XB]
        lows.append(w)
        if w is not None:
            end = end + w * xlo_ref[:, (e + 1) * XB - 1 : (e + 1) * XB]
        w = end
    highs = [None] * blocks
    w = None
    for e in reversed(range(blocks)):
        end = line_ref[:, e * XB : e * XB + 1]
        highs[e] = w
        if w is not None:
            end = end + w * xhi_ref[:, e * XB : e * XB + 1]
        w = end
    for e in range(blocks):
        cols = slice(e * XB, (e + 1) * XB)
        value = line_ref[:, cols]
        if lows[e] is not None:
            value = value + lows[e] * xlo_ref[:, cols]
        if highs[e] is not None:
            value = value + highs[e] * xhi_ref[:, cols]
        line_ref[:, cols] = value

    @pl.when(step == 0)
    def _():
        sz_ref[...] = jnp.zeros_like(sz_ref)

    def solve(z, carry):
        zz = step * zb + z
        base = pl.multiple_of(z * rows, rows)
        high, low = split(line_ref[pl.ds(base, rows), :])
        both = jnp.concatenate([high, low], axis=0)
        result = jnp.dot(ay_ref[...], both, preferred_element_type=f32)
        value = result[:rows] + result[rows:]
        t_ref[z] = value
        sy_ref[0, pl.ds(z, 1), :] = value[rows - 1 :]
        sy_ref[1, pl.ds(z, 1), :] = value[:1]
        sz_ref[0] = sz_ref[0] + wz_ref[0, zz] * value
        sz_ref[1] = sz_ref[1] + wz_ref[1, zz] * value
        return carry

    lax.fori_loop(0, zb, solve, 0)


def explicit(u, o, halos, tabs):
    nz, rows, nx = u.shape
    zb = ZB
    steps = nz // zb
    whole = lambda a: pl.BlockSpec(a.shape, lambda s: (0,) * a.ndim)
    smem = pl.BlockSpec(memory_space=pltpu.SMEM)
    field = pl.BlockSpec((zb, rows, nx), lambda s: (s, 0, 0))
    ylo, yhi, zlo, zhi = halos
    in_arrays = [
        (u, field),
        (u, pl.BlockSpec((1, rows, nx), lambda s: (jnp.maximum(s * zb - 1, 0), 0, 0))),
        (u, pl.BlockSpec((1, rows, nx), lambda s: (jnp.minimum(s * zb + zb, nz - 1), 0, 0))),
        (o, field),
        (ylo, whole(ylo)), (yhi, whole(yhi)), (zlo, whole(zlo)), (zhi, whole(zhi)),
        (tabs["cx"], whole(tabs["cx"])),
        (tabs["cup"], whole(tabs["cup"])),
        (tabs["cdn"], whole(tabs["cdn"])),
        (tabs["cz"], smem),
        (tabs["wz"], smem),
        (tabs["ay"], whole(tabs["ay"])),
        (tabs["axh"], whole(tabs["axh"])),
        (tabs["axl"], whole(tabs["axl"])),
        (tabs["xlo"], whole(tabs["xlo"])),
        (tabs["xhi"], whole(tabs["xhi"])),
    ]
    return pl.pallas_call(
        explicit_kernel,
        grid=(steps,),
        in_specs=[s for _, s in in_arrays],
        out_specs=[
            field,
            pl.BlockSpec((2, zb, nx), lambda s: (0, s, 0)),
            pl.BlockSpec((2, rows, nx), lambda s: (0, 0, 0)),
        ],
        out_shape=[
            jax.ShapeDtypeStruct(u.shape, f32),
            jax.ShapeDtypeStruct((2, nz, nx), f32),
            jax.ShapeDtypeStruct((2, rows, nx), f32),
        ],
        scratch_shapes=[
            pltpu.VMEM((zb * rows, nx), f32),
            pltpu.VMEM((zb * rows, nx), f32),
        ],
        compiler_params=pltpu.CompilerParams(
            dimension_semantics=("arbitrary",), vmem_limit_bytes=48 * 2**20
        ),
        name="explicit",
    )(*[a for a, _ in in_arrays])


def update_kernel(
    t_ref, u_ref, p_ref, q_ref, zl_ref, zr_ref, flo_ref, fhi_ref, coef_ref,
    out_ref, e_ref,
):
    nz, sub, nx = t_ref.shape
    lo = jnp.concatenate([flo_ref[...]] * (nx // LANES), axis=1)
    hi = jnp.concatenate([fhi_ref[...]] * (nx // LANES), axis=1)

    def forward(z, carry):
        v = t_ref[z] + lo * p_ref[pl.ds(z, 1), :] + hi * q_ref[pl.ds(z, 1), :]
        e = coef_ref[0, z] * v
        e_ref[z] = e
        s = carry + e
        out_ref[z] = u_ref[z] + s
        return coef_ref[1, z] * s

    lax.fori_loop(0, nz, forward, coef_ref[3, 0] * zl_ref[...], unroll=4)

    def backward(k, carry):
        z = nz - 1 - k
        out_ref[z] = out_ref[z] + carry
        return coef_ref[2, z] * (carry + e_ref[z])

    lax.fori_loop(0, nz, backward, coef_ref[3, 1] * zr_ref[...], unroll=4)


def update(t, u, p, q, zl, zr, tabs):
    nz, rows, nx = u.shape
    field = pl.BlockSpec((nz, SUB, nx), lambda r: (0, r, 0))
    flat = pl.BlockSpec((nz, nx), lambda r: (0, 0))
    tile = pl.BlockSpec((SUB, nx), lambda r: (r, 0))
    lane = pl.BlockSpec((SUB, LANES), lambda r: (r, 0))
    return pl.pallas_call(
        update_kernel,
        grid=(rows // SUB,),
        in_specs=[
            field, field, flat, flat, tile, tile, lane, lane,
            pl.BlockSpec(memory_space=pltpu.SMEM),
        ],
        out_specs=field,
        out_shape=jax.ShapeDtypeStruct(u.shape, f32),
        scratch_shapes=[pltpu.VMEM((nz, SUB, nx), f32)],
        compiler_params=pltpu.CompilerParams(
            dimension_semantics=("arbitrary",), vmem_limit_bytes=24 * 2**20
        ),
        name="update",
    )(t, u, p, q, zl, zr, tabs["flo"], tabs["fhi"], tabs["coef"])


def halo(u):
    ny, nz = lax.axis_size("gy"), lax.axis_size("gz")
    up = lambda n: [(i, i + 1) for i in range(n - 1)]
    down = lambda n: [(i + 1, i) for i in range(n - 1)]
    ylo = lax.ppermute(u[:, -1, :], "gy", up(ny))
    yhi = lax.ppermute(u[:, 0, :], "gy", down(ny))
    zlo = lax.ppermute(u[-1], "gz", up(nz))
    zhi = lax.ppermute(u[0], "gz", down(nz))
    return ylo, yhi, zlo, zhi


def x_tables(inverse):
    nx = inverse.shape[0]
    blocks = nx // XB
    diag = jnp.stack(
        [inverse[e * XB : (e + 1) * XB, e * XB : (e + 1) * XB].T for e in range(blocks)]
    )
    high, low = halves(diag)
    zero = jnp.zeros((XB,), f32)
    lows, highs = [zero], []
    for e in range(1, blocks):
        c = e * XB - 1
        lows.append(inverse[e * XB : (e + 1) * XB, c] / inverse[c, c])
    for e in range(blocks - 1):
        c = (e + 1) * XB
        highs.append(inverse[e * XB : (e + 1) * XB, c] / inverse[c, c])
    highs.append(zero)
    return high, low, jnp.concatenate(lows)[None], jnp.concatenate(highs)[None]


def body(phase_field, others, cond_x, cond_y, cond_z, inverse_x, inverse_y, inverse_z):
    depth, rows, nx = phase_field.shape
    ty = line_tables(inverse_y, "gy", rows)
    tz = line_tables(inverse_z, "gz", depth)
    y0 = lax.axis_index("gy") * rows
    z0 = lax.axis_index("gz") * depth
    ye = lax.dynamic_slice_in_dim(jnp.pad(cond_y, (1, 1)), y0, rows + 1)
    ze = lax.dynamic_slice_in_dim(jnp.pad(cond_z, (1, 1)), z0, depth + 1)
    axh, axl, xlo, xhi = x_tables(inverse_x)
    ah, al = halves(ty["block"])
    ay = jnp.concatenate(
        [
            jnp.concatenate([ah, ah], axis=1),
            jnp.concatenate([al, jnp.zeros_like(al)], axis=1),
        ],
        axis=0,
    )
    blk = tz["block"]
    shifted = jnp.eye(depth, k=-1, dtype=f32)
    ratio_up = jnp.sum(blk * shifted, axis=0) / tz["diag"]
    sup = jnp.sum(blk * shifted.T, axis=0) / tz["diag"]
    ends = jnp.pad(jnp.stack([tz["from_low"][0], tz["from_high"][-1]]), (0, depth - 2))
    tabs = dict(
        cx=jnp.broadcast_to(jnp.pad(cond_x, (0, 1))[None], (SUB, nx)),
        cup=wide(ye[1:]),
        cdn=wide(ye[:-1]),
        cz=ze,
        wz=jnp.stack([blk[-1], blk[0]]),
        ay=ay,
        axh=axh,
        axl=axl,
        xlo=xlo,
        xhi=xhi,
        flo=wide(ty["from_low"]),
        fhi=wide(ty["from_high"]),
        coef=jnp.stack([tz["diag"], ratio_up, sup, ends]),
    )
    u = phase_field
    for step in range(STEPS):
        t, sy, sz = explicit(u, others, halo(u), tabs)
        p, q = carries_paired(sy, ty, "gy")
        zl, zr = carries_direct(sz[0], sz[1], tz, "gz")
        pq = jnp.stack([p, q])
        up = jnp.sum(pq * tabs["wz"][0][None, :, None], axis=1)
        down = jnp.sum(pq * tabs["wz"][1][None, :, None], axis=1)
        cl, cr = carries_direct(up, down, tz, "gz")
        lo, hi = ty["from_low"][:, None], ty["from_high"][:, None]
        zl = zl + lo * cl[0] + hi * cl[1]
        zr = zr + lo * cr[0] + hi * cr[1]
        u = update(t, u, p, q, zl, zr, tabs)
    return u


def solution(mesh):
    placed = (P("gz", "gy", None), P("gz", "gy", None), P(), P(), P(), P(), P(), P())
    return jax.shard_map(
        body, mesh=mesh, in_specs=placed, out_specs=P("gz", "gy", None), check_vma=False
    )
```

time: 1690 us -> 231 us (0.14)
  blocking collectives: 1150 us -> 0 us
  local copies, waits for them, and re-layouts: 211 us -> 35.2 us
  matrix products: 170 us -> 0 us
  other arithmetic: 129 us -> 16.3 us
  Pallas kernels: 0 us -> 72.8 us
  waiting for transfers between devices: 2.24 us -> 39.9 us
  starting transfers between devices: 18.8 us -> 53.6 us
    all_to_all x8 -> x0, blocking collectives: 1150 us -> none  [the longest x2 378 us: body(): moved = lax.all_to_all(moved, 'gy', split_axis=0, concat_axis=1, tiled=True)]
    dot_general x6 -> x0, matrix products: 170 us -> none  [the longest x2 79.8 us: along_x(): jnp.einsum('zyx,wx->zyw', field, inverse, precision=lax.Precision.HIGHEST)]
    all_to_all x11 -> x0, local copies, waits for them, and re-layouts: 73.2 us -> none  [the longest x5 52.7 us: body(): moved = lax.all_to_all(moved, 'gz', split_axis=2, concat_axis=0, tiled=True)]
    pallas_call x0 -> x4, Pallas kernels: none -> 72.8 us  [the longest x2 57.3 us: explicit(): pl.pallas_call(explicit_kernel, grid=(steps,), in_specs=[s for _, s in in...]
    all_to_all x2 -> x0, other arithmetic: 56.4 us -> none  [body(): moved = lax.all_to_all(moved, 'gz', split_axis=2, concat_axis=0, tiled=True)]
    dot_general x4 -> x0, local copies, waits for them, and re-layouts: 50.7 us -> none  [the longest x2 32.4 us: along_x(): jnp.einsum('zyx,wx->zyw', field, inverse, precision=lax.Precision.HIGHEST)]
    mul x6 -> x0, other arithmetic: 47.2 us -> none  [the longest x2 20.8 us: stencil(): flux_x = jnp.pad(jnp.diff(field, axis=2) * cond_x, ((0, 0), (0, 0), (1, 1)))]
    unnamed x22 -> x42, local copies, waits for them, and re-layouts: 62.5 us -> 15.5 us
  transfers between devices with their start and end apart: 8 -> 30, of which waited for: 2 -> 11; matrix products, arithmetic and copies ran while one was open for 2% -> 14% of each run, Pallas kernels for 0% -> 0%
where the time goes in v1:
time: 231 us; the launch traced here: 230 us
  Pallas kernels  72.8 us (32%)
  starting transfers between devices  53.6 us (23%)
  waiting for transfers between devices  39.9 us (17%)
  local copies, waits for them, and re-layouts  35.2 us (15%)
  other arithmetic  16.3 us (7%)
  between operations  11.9 us (5%)
    pallas_call x2, Pallas kernels, explicit(): pl.pallas_call(explicit_kernel, grid=(steps,), in_specs=[s for _, s in in...  57.3 us
    ppermute x12, waiting for transfers between devices, carries_direct(): lax.ppermute(jnp.where(dest > me, up, down), axis, cyclic(parts, k))  27.5 us
    ppermute x12, starting transfers between devices, carries_direct(): lax.ppermute(jnp.where(dest > me, up, down), axis, cyclic(parts, k))  17.9 us
    unnamed x42, local copies, waits for them, and re-layouts  15.5 us
    pallas_call x2, Pallas kernels, update(): pl.pallas_call(update_kernel, grid=(rows // SUB,), in_specs=[field, field...  15.4 us
    ppermute x6, starting transfers between devices, carries_paired(): lax.ppermute(jnp.where(dest > chip, up, down), axis, cyclic(parts, k, 2))  11.2 us
    ppermute x2, starting transfers between devices, halo(): zlo = lax.ppermute(u[-1], 'gz', up(nz))  9.42 us
    ppermute x6, waiting for transfers between devices, carries_paired(): lax.ppermute(jnp.where(dest > chip, up, down), axis, cyclic(parts, k, 2))  7.61 us
  transfers between devices with their start and end apart: 30, of which 11 were waited for; matrix products, arithmetic and copies ran while one was open for 14% of the time, Pallas kernels for 0%

profile of v1, /device:TPU:0, one launch (start us, length us, event | category | flops | bytes accessed | tf_op | source)
XLA Modules:
  0.0 229.7 jit_solution(3599085620905069495)
XLA Ops:
  0.0 1.8 fusion.35
  2.4 2.4 %collective-permute-start = (f32[32,1024]{1,0:T(8,128)}, f32[32,1024]{1,0:T(8,128)S(1)}, u32[]{:S(2)}, u32[]{:S(2)}) collective-permute-start(f32[32,1024]{1,0:T(8,128)} %bitcast.164), channel_id=1, source_target_pairs={{0,4},{4,8},{8,12},{12,16},{16,20},{20,24},{24,28},{1,5},{5,9},{9,... | collective-permute-start | bytes 393224 | tf_op jit(solution)/shard_map/ppermute | solution.py:374
  5.5 1.3 collective-permute-start.1
  6.8 1.8 slice_bitcast_fusion.2
  8.6 1.3 collective-permute-start.3
  9.9 4.9 %collective-permute-start.2 = (f32[64,1024]{1,0:T(8,128)S(1)}, f32[64,1024]{1,0:T(8,128)S(1)}, u32[]{:S(2)}, u32[]{:S(2)}) collective-permute-start(f32[64,1024]{1,0:T(8,128)S(1)} %get-tuple-element.51), channel_id=1, source_target_pairs={{0,1},{1,2},{2,3},{4,5},{5,6},{6,7},{8,9},{9,10},{10,11},{12,13},{... | collective-permute-start | bytes 786440 | tf_op jit(solution)/shard_map/ppermute | solution.py:376
  14.7 0.9 slice.237
  15.7 0.9 slice.232
  16.6 1.3 slice.228
  17.9 1.3 slice.222
  19.1 1.4 fusion.36
  20.6 1.3 fusion.37
  21.9 0.8 pad_dynamic-slice_fusion
  23.3 0.8 fusion.40
  24.1 0.8 select_reduce_fusion.1
  27.4 0.8 reduce-precision_convert_fusion.1
  28.8 5.4 %fusion.12 = (f32[256]{0:T(256)S(1)}, f32[256]{0:T(256)S(1)}, f32[256]{0:T(256)S(1)}, f32[256]{0:T(256)S(1)}, f32[256]{0:T(256)S(1)}, /*index=5*/f32[256]{0:T(256)S(1)}) fusion(f32[1024,1024]{1,0:T(8,128)} %param.13, f32[]{:T(128)} %bitcast.16, f32[]{:T(128)} %bitcast.14, f32[]{:T(128)} %bitcast.13, f32[]{:T(128)} %bitcast.12, f32[]{:T(128)} %bitcast.17, ...), kind=kLoop, calls=%fused_computation.57 | loop fusion | flops 1536 | bytes 12312 | tf_op jit(solution)/shard_map/div | solution.py:395
  34.2 0.7 pad_dynamic-slice_fusion.1.cz_ref
  34.9 0.7 pad.17
  36.5 0.7 broadcast_in_dim.17.cup_ref
  37.4 28.4 %explicit.2 = (f32[32,64,1024]{2,1,0:T(8,128)}, f32[2,32,1024]{2,1,0:T(8,128)S(1)}, f32[2,64,1024]{2,1,0:T(8,128)S(1)}) custom-call(f32[32,64,1024]{2,1,0:T(8,128)} %u_ref.3, f32[32,64,1024]{2,1,0:T(8,128)} %u_ref.3, f32[32,64,1024]{2,1,0:T(8,128)} %u_ref.3, f32[32,64,1024]{2,1,0:T(8,128)} %o_ref.3, f32[32,1024]{1,0:T(8,128)S(1)} %collective-permute-done.ylo_ref, ...), custom_call_target="tpu_custom_call" | custom-call | tf_op jit(solution)/shard_map/explicit/pallas_call | solution.py:296
  65.8 2.5 %collective-permute-start.4 = (f32[2,16,1024]{2,1,0:T(8,128)S(1)}, f32[2,16,1024]{2,1,0:T(8,128)S(1)}, u32[]{:S(2)}, u32[]{:S(2)}) collective-permute-start(f32[2,16,1024]{2,1,0:T(8,128)S(1)} %slice_select_fusion.3), channel_id=1, source_target_pairs={{0,4},{4,0},{8,12},{12,8},{16,20},{20,16},{24,28},{28,24},{1,5},{5... | collective-permute-start | bytes 393224 | tf_op jit(solution)/shard_map/ppermute | solution.py:116
  72.7 0.7 fusion.45
  77.1 1.4 fusion.39
  82.4 1.4 fusion.38
  83.7 2.3 fusion.26
  86.1 1.2 broadcast_select_fusion.13
  87.3 2.5 %collective-permute-start.5 = (f32[16,1024]{1,0:T(8,128)S(1)}, f32[16,1024]{1,0:T(8,128)S(1)}, u32[]{:S(2)}, u32[]{:S(2)}) collective-permute-start(f32[16,1024]{1,0:T(8,128)S(1)} %get-tuple-element.43), channel_id=1, source_target_pairs={{0,8},{4,12},{8,16},{12,20},{16,24},{20,28},{24,0},{28,4},{1,9},{5... | collective-permute-start | bytes 196616 | tf_op jit(solution)/shard_map/ppermute | solution.py:125
  89.9 2.7 %collective-permute-start.6 = (f32[16,1024]{1,0:T(8,128)S(1)}, f32[16,1024]{1,0:T(8,128)S(1)}, u32[]{:S(2)}, u32[]{:S(2)}) collective-permute-start(f32[16,1024]{1,0:T(8,128)S(1)} %get-tuple-element.98), channel_id=1, source_target_pairs={{0,16},{4,20},{8,24},{12,28},{16,0},{20,4},{24,8},{28,12},{1,17},{... | collective-permute-start | bytes 196616 | tf_op jit(solution)/shard_map/ppermute | solution.py:125
  92.5 1.3 collective-permute-start.7
  94.5 2.8 %collective-permute-done.6 = f32[16,1024]{1,0:T(8,128)S(1)} collective-permute-done((f32[16,1024]{1,0:T(8,128)S(1)}, f32[16,1024]{1,0:T(8,128)S(1)}, u32[]{:S(2)}, u32[]{:S(2)}) %collective-permute-start.6) | collective-permute-done | bytes 65568 | tf_op jit(solution)/shard_map/ppermute | solution.py:125
  97.7 2.4 %collective-permute-start.9 = (f32[64,1024]{1,0:T(8,128)S(1)}, f32[64,1024]{1,0:T(8,128)S(1)}, u32[]{:S(2)}, u32[]{:S(2)}) collective-permute-start(f32[64,1024]{1,0:T(8,128)S(1)} %get-tuple-element.77), channel_id=1, source_target_pairs={{0,1},{1,2},{2,3},{3,0},{4,5},{5,6},{6,7},{7,4},{8,9},{9,10},{10,1... | collective-permute-start | bytes 786440 | tf_op jit(solution)/shard_map/ppermute | solution.py:92
  100.9 1.5 collective-permute-start.12
  102.4 1.5 collective-permute-start.14
  103.9 1.5 collective-permute-start.13
  105.4 7.8 %collective-permute-done.12 = f32[2,1024]{1,0:T(2,128)S(1)} collective-permute-done((f32[2,1024]{1,0:T(2,128)S(1)}, f32[2,1024]{1,0:T(2,128)S(1)}, u32[]{:S(2)}, u32[]{:S(2)}) %collective-permute-start.12) | collective-permute-done | bytes 8224 | tf_op jit(solution)/shard_map/ppermute | solution.py:92
  113.3 1.5 collective-permute-start.10
  114.8 5.9 %collective-permute-done.10 = f32[64,1024]{1,0:T(8,128)S(1)} collective-permute-done((f32[64,1024]{1,0:T(8,128)S(1)}, f32[64,1024]{1,0:T(8,128)S(1)}, u32[]{:S(2)}, u32[]{:S(2)}) %collective-permute-start.10) | collective-permute-done | bytes 262176 | tf_op jit(solution)/shard_map/ppermute | solution.py:92
  121.1 3.4 %copy-done.2 = f32[32,64,1024]{2,1,0:T(8,128)S(1)} copy-done((f32[32,64,1024]{2,1,0:T(8,128)S(1)}, f32[32,64,1024]{2,1,0:T(8,128)}, u32[]{:S(2)}) %copy-start.2) | copy-done | bytes 8388632
  124.5 3.4 %copy-done.3 = f32[32,64,1024]{2,1,0:T(8,128)S(1)} copy-done((f32[32,64,1024]{2,1,0:T(8,128)S(1)}, f32[32,64,1024]{2,1,0:T(8,128)}, u32[]{:S(2)}) %copy-start.3) | copy-done | bytes 8388632
  127.9 7.3 %update.2.u_ref.below_ref.above_ref = f32[32,64,1024]{2,1,0:T(8,128)S(1)} custom-call(f32[32,64,1024]{2,1,0:T(8,128)S(1)} %copy-done.3, f32[32,64,1024]{2,1,0:T(8,128)S(1)} %copy-done.2, f32[32,1024]{1,0:T(8,128)S(1)} %get-tuple-element.91.p_ref, f32[32,1024]{1,0:T(8,128)S(1)} %get-tuple-element.90.q_ref, f32[64,1024]{1,0:T(8,128)S(1)} %get-tuple-element.73.zl_ref, ...), custom_call_target="tpu_custom_call" | custom-call | tf_op jit(solution)/shard_map/update/pallas_call | solution.py:353
  135.2 1.3 collective-permute-start.18
  136.5 4.6 %collective-permute-start.17 = (f32[64,1024]{1,0:T(8,128)S(1)}, f32[64,1024]{1,0:T(8,128)S(1)}, u32[]{:S(2)}, u32[]{:S(2)}) collective-permute-start(f32[64,1024]{1,0:T(8,128)S(1)} %get-tuple-element.47), channel_id=1, source_target_pairs={{0,1},{1,2},{2,3},{4,5},{5,6},{6,7},{8,9},{9,10},{10,11},{12,13},{... | collective-permute-start | bytes 786440 | tf_op jit(solution)/shard_map/ppermute | solution.py:376
  141.4 1.3 collective-permute-start.15
  142.7 1.3 collective-permute-start.16
  144.0 3.8 %collective-permute-done.16.yhi_ref = f32[32,1024]{1,0:T(8,128)S(1)} collective-permute-done((f32[32,1024]{1,0:T(8,128)S(1)}, f32[32,1024]{1,0:T(8,128)S(1)}, u32[]{:S(2)}, u32[]{:S(2)}) %collective-permute-start.16) | collective-permute-done | bytes 131104 | tf_op jit(solution)/shard_map/ppermute | solution.py:375
  147.8 28.9 %explicit.3 = (f32[32,64,1024]{2,1,0:T(8,128)}, f32[2,32,1024]{2,1,0:T(8,128)S(1)}, f32[2,64,1024]{2,1,0:T(8,128)S(1)}) custom-call(f32[32,64,1024]{2,1,0:T(8,128)} %copy-done, f32[32,64,1024]{2,1,0:T(8,128)} %copy-done, f32[32,64,1024]{2,1,0:T(8,128)} %copy-done, f32[32,64,1024]{2,1,0:T(8,128)} %o_ref.3, f32[32,1024]{1,0:T(8,128)S(1)} %collective-permute-done.15.ylo_ref, ...), custom_call_target="tpu_custom_call" | custom-call | tf_op jit(solution)/shard_map/explicit/pallas_call | solution.py:296
  176.7 3.6 %collective-permute-start.19 = (f32[2,16,1024]{2,1,0:T(8,128)S(1)}, f32[2,16,1024]{2,1,0:T(8,128)S(1)}, u32[]{:S(2)}, u32[]{:S(2)}) collective-permute-start(f32[2,16,1024]{2,1,0:T(8,128)S(1)} %slice_select_fusion.1), channel_id=1, source_target_pairs={{0,4},{4,0},{8,12},{12,8},{16,20},{20,16},{24,28},{28,24},{1,5},{5... | collective-permute-start | bytes 393224 | tf_op jit(solution)/shard_map/ppermute | solution.py:116
  180.3 1.0 collective-permute-done.19
  181.3 1.2 broadcast_select_fusion.12
  182.7 1.7 collective-permute-start.21
  184.5 2.8 %collective-permute-start.22 = (f32[16,1024]{1,0:T(8,128)S(1)}, f32[16,1024]{1,0:T(8,128)S(1)}, u32[]{:S(2)}, u32[]{:S(2)}) collective-permute-start(f32[16,1024]{1,0:T(8,128)S(1)} %get-tuple-element.97), channel_id=1, source_target_pairs={{0,24},{4,28},{8,0},{12,4},{16,8},{20,12},{24,16},{28,20},{1,25},{... | collective-permute-start | bytes 196616 | tf_op jit(solution)/shard_map/ppermute | solution.py:125
  187.3 2.2 collective-permute-done.20
  189.5 1.8 collective-permute-done.21
  191.5 2.4 %collective-permute-start.24 = (f32[64,1024]{1,0:T(8,128)S(1)}, f32[64,1024]{1,0:T(8,128)S(1)}, u32[]{:S(2)}, u32[]{:S(2)}) collective-permute-start(f32[64,1024]{1,0:T(8,128)S(1)} %get-tuple-element.74), channel_id=1, source_target_pairs={{0,1},{1,2},{2,3},{3,0},{4,5},{5,6},{6,7},{7,4},{8,9},{9,10},{10,1... | collective-permute-start | bytes 786440 | tf_op jit(solution)/shard_map/ppermute | solution.py:92
  194.7 1.5 collective-permute-start.27
  196.2 1.5 collective-permute-start.29
  197.7 1.5 collective-permute-start.28
  199.2 7.9 %collective-permute-done.27 = f32[2,1024]{1,0:T(2,128)S(1)} collective-permute-done((f32[2,1024]{1,0:T(2,128)S(1)}, f32[2,1024]{1,0:T(2,128)S(1)}, u32[]{:S(2)}, u32[]{:S(2)}) %collective-permute-start.27) | collective-permute-done | bytes 8224 | tf_op jit(solution)/shard_map/ppermute | solution.py:92
  207.0 1.5 collective-permute-start.25
  208.6 5.9 %collective-permute-done.25 = f32[64,1024]{1,0:T(8,128)S(1)} collective-permute-done((f32[64,1024]{1,0:T(8,128)S(1)}, f32[64,1024]{1,0:T(8,128)S(1)}, u32[]{:S(2)}, u32[]{:S(2)}) %collective-permute-start.25) | collective-permute-done | bytes 262176 | tf_op jit(solution)/shard_map/ppermute | solution.py:92
  214.7 3.4 %copy-done.1 = f32[32,64,1024]{2,1,0:T(8,128)S(1)} copy-done((f32[32,64,1024]{2,1,0:T(8,128)S(1)}, f32[32,64,1024]{2,1,0:T(8,128)}, u32[]{:S(2)}) %copy-start.1) | copy-done | bytes 8388632
  218.1 3.4 %copy-done.4 = f32[32,64,1024]{2,1,0:T(8,128)S(1)} copy-done((f32[32,64,1024]{2,1,0:T(8,128)S(1)}, f32[32,64,1024]{2,1,0:T(8,128)}, u32[]{:S(2)}) %copy-start.4) | copy-done | bytes 8388632
  221.5 8.2 %update.3 = f32[32,64,1024]{2,1,0:T(8,128)} custom-call(f32[32,64,1024]{2,1,0:T(8,128)S(1)} %copy-done.4, f32[32,64,1024]{2,1,0:T(8,128)S(1)} %copy-done.1, f32[32,1024]{1,0:T(8,128)S(1)} %get-tuple-element.89.p_ref, f32[32,1024]{1,0:T(8,128)S(1)} %get-tuple-element.88.q_ref, f32[64,1024]{1,0:T(8,128)S(1)} %get-tuple-element.71.zl_ref, ...), custom_call_target="tpu_custom_call" | custom-call | tf_op jit(solution)/shard_map/update/pallas_call | solution.py:353
  (117 shorter events, 10.7 us)
Async XLA Ops:
  2.4 34.0 %collective-permute-start = (f32[32,1024]{1,0:T(8,128)}, f32[32,1024]{1,0:T(8,128)S(1)}, u32[]{:S(2)}, u32[]{:S(2)}) collective-permute-start(f32[32,1024]{1,0:T(8,128)} %bitcast.164), channel_id=1, source_target_pairs={{0,4},{4,8},{8,12},{12,16},{16,20},{20,24},{24,28},{1,5},{5,9},{9,... | collective-permute-start | bytes 393224 | tf_op jit(solution)/shard_map/ppermute | solution.py:374
  5.5 30.9 %collective-permute-start.1 = (f32[32,1024]{1,0:T(8,128)}, f32[32,1024]{1,0:T(8,128)S(1)}, u32[]{:S(2)}, u32[]{:S(2)}) collective-permute-start(f32[32,1024]{1,0:T(8,128)} %bitcast.163), channel_id=1, source_target_pairs={{4,0},{8,4},{12,8},{16,12},{20,16},{24,20},{28,24},{5,1},{9,5},{13... | collective-permute-start | bytes 393224 | tf_op jit(solution)/shard_map/ppermute | solution.py:375
  8.6 27.9 %collective-permute-start.3 = (f32[64,1024]{1,0:T(8,128)}, f32[64,1024]{1,0:T(8,128)S(1)}, u32[]{:S(2)}, u32[]{:S(2)}) collective-permute-start(f32[64,1024]{1,0:T(8,128)} %get-tuple-element.50), channel_id=1, source_target_pairs={{1,0},{2,1},{3,2},{5,4},{6,5},{7,6},{9,8},{10,9},{11,10},{13,12},{... | collective-permute-start | bytes 786440 | tf_op jit(solution)/shard_map/ppermute | solution.py:377
  9.9 26.6 %collective-permute-start.2 = (f32[64,1024]{1,0:T(8,128)S(1)}, f32[64,1024]{1,0:T(8,128)S(1)}, u32[]{:S(2)}, u32[]{:S(2)}) collective-permute-start(f32[64,1024]{1,0:T(8,128)S(1)} %get-tuple-element.51), channel_id=1, source_target_pairs={{0,1},{1,2},{2,3},{4,5},{5,6},{6,7},{8,9},{9,10},{10,11},{12,13},{... | collective-permute-start | bytes 786440 | tf_op jit(solution)/shard_map/ppermute | solution.py:376
  24.1 12.2 %copy-start.7 = (f32[1,32]{1,0:T(1,128)}, f32[1,32]{1,0:T(1,128)S(1)}, u32[]{:S(2)}) copy-start(f32[1,32]{1,0:T(1,128)S(1)} %get-tuple-element.104) | copy-start | bytes 388
  24.1 12.2 %copy-start.9 = (f32[1,32]{1,0:T(1,128)}, f32[1,32]{1,0:T(1,128)S(1)}, u32[]{:S(2)}) copy-start(f32[1,32]{1,0:T(1,128)S(1)} %get-tuple-element.105) | copy-start | bytes 388
  24.9 11.3 %copy-start.13 = (f32[32]{0:T(128)}, f32[32]{0:T(128)S(1)}, u32[]{:S(2)}) copy-start(f32[32]{0:T(128)S(1)} %get-tuple-element.31) | copy-start | bytes 388
  37.3 31.0 %copy-start.11 = (f32[4,4]{1,0:T(4,128)S(1)}, f32[4,4]{1,0:T(4,128)}, u32[]{:S(2)}) copy-start(f32[4,4]{1,0:T(4,128)} %broadcast_divide_fusion.2) | copy-start | bytes 196
  37.3 31.0 %copy-start.12 = (f32[4,4]{1,0:T(4,128)S(1)}, f32[4,4]{1,0:T(4,128)}, u32[]{:S(2)}) copy-start(f32[4,4]{1,0:T(4,128)} %broadcast_divide_fusion.3) | copy-start | bytes 196
  37.3 35.4 %copy-start.5 = (f32[8,8]{1,0:T(8,128)S(1)}, f32[8,8]{1,0:T(8,128)}, u32[]{:S(2)}) copy-start(f32[8,8]{1,0:T(8,128)} %broadcast_divide_fusion) | copy-start | bytes 772
  37.3 35.4 %copy-start.6 = (f32[8,8]{1,0:T(8,128)S(1)}, f32[8,8]{1,0:T(8,128)}, u32[]{:S(2)}) copy-start(f32[8,8]{1,0:T(8,128)} %broadcast_divide_fusion.1) | copy-start | bytes 772
  37.3 56.6 %copy-start.14 = (f32[32]{0:T(128)S(1)}, f32[32]{0:T(128)}, u32[]{:S(2)}) copy-start(f32[32]{0:T(128)} %copy-done.13) | copy-start | bytes 388
  37.3 56.5 %copy-start.15 = (f32[1,32]{1,0:T(1,128)S(1)}, f32[1,32]{1,0:T(1,128)}, u32[]{:S(2)}) copy-start(f32[1,32]{1,0:T(1,128)} %get-tuple-element.142) | copy-start | bytes 388
  37.3 56.5 %copy-start.16 = (f32[1,32]{1,0:T(1,128)S(1)}, f32[1,32]{1,0:T(1,128)}, u32[]{:S(2)}) copy-start(f32[1,32]{1,0:T(1,128)} %get-tuple-element.143) | copy-start | bytes 388
  37.3 63.4 %copy-start.8 = (f32[1,32]{1,0:T(1,128)S(1)}, f32[1,32]{1,0:T(1,128)}, u32[]{:S(2)}) copy-start(f32[1,32]{1,0:T(1,128)} %copy-done.7) | copy-start | bytes 388
  37.4 63.4 %copy-start.10 = (f32[1,32]{1,0:T(1,128)S(1)}, f32[1,32]{1,0:T(1,128)}, u32[]{:S(2)}) copy-start(f32[1,32]{1,0:T(1,128)} %copy-done.9) | copy-start | bytes 388
  65.8 20.3 %collective-permute-start.4 = (f32[2,16,1024]{2,1,0:T(8,128)S(1)}, f32[2,16,1024]{2,1,0:T(8,128)S(1)}, u32[]{:S(2)}, u32[]{:S(2)}) collective-permute-start(f32[2,16,1024]{2,1,0:T(8,128)S(1)} %slice_select_fusion.3), channel_id=1, source_target_pairs={{0,4},{4,0},{8,12},{12,8},{16,20},{20,16},{24,28},{28,24},{1,5},{5... | collective-permute-start | bytes 393224 | tf_op jit(solution)/shard_map/ppermute | solution.py:116
  87.3 7.2 %collective-permute-start.5 = (f32[16,1024]{1,0:T(8,128)S(1)}, f32[16,1024]{1,0:T(8,128)S(1)}, u32[]{:S(2)}, u32[]{:S(2)}) collective-permute-start(f32[16,1024]{1,0:T(8,128)S(1)} %get-tuple-element.43), channel_id=1, source_target_pairs={{0,8},{4,12},{8,16},{12,20},{16,24},{20,28},{24,0},{28,4},{1,9},{5... | collective-permute-start | bytes 196616 | tf_op jit(solution)/shard_map/ppermute | solution.py:125
  89.9 7.4 %collective-permute-start.6 = (f32[16,1024]{1,0:T(8,128)S(1)}, f32[16,1024]{1,0:T(8,128)S(1)}, u32[]{:S(2)}, u32[]{:S(2)}) collective-permute-start(f32[16,1024]{1,0:T(8,128)S(1)} %get-tuple-element.98), channel_id=1, source_target_pairs={{0,16},{4,20},{8,24},{12,28},{16,0},{20,4},{24,8},{28,12},{1,17},{... | collective-permute-start | bytes 196616 | tf_op jit(solution)/shard_map/ppermute | solution.py:125
  92.5 5.0 %collective-permute-start.7 = (f32[16,1024]{1,0:T(8,128)S(1)}, f32[16,1024]{1,0:T(8,128)S(1)}, u32[]{:S(2)}, u32[]{:S(2)}) collective-permute-start(f32[16,1024]{1,0:T(8,128)S(1)} %get-tuple-element.99), channel_id=1, source_target_pairs={{0,24},{4,28},{8,0},{12,4},{16,8},{20,12},{24,16},{28,20},{1,25},{... | collective-permute-start | bytes 196616 | tf_op jit(solution)/shard_map/ppermute | solution.py:125
  97.6 3.1 %collective-permute-start.8 = (f32[2,16,1024]{2,1,0:T(8,128)S(1)}, f32[2,16,1024]{2,1,0:T(8,128)S(1)}, u32[]{:S(2)}, u32[]{:S(2)}) collective-permute-start(f32[2,16,1024]{2,1,0:T(8,128)S(1)} %fusion.17), channel_id=1, source_target_pairs={{0,4},{4,0},{8,12},{12,8},{16,20},{20,16},{24,28},{28,24},{1,5},{5... | collective-permute-start | bytes 393224 | tf_op jit(solution)/shard_map/ppermute | solution.py:144
  97.7 17.1 %collective-permute-start.9 = (f32[64,1024]{1,0:T(8,128)S(1)}, f32[64,1024]{1,0:T(8,128)S(1)}, u32[]{:S(2)}, u32[]{:S(2)}) collective-permute-start(f32[64,1024]{1,0:T(8,128)S(1)} %get-tuple-element.77), channel_id=1, source_target_pairs={{0,1},{1,2},{2,3},{3,0},{4,5},{5,6},{6,7},{7,4},{8,9},{9,10},{10,1... | collective-permute-start | bytes 786440 | tf_op jit(solution)/shard_map/ppermute | solution.py:92
  100.1 14.7 %collective-permute-start.11 = (f32[64,1024]{1,0:T(8,128)S(1)}, f32[64,1024]{1,0:T(8,128)S(1)}, u32[]{:S(2)}, u32[]{:S(2)}) collective-permute-start(f32[64,1024]{1,0:T(8,128)S(1)} %get-tuple-element.78), channel_id=1, source_target_pairs={{0,3},{1,0},{2,1},{3,2},{4,7},{5,4},{6,5},{7,6},{8,11},{9,8},{10,9... | collective-permute-start | bytes 786440 | tf_op jit(solution)/shard_map/ppermute | solution.py:92
  100.9 12.3 %collective-permute-start.12 = (f32[2,1024]{1,0:T(2,128)S(1)}, f32[2,1024]{1,0:T(2,128)S(1)}, u32[]{:S(2)}, u32[]{:S(2)}) collective-permute-start(f32[2,1024]{1,0:T(2,128)S(1)} %get-tuple-element.113), channel_id=1, source_target_pairs={{0,1},{1,2},{2,3},{3,0},{4,5},{5,6},{6,7},{7,4},{8,9},{9,10},{10,1... | collective-permute-start | bytes 24584 | tf_op jit(solution)/shard_map/ppermute | solution.py:92
  102.4 12.3 %collective-permute-start.14 = (f32[2,1024]{1,0:T(2,128)S(1)}, f32[2,1024]{1,0:T(2,128)S(1)}, u32[]{:S(2)}, u32[]{:S(2)}) collective-permute-start(f32[2,1024]{1,0:T(2,128)S(1)} %get-tuple-element.114), channel_id=1, source_target_pairs={{0,3},{1,0},{2,1},{3,2},{4,7},{5,4},{6,5},{7,6},{8,11},{9,8},{10,9... | collective-permute-start | bytes 24584 | tf_op jit(solution)/shard_map/ppermute | solution.py:92
  103.9 10.9 %collective-permute-start.13 = (f32[2,1024]{1,0:T(2,128)S(1)}, f32[2,1024]{1,0:T(2,128)S(1)}, u32[]{:S(2)}, u32[]{:S(2)}) collective-permute-start(f32[2,1024]{1,0:T(2,128)S(1)} %get-tuple-element.115), channel_id=1, source_target_pairs={{0,2},{1,3},{2,0},{3,1},{4,6},{5,7},{6,4},{7,5},{8,10},{9,11},{10,... | collective-permute-start | bytes 24584 | tf_op jit(solution)/shard_map/ppermute | solution.py:92
  113.3 7.5 %collective-permute-start.10 = (f32[64,1024]{1,0:T(8,128)S(1)}, f32[64,1024]{1,0:T(8,128)S(1)}, u32[]{:S(2)}, u32[]{:S(2)}) collective-permute-start(f32[64,1024]{1,0:T(8,128)S(1)} %get-tuple-element.79), channel_id=1, source_target_pairs={{0,2},{1,3},{2,0},{3,1},{4,6},{5,7},{6,4},{7,5},{8,10},{9,11},{10,... | collective-permute-start | bytes 786440 | tf_op jit(solution)/shard_map/ppermute | solution.py:92
  121.1 3.4 %copy-start.2 = (f32[32,64,1024]{2,1,0:T(8,128)S(1)}, f32[32,64,1024]{2,1,0:T(8,128)}, u32[]{:S(2)}) copy-start(f32[32,64,1024]{2,1,0:T(8,128)} %u_ref.3) | copy-start | bytes 25165828
  124.5 3.4 %copy-start.3 = (f32[32,64,1024]{2,1,0:T(8,128)S(1)}, f32[32,64,1024]{2,1,0:T(8,128)}, u32[]{:S(2)}) copy-start(f32[32,64,1024]{2,1,0:T(8,128)} %get-tuple-element.11.t_ref) | copy-start | bytes 25165828
  135.1 12.6 %copy-start = (f32[32,64,1024]{2,1,0:T(8,128)}, f32[32,64,1024]{2,1,0:T(8,128)S(1)}, u32[]{:S(2)}) copy-start(f32[32,64,1024]{2,1,0:T(8,128)S(1)} %update.2.u_ref.below_ref.above_ref) | copy-start | bytes 25165828
  135.2 12.6 %collective-permute-start.18 = (f32[64,1024]{1,0:T(8,128)S(1)}, f32[64,1024]{1,0:T(8,128)S(1)}, u32[]{:S(2)}, u32[]{:S(2)}) collective-permute-start(f32[64,1024]{1,0:T(8,128)S(1)} %get-tuple-element.46), channel_id=1, source_target_pairs={{1,0},{2,1},{3,2},{5,4},{6,5},{7,6},{9,8},{10,9},{11,10},{13,12},{... | collective-permute-start | bytes 786440 | tf_op jit(solution)/shard_map/ppermute | solution.py:377
  136.5 11.3 %collective-permute-start.17 = (f32[64,1024]{1,0:T(8,128)S(1)}, f32[64,1024]{1,0:T(8,128)S(1)}, u32[]{:S(2)}, u32[]{:S(2)}) collective-permute-start(f32[64,1024]{1,0:T(8,128)S(1)} %get-tuple-element.47), channel_id=1, source_target_pairs={{0,1},{1,2},{2,3},{4,5},{5,6},{6,7},{8,9},{9,10},{10,11},{12,13},{... | collective-permute-start | bytes 786440 | tf_op jit(solution)/shard_map/ppermute | solution.py:376
  141.4 2.6 %collective-permute-start.15 = (f32[32,1024]{1,0:T(8,128)S(1)}, f32[32,1024]{1,0:T(8,128)S(1)}, u32[]{:S(2)}, u32[]{:S(2)}) collective-permute-start(f32[32,1024]{1,0:T(8,128)S(1)} %bitcast.182), channel_id=1, source_target_pairs={{0,4},{4,8},{8,12},{12,16},{16,20},{20,24},{24,28},{1,5},{5,9},{9,... | collective-permute-start | bytes 393224 | tf_op jit(solution)/shard_map/ppermute | solution.py:374
  142.7 5.1 %collective-permute-start.16 = (f32[32,1024]{1,0:T(8,128)S(1)}, f32[32,1024]{1,0:T(8,128)S(1)}, u32[]{:S(2)}, u32[]{:S(2)}) collective-permute-start(f32[32,1024]{1,0:T(8,128)S(1)} %bitcast.181), channel_id=1, source_target_pairs={{4,0},{8,4},{12,8},{16,12},{20,16},{24,20},{28,24},{5,1},{9,5},{13... | collective-permute-start | bytes 393224 | tf_op jit(solution)/shard_map/ppermute | solution.py:375
  176.7 4.6 %collective-permute-start.19 = (f32[2,16,1024]{2,1,0:T(8,128)S(1)}, f32[2,16,1024]{2,1,0:T(8,128)S(1)}, u32[]{:S(2)}, u32[]{:S(2)}) collective-permute-start(f32[2,16,1024]{2,1,0:T(8,128)S(1)} %slice_select_fusion.1), channel_id=1, source_target_pairs={{0,4},{4,0},{8,12},{12,8},{16,20},{20,16},{24,28},{28,24},{1,5},{5... | collective-permute-start | bytes 393224 | tf_op jit(solution)/shard_map/ppermute | solution.py:116
  182.6 6.9 %collective-permute-start.20 = (f32[16,1024]{1,0:T(8,128)S(1)}, f32[16,1024]{1,0:T(8,128)S(1)}, u32[]{:S(2)}, u32[]{:S(2)}) collective-permute-start(f32[16,1024]{1,0:T(8,128)S(1)} %get-tuple-element.36), channel_id=1, source_target_pairs={{0,8},{4,12},{8,16},{12,20},{16,24},{20,28},{24,0},{28,4},{1,9},{5... | collective-permute-start | bytes 196616 | tf_op jit(solution)/shard_map/ppermute | solution.py:125
  182.7 8.5 %collective-permute-start.21 = (f32[16,1024]{1,0:T(8,128)S(1)}, f32[16,1024]{1,0:T(8,128)S(1)}, u32[]{:S(2)}, u32[]{:S(2)}) collective-permute-start(f32[16,1024]{1,0:T(8,128)S(1)} %get-tuple-element.96), channel_id=1, source_target_pairs={{0,16},{4,20},{8,24},{12,28},{16,0},{20,4},{24,8},{28,12},{1,17},{... | collective-permute-start | bytes 196616 | tf_op jit(solution)/shard_map/ppermute | solution.py:125
  184.5 6.8 %collective-permute-start.22 = (f32[16,1024]{1,0:T(8,128)S(1)}, f32[16,1024]{1,0:T(8,128)S(1)}, u32[]{:S(2)}, u32[]{:S(2)}) collective-permute-start(f32[16,1024]{1,0:T(8,128)S(1)} %get-tuple-element.97), channel_id=1, source_target_pairs={{0,24},{4,28},{8,0},{12,4},{16,8},{20,12},{24,16},{28,20},{1,25},{... | collective-permute-start | bytes 196616 | tf_op jit(solution)/shard_map/ppermute | solution.py:125
  191.3 3.1 %collective-permute-start.23 = (f32[2,16,1024]{2,1,0:T(8,128)S(1)}, f32[2,16,1024]{2,1,0:T(8,128)S(1)}, u32[]{:S(2)}, u32[]{:S(2)}) collective-permute-start(f32[2,16,1024]{2,1,0:T(8,128)S(1)} %fusion.15), channel_id=1, source_target_pairs={{0,4},{4,0},{8,12},{12,8},{16,20},{20,16},{24,28},{28,24},{1,5},{5... | collective-permute-start | bytes 393224 | tf_op jit(solution)/shard_map/ppermute | solution.py:144
  191.5 17.1 %collective-permute-start.24 = (f32[64,1024]{1,0:T(8,128)S(1)}, f32[64,1024]{1,0:T(8,128)S(1)}, u32[]{:S(2)}, u32[]{:S(2)}) collective-permute-start(f32[64,1024]{1,0:T(8,128)S(1)} %get-tuple-element.74), channel_id=1, source_target_pairs={{0,1},{1,2},{2,3},{3,0},{4,5},{5,6},{6,7},{7,4},{8,9},{9,10},{10,1... | collective-permute-start | bytes 786440 | tf_op jit(solution)/shard_map/ppermute | solution.py:92
  193.9 14.7 %collective-permute-start.26 = (f32[64,1024]{1,0:T(8,128)S(1)}, f32[64,1024]{1,0:T(8,128)S(1)}, u32[]{:S(2)}, u32[]{:S(2)}) collective-permute-start(f32[64,1024]{1,0:T(8,128)S(1)} %get-tuple-element.75), channel_id=1, source_target_pairs={{0,3},{1,0},{2,1},{3,2},{4,7},{5,4},{6,5},{7,6},{8,11},{9,8},{10,9... | collective-permute-start | bytes 786440 | tf_op jit(solution)/shard_map/ppermute | solution.py:92
  194.7 12.4 %collective-permute-start.27 = (f32[2,1024]{1,0:T(2,128)S(1)}, f32[2,1024]{1,0:T(2,128)S(1)}, u32[]{:S(2)}, u32[]{:S(2)}) collective-permute-start(f32[2,1024]{1,0:T(2,128)S(1)} %get-tuple-element.110), channel_id=1, source_target_pairs={{0,1},{1,2},{2,3},{3,0},{4,5},{5,6},{6,7},{7,4},{8,9},{9,10},{10,1... | collective-permute-start | bytes 24584 | tf_op jit(solution)/shard_map/ppermute | solution.py:92
  196.2 12.4 %collective-permute-start.29 = (f32[2,1024]{1,0:T(2,128)S(1)}, f32[2,1024]{1,0:T(2,128)S(1)}, u32[]{:S(2)}, u32[]{:S(2)}) collective-permute-start(f32[2,1024]{1,0:T(2,128)S(1)} %get-tuple-element.111), channel_id=1, source_target_pairs={{0,3},{1,0},{2,1},{3,2},{4,7},{5,4},{6,5},{7,6},{8,11},{9,8},{10,9... | collective-permute-start | bytes 24584 | tf_op jit(solution)/shard_map/ppermute | solution.py:92
  197.7 10.9 %collective-permute-start.28 = (f32[2,1024]{1,0:T(2,128)S(1)}, f32[2,1024]{1,0:T(2,128)S(1)}, u32[]{:S(2)}, u32[]{:S(2)}) collective-permute-start(f32[2,1024]{1,0:T(2,128)S(1)} %get-tuple-element.112), channel_id=1, source_target_pairs={{0,2},{1,3},{2,0},{3,1},{4,6},{5,7},{6,4},{7,5},{8,10},{9,11},{10,... | collective-permute-start | bytes 24584 | tf_op jit(solution)/shard_map/ppermute | solution.py:92
  207.0 7.5 %collective-permute-start.25 = (f32[64,1024]{1,0:T(8,128)S(1)}, f32[64,1024]{1,0:T(8,128)S(1)}, u32[]{:S(2)}, u32[]{:S(2)}) collective-permute-start(f32[64,1024]{1,0:T(8,128)S(1)} %get-tuple-element.76), channel_id=1, source_target_pairs={{0,2},{1,3},{2,0},{3,1},{4,6},{5,7},{6,4},{7,5},{8,10},{9,11},{10,... | collective-permute-start | bytes 786440 | tf_op jit(solution)/shard_map/ppermute | solution.py:92
  214.7 3.4 %copy-start.1 = (f32[32,64,1024]{2,1,0:T(8,128)S(1)}, f32[32,64,1024]{2,1,0:T(8,128)}, u32[]{:S(2)}) copy-start(f32[32,64,1024]{2,1,0:T(8,128)} %copy-done) | copy-start | bytes 25165828
  218.1 3.4 %copy-start.4 = (f32[32,64,1024]{2,1,0:T(8,128)S(1)}, f32[32,64,1024]{2,1,0:T(8,128)}, u32[]{:S(2)}) copy-start(f32[32,64,1024]{2,1,0:T(8,128)} %get-tuple-element.14.t_ref) | copy-start | bytes 25165828

commit v2 on v0

v2 whole, which is shorter than its diff:
```python
import functools

import jax
import jax.numpy as jnp
from jax import lax
from jax.experimental import pallas as pl
from jax.experimental.pallas import tpu as pltpu
from jax.sharding import PartitionSpec as P


STEPS = 2
REACTION = 2.0
LANES = 128
SUB = 8
XB = 256
ZB = 8

DIAG, UP, DOWN, SUM_UP, SUM_DOWN, COND, MISC, CHIPS, LINES = range(9)
TABLE_ROWS = 16
Z_LOW, Z_HIGH, Y_LOW, Y_HIGH, MIX, KEEP, GIVE = 0, 1, 2, 3, 4, 8, 12
FAR = 64

f32 = jnp.float32
bf16 = jnp.bfloat16


def split(a):
    high = a.astype(bf16)
    low = (a - high.astype(f32)).astype(bf16)
    return high, low


def wide_rows(ref, rows, nx):
    return jnp.concatenate([ref[rows]] * (nx // LANES), axis=1)


def full(a):
    return pl.BlockSpec(a.shape, lambda *_: (0,) * len(a.shape))


def smem():
    return pl.BlockSpec(memory_space=pltpu.SMEM)


def call(kernel, out_shape, operands, **kw):
    limit = kw.pop("vmem", 16)
    return pl.pallas_call(
        kernel,
        out_shape=out_shape,
        compiler_params=pltpu.CompilerParams(
            dimension_semantics=("arbitrary",) * len(kw.get("grid", ())),
            vmem_limit_bytes=limit * 2**20,
        ),
        **kw,
    )(*operands)


def shape(*dims, dtype=f32):
    return jax.ShapeDtypeStruct(dims, dtype)


def strip_of(ref, start, count):
    total = ref.shape[0]
    top = pl.multiple_of(lax.rem(start - SUB + total, total), SUB)
    end = pl.multiple_of(lax.rem(start + count, total), SUB)
    rows = jnp.concatenate(
        [
            ref[pl.ds(top, SUB), :],
            ref[pl.ds(pl.multiple_of(start, SUB), count), :],
            ref[pl.ds(end, SUB), :],
        ],
        axis=0,
    )
    return pltpu.roll(rows, lax.rem(total - start, total), 1)


def entry(ref, i, j):
    total = ref.shape[0]
    i = lax.rem(i + total, total)
    j = lax.rem(j + total, total)
    row = ref[pl.ds(i, 1), :]
    lane = lax.broadcasted_iota(jnp.int32, row.shape, 1)
    return jnp.sum(jnp.where(lane == j, row, 0.0), axis=1, keepdims=True)


def over_pivot(ref, i, j):
    return entry(ref, i, j) / entry(ref, j, j)


def tables_kernel(
    ids_ref, ax_ref, lower_ref, lpiv_ref, upper_ref, upiv_ref, ay_ref, az_ref,
    cy_ref, cz_ref,
    axh_ref, axl_ref, xlo_ref, xhi_ref, wide_ref, mat_ref, scal_ref,
    *, rows, depth, ny, nz,
):
    e = pl.program_id(0)
    last = pl.num_programs(0) - 1
    high, low = split(ax_ref[...].T)
    axh_ref[0] = high
    axl_ref[0] = low
    from_low = lower_ref[...].T[LANES - 1 :] / lpiv_ref[SUB - 1 :, LANES - 1 :]
    from_high = upper_ref[...].T[:1] / upiv_ref[:1, :1]
    xlo_ref[...] = jnp.where(e > 0, from_low, 0.0)
    xhi_ref[...] = jnp.where(e < last, from_high, 0.0)

    @pl.when(e == 0)
    def _():
        gy, gz = ids_ref[0], ids_ref[1]
        y0, z0 = gy * rows, gz * depth
        ys = strip_of(ay_ref, y0, rows)
        zs = strip_of(az_ref, z0, depth)
        end = ay_ref.shape[0] - 1
        pad = jnp.zeros((SUB - 2, 1), f32)

        def arranged(column):
            return jnp.concatenate(
                [
                    column[SUB : SUB + rows],
                    column[SUB - 1 : SUB],
                    column[SUB + rows : SUB + rows + 1],
                    pad,
                ],
                axis=0,
            )

        lo = arranged(ys[:, end:] / ys[SUB - 1 : SUB, end:])
        hi = arranged(
            ys[:, rows : rows + 1] / ys[SUB + rows : SUB + rows + 1, rows : rows + 1]
        )
        wide_ref[0] = jnp.broadcast_to(lo, (rows + SUB, LANES))
        wide_ref[1] = jnp.broadcast_to(hi, (rows + SUB, LANES))
        cy = pltpu.roll(cy_ref[...], lax.rem(cy_ref.shape[1] - y0, cy_ref.shape[1]), 1)
        cy = jnp.broadcast_to(cy[:, :LANES], (LANES, LANES)).T
        wide_ref[2] = cy[1 : rows + 1 + SUB]
        wide_ref[3] = cy[: rows + SUB]
        bh, bl = split(ys[SUB : SUB + rows, :rows])
        mat_ref[:rows, :] = jnp.concatenate([bh, bh], axis=1)
        mat_ref[rows:, :] = jnp.concatenate([bl, jnp.zeros_like(bl)], axis=1)

        total = az_ref.shape[0]
        r = lax.broadcasted_iota(jnp.int32, zs.shape, 0)
        c = lax.broadcasted_iota(jnp.int32, zs.shape, 1)
        pick = lambda shift: jnp.sum(
            jnp.where(r == c + (SUB + shift), zs, 0.0), axis=0, keepdims=True
        )
        lane = lax.broadcasted_iota(jnp.int32, (1, total), 1)
        diag = jnp.where(lane < depth, pick(0), 1.0)
        scal_ref[...] = jnp.zeros_like(scal_ref)

        def row(index, value):
            scal_ref[index : index + 1, :] = value[:, :LANES]

        row(DIAG, diag)
        row(UP, pick(1) / diag)
        row(DOWN, pick(-1) / diag)
        row(SUM_UP, zs[SUB + depth - 1 : SUB + depth])
        row(SUM_DOWN, zs[SUB : SUB + 1])
        cz = pltpu.roll(cz_ref[...], lax.rem(cz_ref.shape[1] - z0, cz_ref.shape[1]), 1)
        row(COND, cz)

        lane = lax.broadcasted_iota(jnp.int32, (1, LANES), 1)

        def fill(index, values):
            line = jnp.zeros((1, LANES), f32)
            for at, value in values.items():
                line = jnp.where(lane == at, value, line)
            row(index, line)

        far = total - 1
        core = lax.rem(gy, 2)
        chip = gy // 2
        chips = ny // 2
        yb = chip * (2 * rows)
        one = jnp.ones((1, 1), f32)
        zero = jnp.zeros((1, 1), f32)
        up = over_pivot(ay_ref, yb + 2 * rows - 1, yb + rows - 1)
        down = over_pivot(ay_ref, yb, yb + rows)
        through_up = over_pivot(ay_ref, yb + rows - 1, yb - 1)
        through_down = over_pivot(ay_ref, yb + rows, yb + 2 * rows)
        by_core = lambda a, b: jnp.where(core == 0, a, b)
        fill(
            MISC,
            {
                Z_LOW: zs[SUB : SUB + 1, far:] / zs[SUB - 1 : SUB, far:],
                Z_HIGH: zs[SUB + depth - 1 : SUB + depth, depth : depth + 1]
                / zs[SUB + depth : SUB + depth + 1, depth : depth + 1],
                Y_LOW: ys[SUB - 1 : SUB, :1] / ys[SUB : SUB + 1, :1],
                Y_HIGH: ys[SUB + rows : SUB + rows + 1, rows - 1 : rows]
                / ys[SUB + rows - 1 : SUB + rows, rows - 1 : rows],
                MIX: by_core(up, one),
                MIX + 1: by_core(one, up),
                MIX + 2: by_core(one, down),
                MIX + 3: by_core(down, one),
                KEEP: by_core(one, through_up),
                KEEP + 1: by_core(zero, one),
                KEEP + 2: by_core(through_down, one),
                KEEP + 3: by_core(one, zero),
                GIVE: by_core(through_up, one),
                GIVE + 1: by_core(one, zero),
                GIVE + 2: by_core(one, through_down),
                GIVE + 3: by_core(zero, one),
            },
        )
        values = {}
        for k in range(1, chips):
            src = lax.rem(chip - k + chips, chips)
            below = src < chip
            a = over_pivot(ay_ref, yb - 1, (src + 1) * 2 * rows - 1)
            b = over_pivot(ay_ref, yb + 2 * rows, src * 2 * rows)
            values[k] = jnp.where(below, a, 0.0)
            values[FAR + k] = jnp.where(below, 0.0, b)
        fill(CHIPS, values)
        values = {}
        for k in range(1, nz):
            src = lax.rem(gz - k + nz, nz)
            below = src < gz
            a = over_pivot(az_ref, z0 - 1, (src + 1) * depth - 1)
            b = over_pivot(az_ref, z0 + depth, src * depth)
            values[k] = jnp.where(below, a, 0.0)
            values[FAR + k] = jnp.where(below, 0.0, b)
        fill(LINES, values)


def tables(ids, inverse_x, inverse_y, inverse_z, cond_y, cond_z, rows, depth):
    nx = inverse_x.shape[0]
    blocks = nx // XB
    ny, nz = lax.axis_size("gy"), lax.axis_size("gz")
    q, s = XB // LANES, XB // SUB
    round_up = lambda n: -(-n // LANES) * LANES
    cy = jnp.pad(cond_y, (1, round_up(cond_y.shape[0] + 2 + LANES) - cond_y.shape[0] - 1))[None]
    cz = jnp.pad(cond_z, (1, round_up(cond_z.shape[0] + 2 + LANES) - cond_z.shape[0] - 1))[None]
    column = lambda at: pl.BlockSpec((XB, LANES), lambda e: (e, at(e)))
    low = lambda e: jnp.maximum(q * e - 1, 0)
    top = lambda e: jnp.minimum(q * e + q, q * blocks - 1)
    return call(
        functools.partial(tables_kernel, rows=rows, depth=depth, ny=ny, nz=nz),
        [
            shape(blocks, XB, XB, dtype=bf16),
            shape(blocks, XB, XB, dtype=bf16),
            shape(1, nx),
            shape(1, nx),
            shape(4, rows + SUB, LANES),
            shape(2 * rows, 2 * rows, dtype=bf16),
            shape(TABLE_ROWS, LANES),
        ],
        (ids, inverse_x, inverse_x, inverse_x, inverse_x, inverse_x, inverse_y, inverse_z, cy, cz),
        grid=(blocks,),
        in_specs=[
            smem(),
            pl.BlockSpec((XB, XB), lambda e: (e, e)),
            column(low),
            pl.BlockSpec((SUB, LANES), lambda e: (jnp.maximum(s * e - 1, 0), low(e))),
            column(top),
            pl.BlockSpec(
                (SUB, LANES), lambda e: (jnp.minimum(s * e + s, s * blocks - 1), top(e))
            ),
            full(inverse_y), full(inverse_z), full(cy), full(cz),
        ],
        out_specs=[
            pl.BlockSpec((1, XB, XB), lambda e: (e, 0, 0)),
            pl.BlockSpec((1, XB, XB), lambda e: (e, 0, 0)),
            pl.BlockSpec((1, XB), lambda e: (0, e)),
            pl.BlockSpec((1, XB), lambda e: (0, e)),
            full(shape(4, rows + SUB, LANES)),
            full(shape(2 * rows, 2 * rows)),
            full(shape(TABLE_ROWS, LANES)),
        ],
        name="tables",
    )


def explicit_kernel(
    ids_ref, scal_ref, u_ref, below_ref, above_ref, o_ref, ylo_ref, yhi_ref,
    zlo_ref, zhi_ref, cx_ref, wide_ref, ay_ref, axh_ref, axl_ref, xlo_ref, xhi_ref,
    t_ref, edge_ref, mine_ref, theirs_ref, *rest, nz,
):
    pays = rest[: nz - 1]
    rhs_ref, line_ref, sy_ref, sz_ref, low_ref, high_ref = rest[nz - 1 :]
    step = pl.program_id(0)
    steps = pl.num_programs(0)
    zb, rows, nx = u_ref.shape
    tiles = rows // SUB
    blocks = nx // XB
    sub = lax.broadcasted_iota(jnp.int32, (SUB, nx), 0)

    low_ref[...] = jnp.where(step > 0, below_ref[0], zlo_ref[...])
    high_ref[...] = jnp.where(step < steps - 1, above_ref[0], zhi_ref[...])

    def plane(z, below, above):
        zz = step * zb + z
        c_dn = scal_ref[COND, zz]
        c_up = scal_ref[COND, zz + 1]
        cx = jnp.broadcast_to(cx_ref[...], (SUB, nx))
        before = jnp.broadcast_to(ylo_ref[pl.ds(zz, 1), :], (SUB, nx))
        current = u_ref[z, :SUB, :]
        down_roll = pltpu.roll(current, 1, 0)
        for r in range(tiles):
            own = slice(r * SUB, (r + 1) * SUB)
            if r + 1 < tiles:
                following = u_ref[z, (r + 1) * SUB : (r + 2) * SUB, :]
                up_next = pltpu.roll(following, SUB - 1, 0)
                down_next = pltpu.roll(following, 1, 0)
            else:
                following = down_next = None
                up_next = jnp.broadcast_to(yhi_ref[pl.ds(zz, 1), :], (SUB, nx))
            c = current
            down = jnp.where(sub == 0, before, down_roll)
            up = jnp.where(sub == SUB - 1, up_next, pltpu.roll(c, SUB - 1, 0))
            fx = (pltpu.roll(c, nx - 1, 1) - c) * cx
            total = fx - pltpu.roll(fx, 1, 1)
            cup = wide_rows(wide_ref, (2, own), nx)
            cdn = wide_rows(wide_ref, (3, own), nx)
            total = total + ((up - c) * cup - (c - down) * cdn)
            total = total + ((above(own) - c) * c_up - (c - below(own)) * c_dn)
            o = o_ref[z, own, :]
            total = total + (REACTION * c) * (1.0 - c * c - 2.0 * o)
            rhs_ref[pl.ds(pl.multiple_of(z * rows + r * SUB, SUB), SUB), :] = total
            before = down_roll
            current = following
            down_roll = down_next

    plane(0, lambda own: low_ref[own, :], lambda own: u_ref[1, own, :])

    def inner(z, carry):
        plane(z, lambda own: u_ref[z - 1, own, :], lambda own: u_ref[z + 1, own, :])
        return carry

    lax.fori_loop(1, zb - 1, inner, 0)
    plane(zb - 1, lambda own: u_ref[zb - 2, own, :], lambda own: high_ref[own, :])

    dot = functools.partial(jnp.dot, preferred_element_type=f32)
    for e in range(blocks):
        cols = slice(e * XB, (e + 1) * XB)
        high, low = split(rhs_ref[:, cols])
        line_ref[:, cols] = (
            dot(high, axh_ref[e]) + dot(low, axh_ref[e]) + dot(high, axl_ref[e])
        )
    lows = [None]
    for e in range(blocks - 1):
        at = slice((e + 1) * XB - 1, (e + 1) * XB)
        end = line_ref[:, at]
        if lows[e] is not None:
            end = end + lows[e] * xlo_ref[:, at]
        lows.append(end)
    highs = [None] * blocks
    for e in reversed(range(1, blocks)):
        at = slice(e * XB, e * XB + 1)
        end = line_ref[:, at]
        if highs[e] is not None:
            end = end + highs[e] * xhi_ref[:, at]
        highs[e - 1] = end
    for e in range(blocks):
        cols = slice(e * XB, (e + 1) * XB)
        value = line_ref[:, cols]
        if lows[e] is not None:
            value = value + lows[e] * xlo_ref[:, cols]
        if highs[e] is not None:
            value = value + highs[e] * xhi_ref[:, cols]
        line_ref[:, cols] = value

    @pl.when(step == 0)
    def _():
        sz_ref[...] = jnp.zeros_like(sz_ref)

    y_low = scal_ref[MISC, Y_LOW]
    y_high = scal_ref[MISC, Y_HIGH]

    def solve(z, carry):
        zz = step * zb + z
        base = pl.multiple_of(z * rows, rows)
        high, low = split(line_ref[pl.ds(base, rows), :])
        both = jnp.concatenate([high, low], axis=0)
        result = dot(ay_ref[...], both)
        value = result[:rows] + result[rows:]
        t_ref[z] = value
        first, final = value[:1], value[rows - 1 :]
        sy_ref[0, pl.ds(z, 1), :] = final
        sy_ref[1, pl.ds(z, 1), :] = first
        edge_ref[z, 0:1, :] = y_low * first
        edge_ref[z, 1:2, :] = y_high * final
        sz_ref[0] = sz_ref[0] + scal_ref[SUM_UP, zz] * value
        sz_ref[1] = sz_ref[1] + scal_ref[SUM_DOWN, zz] * value
        return carry

    lax.fori_loop(0, zb, solve, 0)

    half = mine_ref.shape[1]
    part = (step * zb) // half
    at = pl.ds(pl.multiple_of(step * zb - part * half, SUB), zb)
    core = lax.rem(ids_ref[0], 2)

    @pl.when(part == core)
    def _():
        mine_ref[:, at, :] = sy_ref[...]

    @pl.when(part != core)
    def _():
        theirs_ref[:, at, :] = sy_ref[...]

    @pl.when(step == steps - 1)
    def _():
        for k in range(1, nz):
            higher = ids_ref[1] + k < nz
            pays[k - 1][...] = jnp.where(higher, sz_ref[0], sz_ref[1])


def explicit(ids, scal, u, o, halos, tabs, cx):
    depth, rows, nx = u.shape
    axh, axl, xlo, xhi, wide, mat = tabs
    nz = lax.axis_size("gz")
    zb = ZB
    steps = depth // zb
    half = depth // 2
    field = pl.BlockSpec((zb, rows, nx), lambda s: (s, 0, 0))
    below = pl.BlockSpec((1, rows, nx), lambda s: (jnp.maximum(s * zb - 1, 0), 0, 0))
    above = pl.BlockSpec(
        (1, rows, nx), lambda s: (jnp.minimum(s * zb + zb, depth - 1), 0, 0)
    )
    rest = (*halos, cx, wide, mat, axh, axl, xlo, xhi)
    outs = [
        shape(depth, rows, nx),
        shape(depth, SUB, nx),
        shape(2, half, nx),
        shape(2, half, nx),
    ] + [shape(rows, nx)] * (nz - 1)
    return call(
        functools.partial(explicit_kernel, nz=nz),
        outs,
        (ids, scal, u, u, u, o, *rest),
        grid=(steps,),
        in_specs=[smem(), smem(), field, below, above, field, *map(full, rest)],
        out_specs=[field, pl.BlockSpec((zb, SUB, nx), lambda s: (s, 0, 0))]
        + [full(a) for a in outs[2:]],
        scratch_shapes=[
            pltpu.VMEM((zb * rows, nx), f32),
            pltpu.VMEM((zb * rows, nx), f32),
            pltpu.VMEM((2, zb, nx), f32),
            pltpu.VMEM((2, rows, nx), f32),
            pltpu.VMEM((rows, nx), f32),
            pltpu.VMEM((rows, nx), f32),
        ],
        vmem=48,
        name="explicit",
    )


def chip_kernel(ids_ref, scal_ref, mine_ref, other_ref, *pays):
    mix = lambda i: scal_ref[MISC, MIX + i]
    up = mix(0) * mine_ref[0] + mix(1) * other_ref[0]
    down = mix(2) * mine_ref[1] + mix(3) * other_ref[1]
    chip = ids_ref[0] // 2
    for k, pay in enumerate(pays, 1):
        pay[...] = jnp.where(chip + k < len(pays) + 1, up, down)


def share_kernel(scal_ref, mine_ref, other_ref, *rest):
    *gots, keep_ref, give_ref = rest
    low = jnp.zeros_like(gots[0])
    high = jnp.zeros_like(gots[0])
    for k, got in enumerate(gots, 1):
        low = low + scal_ref[CHIPS, k] * got[...]
        high = high + scal_ref[CHIPS, FAR + k] * got[...]
    keep = lambda i: scal_ref[MISC, KEEP + i]
    give = lambda i: scal_ref[MISC, GIVE + i]
    keep_ref[0] = keep(0) * low + keep(1) * other_ref[0]
    keep_ref[1] = keep(2) * high + keep(3) * other_ref[1]
    give_ref[0] = give(0) * low + give(1) * mine_ref[0]
    give_ref[1] = give(2) * high + give(3) * mine_ref[1]


def corner_kernel(ids_ref, scal_ref, keep_ref, back_ref, *pays):
    half = keep_ref.shape[1]
    core = lax.rem(ids_ref[0], 2)
    near, far = core * half, (1 - core) * half
    up = jnp.zeros((2, keep_ref.shape[2]), f32)
    down = jnp.zeros_like(up)
    for z in range(half):
        for ref, base in ((keep_ref, near), (back_ref, far)):
            row = ref[:, z, :]
            up = up + scal_ref[SUM_UP, base + z] * row
            down = down + scal_ref[SUM_DOWN, base + z] * row
    for k, pay in enumerate(pays, 1):
        pay[...] = jnp.where(ids_ref[1] + k < len(pays) + 1, up, down)


def cyclic(size, k, stride=1):
    groups = size // stride
    return [
        (c * stride + r, ((c + k) % groups) * stride + r)
        for c in range(groups)
        for r in range(stride)
    ]


def update_kernel(
    ids_ref, scal_ref, t_ref, u_ref, edge_ref, keep_ref, back_ref, wide_ref,
    ylo_ref, yhi_ref, zlo_ref, zhi_ref, *rest, nz, final,
):
    gots, corners, rest = rest[: nz - 1], rest[nz - 1 : 2 * nz - 2], rest[2 * nz - 2 :]
    if final:
        out_ref, e_ref, pq_ref = rest
    else:
        out_ref, nylo_ref, nyhi_ref, nzlo_ref, nzhi_ref, e_ref, pq_ref, s_ref = rest
    r = pl.program_id(0)
    depth, _, nx = t_ref.shape
    half = keep_ref.shape[1]
    tiles = wide_ref.shape[1] // SUB - 1
    scal = lambda i, j: scal_ref[i, j]

    @pl.when(r == 0)
    def _():
        core = lax.rem(ids_ref[0], 2)
        near = pl.multiple_of(core * half, SUB)
        far = pl.multiple_of((1 - core) * half, SUB)
        pq_ref[:, pl.ds(near, half), :] = keep_ref[...]
        pq_ref[:, pl.ds(far, half), :] = back_ref[...]

    own = pl.ds(pl.multiple_of(r * SUB, SUB), SUB)
    lo = wide_rows(wide_ref, (0, own), nx)
    hi = wide_rows(wide_ref, (1, own), nx)

    def solve(carry_rows, get_t, put_first, put_second):
        low = jnp.zeros((SUB, nx), f32)
        high = jnp.zeros((SUB, nx), f32)
        for k in range(1, nz):
            value = carry_rows(gots[k - 1])
            value = value + lo * corners[k - 1][0:1, :] + hi * corners[k - 1][1:2, :]
            low = low + scal(LINES, k) * value
            high = high + scal(LINES, FAR + k) * value

        def forward(z, carry):
            v = get_t(z) + lo * pq_ref[0, pl.ds(z, 1), :] + hi * pq_ref[1, pl.ds(z, 1), :]
            e = scal(DIAG, z) * v
            e_ref[z] = e
            s = carry + e
            put_first(z, s)
            return scal(UP, z) * s

        above = lax.fori_loop(0, depth, forward, scal(MISC, Z_LOW) * low, unroll=4)

        def backward(k, carry):
            z = depth - 1 - k
            put_second(z, carry)
            return scal(DOWN, z) * (carry + e_ref[z])

        below = lax.fori_loop(0, depth, backward, scal(MISC, Z_HIGH) * high, unroll=4)
        return low + below, high + above

    def first(z, s):
        out_ref[z] = u_ref[z] + s

    def second(z, b):
        out_ref[z] = out_ref[z] + b

    @pl.when(r < tiles)
    def _():
        below, above = solve(lambda got: got[own, :], lambda z: t_ref[z], first, second)
        if not final:
            nzlo_ref[...] = zlo_ref[...] + below
            nzhi_ref[...] = zhi_ref[...] + above

    if not final:
        y_low = scal(MISC, Y_LOW)
        y_high = scal(MISC, Y_HIGH)
        pad = jnp.zeros((SUB - 2, nx), f32)

        def ends(got):
            rows = got.shape[0]
            return jnp.concatenate(
                [y_low * got[0:1, :], y_high * got[rows - 1 : rows, :], pad], axis=0
            )

        def keep_sum(z, s):
            s_ref[z] = s

        def put(z, b):
            value = s_ref[z] + b
            nylo_ref[pl.ds(z, 1), :] = ylo_ref[pl.ds(z, 1), :] + value[0:1]
            nyhi_ref[pl.ds(z, 1), :] = yhi_ref[pl.ds(z, 1), :] + value[1:2]

        @pl.when(r == tiles)
        def _():
            solve(ends, lambda z: edge_ref[z], keep_sum, put)


def update(ids, scal, t, u, edge, keep, back, wide, halos, gots, corners, final):
    depth, rows, nx = u.shape
    nz = lax.axis_size("gz")
    tiles = rows // SUB
    ylo, yhi, zlo, zhi = halos
    clamp = lambda r: jnp.minimum(r, tiles - 1)
    field = pl.BlockSpec((depth, SUB, nx), lambda r: (0, clamp(r), 0))
    tile = pl.BlockSpec((SUB, nx), lambda r: (clamp(r), 0))
    outs = [shape(depth, rows, nx)]
    out_specs = [field]
    scratch = [pltpu.VMEM((depth, SUB, nx), f32), pltpu.VMEM((2, depth, nx), f32)]
    if not final:
        outs += [shape(depth, nx)] * 2 + [shape(rows, nx)] * 2
        out_specs += [full(ylo), full(yhi), tile, tile]
        scratch += [pltpu.VMEM((depth, SUB, nx), f32)]
    return call(
        functools.partial(update_kernel, nz=nz, final=final),
        outs,
        (ids, scal, t, u, edge, keep, back, wide, ylo, yhi, zlo, zhi, *gots, *corners),
        grid=(tiles if final else tiles + 1,),
        in_specs=[
            smem(), smem(), field, field, full(edge), full(keep), full(back), full(wide),
            full(ylo), full(yhi), tile, tile,
            *map(full, gots), *map(full, corners),
        ],
        out_specs=out_specs,
        scratch_shapes=scratch,
        vmem=32,
        name="update",
    )


def halo(u):
    ny, nz = lax.axis_size("gy"), lax.axis_size("gz")
    up = lambda n: [(i, i + 1) for i in range(n - 1)]
    down = lambda n: [(i + 1, i) for i in range(n - 1)]
    ylo = lax.ppermute(u[:, -1, :], "gy", up(ny))
    yhi = lax.ppermute(u[:, 0, :], "gy", down(ny))
    zlo = lax.ppermute(u[-1], "gz", up(nz))
    zhi = lax.ppermute(u[0], "gz", down(nz))
    return ylo, yhi, zlo, zhi


def body(phase_field, others, cond_x, cond_y, cond_z, inverse_x, inverse_y, inverse_z):
    depth, rows, nx = phase_field.shape
    ny, nz = lax.axis_size("gy"), lax.axis_size("gz")
    half = depth // 2
    ids = jnp.stack([lax.axis_index("gy"), lax.axis_index("gz")])
    halos = halo(phase_field)
    *tabs, scal = tables(
        ids, inverse_x, inverse_y, inverse_z, cond_y, cond_z, rows, depth
    )
    wide = tabs[4]
    cx = jnp.pad(cond_x, (0, 1))[None]
    swap = [(i, i ^ 1) for i in range(ny)]
    u = phase_field
    for step in range(STEPS):
        final = step == STEPS - 1
        t, edge, mine, theirs, *pays = explicit(ids, scal, u, others, halos, tabs, cx)
        gots = []
        for k in range(1, nz):
            gots.append(lax.ppermute(pays[k - 1], "gz", cyclic(nz, k)))
        other = lax.ppermute(theirs, "gy", swap)
        pays = call(
            chip_kernel,
            [shape(half, nx)] * (ny // 2 - 1),
            (ids, scal, mine, other),
            in_specs=[smem(), smem(), full(mine), full(other)],
            name="chip",
        )
        moved = [
            lax.ppermute(pays[k - 1], "gy", cyclic(ny, k, 2))
            for k in range(1, ny // 2)
        ]
        keep, give = call(
            share_kernel,
            [shape(2, half, nx)] * 2,
            (scal, mine, other, *moved),
            in_specs=[smem(), full(mine), full(other), *map(full, moved)],
            name="share",
        )
        back = lax.ppermute(give, "gy", swap)
        pays = call(
            corner_kernel,
            [shape(2, nx)] * (nz - 1),
            (ids, scal, keep, back),
            in_specs=[smem(), smem(), full(keep), full(back)],
            name="corner",
        )
        corners = [lax.ppermute(pays[k - 1], "gz", cyclic(nz, k)) for k in range(1, nz)]
        out = update(
            ids, scal, t, u, edge, keep, back, wide, halos, gots, corners, final
        )
        u, halos = out[0], out[1:]
    return u


def solution(mesh):
    placed = (P("gz", "gy", None), P("gz", "gy", None), P(), P(), P(), P(), P(), P())
    return jax.shard_map(
        body, mesh=mesh, in_specs=placed, out_specs=P("gz", "gy", None), check_vma=False
    )
```

time: 1690 us -> 156 us (0.09)
  blocking collectives: 1150 us -> 0 us
  local copies, waits for them, and re-layouts: 211 us -> 19.5 us
  matrix products: 170 us -> 0 us
  other arithmetic: 129 us -> 0.07 us
  Pallas kernels: 0 us -> 80 us
  starting transfers between devices: 18.8 us -> 38.7 us
    all_to_all x8 -> x0, blocking collectives: 1150 us -> none  [the longest x2 378 us: body(): moved = lax.all_to_all(moved, 'gy', split_axis=0, concat_axis=1, tiled=True)]
    dot_general x6 -> x0, matrix products: 170 us -> none  [the longest x2 79.8 us: along_x(): jnp.einsum('zyx,wx->zyw', field, inverse, precision=lax.Precision.HIGHEST)]
    pallas_call x0 -> x11, Pallas kernels: none -> 80 us  [call(): pl.pallas_call(kernel, out_shape=out_shape, compiler_params=pltpu.Compile...]
    all_to_all x11 -> x0, local copies, waits for them, and re-layouts: 73.2 us -> none  [the longest x5 52.7 us: body(): moved = lax.all_to_all(moved, 'gz', split_axis=2, concat_axis=0, tiled=True)]
    all_to_all x2 -> x0, other arithmetic: 56.4 us -> none  [body(): moved = lax.all_to_all(moved, 'gz', split_axis=2, concat_axis=0, tiled=True)]
    dot_general x4 -> x0, local copies, waits for them, and re-layouts: 50.7 us -> none  [the longest x2 32.4 us: along_x(): jnp.einsum('zyx,wx->zyw', field, inverse, precision=lax.Precision.HIGHEST)]
    unnamed x22 -> x16, local copies, waits for them, and re-layouts: 62.5 us -> 14.5 us
    mul x6 -> x0, other arithmetic: 47.2 us -> none  [the longest x2 20.8 us: stencil(): flux_x = jnp.pad(jnp.diff(field, axis=2) * cond_x, ((0, 0), (0, 0), (1, 1)))]
  transfers between devices with their start and end apart: 8 -> 26, of which waited for: 2 -> 13; matrix products, arithmetic and copies ran while one was open for 2% -> 3% of each run, Pallas kernels for 0% -> 3%
where the time goes in v2:
time: 156 us; the launch traced here: 155 us
  Pallas kernels  80 us (51%)
  starting transfers between devices  38.7 us (25%)
  local copies, waits for them, and re-layouts  19.5 us (12%)
  waiting for transfers between devices  16.5 us (11%)
    pallas_call x11, Pallas kernels, call(): pl.pallas_call(kernel, out_shape=out_shape, compiler_params=pltpu.Compile...  80 us
    unnamed x16, local copies, waits for them, and re-layouts  14.5 us
    ppermute x6, starting transfers between devices, body(): lax.ppermute(pays[k - 1], 'gy', cyclic(ny, k, 2))  9.86 us
    ppermute x6, starting transfers between devices, body(): gots.append(lax.ppermute(pays[k - 1], 'gz', cyclic(nz, k)))  8.31 us
    ppermute x6, starting transfers between devices, body(): lax.ppermute(pays[k - 1], 'gz', cyclic(nz, k))  7.58 us
    ppermute x6, waiting for transfers between devices, body(): lax.ppermute(pays[k - 1], 'gy', cyclic(ny, k, 2))  7.07 us
    ppermute x1, starting transfers between devices, halo(): zlo = lax.ppermute(u[-1], 'gz', up(nz))  5.52 us
    ppermute x6, waiting for transfers between devices, body(): lax.ppermute(pays[k - 1], 'gz', cyclic(nz, k))  4.42 us
  transfers between devices with their start and end apart: 26, of which 13 were waited for; matrix products, arithmetic and copies ran while one was open for 3% of the time, Pallas kernels for 3%

profile of v2, /device:TPU:0, one launch (start us, length us, event | category | flops | bytes accessed | tf_op | source)
XLA Modules:
  0.0 155.0 jit_solution(5173294945679669623)
XLA Ops:
  0.0 1.1 slice_bitcast_fusion
  1.1 1.3 collective-permute-start.3
  2.4 5.5 %collective-permute-start.2 = (f32[64,1024]{1,0:T(8,128)S(1)}, f32[64,1024]{1,0:T(8,128)S(1)}, u32[]{:S(2)}, u32[]{:S(2)}) collective-permute-start(f32[64,1024]{1,0:T(8,128)S(1)} %get-tuple-element.90), channel_id=1, source_target_pairs={{0,1},{1,2},{2,3},{4,5},{5,6},{6,7},{8,9},{9,10},{10,11},{12,13},{... | collective-permute-start | bytes 786440 | tf_op jit(solution)/shard_map/ppermute | solution.py:624
  7.9 1.8 %fusion = (f32[32,1,1024]{2,1,0:T(1,128)S(1)}, f32[32,1,1024]{2,1,0:T(1,128)S(1)}) fusion(f32[32,64,1024]{2,1,0:T(8,128)} %u_ref.3), kind=kLoop, calls=%fused_computation.5 | loop fusion | bytes 524288 | tf_op jit(solution)/shard_map/slice | solution.py:623
  9.7 1.5 collective-permute-start
  11.2 1.3 collective-permute-start.1
  12.5 0.7 pad.13
  13.2 0.7 pad.14
  13.9 0.8 pad.12
  14.7 0.1 pad_add_fusion.ids_ref
  14.8 2.2 %copy-done.2 = f32[1024,1024]{1,0:T(8,128)S(1)} copy-done((f32[1024,1024]{1,0:T(8,128)S(1)}, f32[1024,1024]{1,0:T(8,128)}, u32[]{:S(2)}) %copy-start.2) | copy-done | bytes 4194328
  17.0 1.2 copy-done.5
  18.2 0.8 copy-done.6
  19.0 2.0 %tables.1 = (bf16[4,256,256]{2,1,0:T(8,128)(2,1)S(1)}, bf16[4,256,256]{2,1,0:T(8,128)(2,1)S(1)}, f32[1,1024]{1,0:T(1,128)S(1)}, f32[1,1024]{1,0:T(1,128)S(1)}, f...) custom-call(s32[2]{0:T(128)S(1)} %pad_add_fusion.ids_ref, ...), custom_call_target="tpu_custom_call" | custom-call | tf_op jit(solution)/shard_map/tables/pallas_call | solution.py:47
  21.0 0.0 collective-permute-done.3.zhi_ref
  21.1 27.5 %explicit.2 = (f32[32,64,1024]{2,1,0:T(8,128)}, f32[32,8,1024]{2,1,0:T(8,128)S(1)}, f32[2,16,1024]{2,1,0:T(8,128)S(1)}, f32[2,16,1024]{2,1,0:T(8,128)S(1)}, f32[...) custom-call(s32[2]{0:T(128)S(1)} %pad_add_fusion.ids_ref, ...), custom_call_target="tpu_custom_call" | custom-call | tf_op jit(solution)/shard_map/explicit/pallas_call | solution.py:47
  48.6 3.3 %collective-permute-start.4 = (f32[2,16,1024]{2,1,0:T(8,128)S(1)}, f32[2,16,1024]{2,1,0:T(8,128)S(1)}, u32[]{:S(2)}, u32[]{:S(2)}) collective-permute-start(f32[2,16,1024]{2,1,0:T(8,128)S(1)} %get-tuple-element.57), channel_id=1, source_target_pairs={{0,4},{4,0},{8,12},{12,8},{16,20},{20,16},{24,28},{28,24},{1,5},{5... | collective-permute-start | bytes 393224 | tf_op jit(solution)/shard_map/ppermute | solution.py:648
  51.8 1.0 collective-permute-done.4.other_ref
  52.8 0.7 chip.2
  53.5 2.0 %collective-permute-start.5 = (f32[16,1024]{1,0:T(8,128)S(1)}, f32[16,1024]{1,0:T(8,128)S(1)}, u32[]{:S(2)}, u32[]{:S(2)}) collective-permute-start(f32[16,1024]{1,0:T(8,128)S(1)} %get-tuple-element.58), channel_id=1, source_target_pairs={{0,8},{4,12},{8,16},{12,20},{16,24},{20,28},{24,0},{28,4},{1,9},{5... | collective-permute-start | bytes 196616 | tf_op jit(solution)/shard_map/ppermute | solution.py:657
  55.6 2.4 %collective-permute-start.9 = (f32[64,1024]{1,0:T(8,128)S(1)}, f32[64,1024]{1,0:T(8,128)S(1)}, u32[]{:S(2)}, u32[]{:S(2)}) collective-permute-start(f32[64,1024]{1,0:T(8,128)S(1)} %get-tuple-element.63), channel_id=1, source_target_pairs={{0,1},{1,2},{2,3},{3,0},{4,5},{5,6},{6,7},{7,4},{8,9},{9,10},{10,1... | collective-permute-start | bytes 786440 | tf_op jit(solution)/shard_map/ppermute | solution.py:647
  57.9 2.1 %collective-permute-start.11 = (f32[64,1024]{1,0:T(8,128)S(1)}, f32[64,1024]{1,0:T(8,128)S(1)}, u32[]{:S(2)}, u32[]{:S(2)}) collective-permute-start(f32[64,1024]{1,0:T(8,128)S(1)} %get-tuple-element.65), channel_id=1, source_target_pairs={{0,3},{1,0},{2,1},{3,2},{4,7},{5,4},{6,5},{7,6},{8,11},{9,8},{10,9... | collective-permute-start | bytes 786440 | tf_op jit(solution)/shard_map/ppermute | solution.py:647
  60.0 2.6 %collective-permute-start.6 = (f32[16,1024]{1,0:T(8,128)S(1)}, f32[16,1024]{1,0:T(8,128)S(1)}, u32[]{:S(2)}, u32[]{:S(2)}) collective-permute-start(f32[16,1024]{1,0:T(8,128)S(1)} %get-tuple-element.59), channel_id=1, source_target_pairs={{0,16},{4,20},{8,24},{12,28},{16,0},{20,4},{24,8},{28,12},{1,17},{... | collective-permute-start | bytes 196616 | tf_op jit(solution)/shard_map/ppermute | solution.py:657
  62.6 0.0 collective-permute-done.5.rest_0_
  62.6 1.3 collective-permute-start.7
  64.0 2.5 %collective-permute-done.6.rest_1_ = f32[16,1024]{1,0:T(8,128)S(1)} collective-permute-done((f32[16,1024]{1,0:T(8,128)S(1)}, f32[16,1024]{1,0:T(8,128)S(1)}, u32[]{:S(2)}, u32[]{:S(2)}) %collective-permute-start.6) | collective-permute-done | bytes 65568 | tf_op jit(solution)/shard_map/ppermute | solution.py:657
  66.5 0.5 collective-permute-done.7.rest_2_
  66.9 0.7 share.2
  67.7 0.1 collective-permute-start.8
  67.7 1.3 collective-permute-done.8.back_ref
  69.1 0.8 corner.2
  69.8 0.1 collective-permute-start.12
  70.0 1.9 %collective-permute-start.13 = (f32[2,1024]{1,0:T(2,128)S(1)}, f32[2,1024]{1,0:T(2,128)S(1)}, u32[]{:S(2)}, u32[]{:S(2)}) collective-permute-start(f32[2,1024]{1,0:T(2,128)S(1)} %get-tuple-element.67), channel_id=1, source_target_pairs={{0,2},{1,3},{2,0},{3,1},{4,6},{5,7},{6,4},{7,5},{8,10},{9,11},{10,... | collective-permute-start | bytes 24584 | tf_op jit(solution)/shard_map/ppermute | solution.py:675
  71.9 1.5 collective-permute-start.14
  73.3 0.0 collective-permute-done.11.rest_2_
  73.3 1.1 collective-permute-done.12.rest_3_
  74.5 1.1 collective-permute-done.14.rest_5_
  75.5 3.4 %copy-done.3 = f32[32,64,1024]{2,1,0:T(8,128)S(1)} copy-done((f32[32,64,1024]{2,1,0:T(8,128)S(1)}, f32[32,64,1024]{2,1,0:T(8,128)}, u32[]{:S(2)}) %copy-start.3) | copy-done | bytes 8388632
  78.9 10.1 %update.2 = (f32[32,64,1024]{2,1,0:T(8,128)S(1)}, f32[32,1024]{1,0:T(8,128)S(1)}, f32[32,1024]{1,0:T(8,128)S(1)}, f32[64,1024]{1,0:T(8,128)S(1)}, f32[64,1024]{1,0:T(8,128)S(1)}) custom-call(s32[2]{0:T(128)S(1)} %pad_add_fusion.ids_ref, f32[16,128]{1,0:T(8,128)S(1)} %get-tuple-element.47.scal_ref, f32[32,64,1024]{2,1,0:T(8,128)S(1)} %copy-done.3, ...), custom_call_target="tpu_custom_call" | custom-call | tf_op jit(solution)/shard_map/update/pallas_call | solution.py:47
  89.0 0.0 copy-start
  89.0 3.4 %copy-done = f32[32,64,1024]{2,1,0:T(8,128)} copy-done((f32[32,64,1024]{2,1,0:T(8,128)}, f32[32,64,1024]{2,1,0:T(8,128)S(1)}, u32[]{:S(2)}) %copy-start) | copy-done | bytes 8388632
  92.4 27.7 %explicit.3 = (f32[32,64,1024]{2,1,0:T(8,128)}, f32[32,8,1024]{2,1,0:T(8,128)S(1)}, f32[2,16,1024]{2,1,0:T(8,128)S(1)}, f32[2,16,1024]{2,1,0:T(8,128)S(1)}, f32[...) custom-call(s32[2]{0:T(128)S(1)} %pad_add_fusion.ids_ref, ...), custom_call_target="tpu_custom_call" | custom-call | tf_op jit(solution)/shard_map/explicit/pallas_call | solution.py:47
  120.1 1.3 collective-permute-done.15.other_ref
  121.4 0.7 chip.3
  122.1 0.7 collective-permute-start.16
  122.9 2.4 %collective-permute-start.20 = (f32[64,1024]{1,0:T(8,128)S(1)}, f32[64,1024]{1,0:T(8,128)S(1)}, u32[]{:S(2)}, u32[]{:S(2)}) collective-permute-start(f32[64,1024]{1,0:T(8,128)S(1)} %get-tuple-element.83), channel_id=1, source_target_pairs={{0,1},{1,2},{2,3},{3,0},{4,5},{5,6},{6,7},{7,4},{8,9},{9,10},{10,1... | collective-permute-start | bytes 786440 | tf_op jit(solution)/shard_map/ppermute | solution.py:647
  125.3 0.5 collective-permute-start.21
  125.8 1.0 collective-permute-start.22
  126.7 3.0 %collective-permute-start.17 = (f32[16,1024]{1,0:T(8,128)S(1)}, f32[16,1024]{1,0:T(8,128)S(1)}, u32[]{:S(2)}, u32[]{:S(2)}) collective-permute-start(f32[16,1024]{1,0:T(8,128)S(1)} %get-tuple-element.79), channel_id=1, source_target_pairs={{0,16},{4,20},{8,24},{12,28},{16,0},{20,4},{24,8},{28,12},{1,17},{... | collective-permute-start | bytes 196616 | tf_op jit(solution)/shard_map/ppermute | solution.py:657
  129.7 0.2 collective-permute-start.18
  129.9 3.3 %collective-permute-done.17.rest_1_ = f32[16,1024]{1,0:T(8,128)S(1)} collective-permute-done((f32[16,1024]{1,0:T(8,128)S(1)}, f32[16,1024]{1,0:T(8,128)S(1)}, u32[]{:S(2)}, u32[]{:S(2)}) %collective-permute-start.17) | collective-permute-done | bytes 65568 | tf_op jit(solution)/shard_map/ppermute | solution.py:657
  133.2 0.8 collective-permute-done.18.rest_2_
  134.0 0.7 share.3
  134.7 0.1 collective-permute-start.19
  134.8 1.3 collective-permute-done.19.back_ref
  136.1 0.8 corner.3
  136.9 1.2 collective-permute-start.23
  138.0 1.5 collective-permute-start.24
  139.6 1.4 collective-permute-start.25
  141.0 0.5 collective-permute-done.23.rest_3_
  141.5 0.2 collective-permute-done.24.rest_4_
  141.7 1.5 collective-permute-done.25.rest_5_
  143.2 3.4 %copy-done.4 = f32[32,64,1024]{2,1,0:T(8,128)S(1)} copy-done((f32[32,64,1024]{2,1,0:T(8,128)S(1)}, f32[32,64,1024]{2,1,0:T(8,128)}, u32[]{:S(2)}) %copy-start.4) | copy-done | bytes 8388632
  146.6 8.4 %update.3 = f32[32,64,1024]{2,1,0:T(8,128)} custom-call(s32[2]{0:T(128)S(1)} %pad_add_fusion.ids_ref, f32[16,128]{1,0:T(8,128)S(1)} %get-tuple-element.47.scal_ref, f32[32,64,1024]{2,1,0:T(8,128)S(1)} %copy-done.4, f32[32,64,1024]{2,1,0:T(8,128)S(1)} %copy-done.1, f32[32,8,1024]{2,1,0:T(8,128)S(1)} %get-tuple-element.75.edge_ref, ...), custom_call_target="tpu_custom_call" | custom-call | tf_op jit(solution)/shard_map/update/pallas_call | solution.py:47
  (23 shorter events, 0.1 us)
Async XLA Ops:
  1.1 20.0 %collective-permute-start.3 = (f32[64,1024]{1,0:T(8,128)S(1)}, f32[64,1024]{1,0:T(8,128)S(1)}, u32[]{:S(2)}, u32[]{:S(2)}) collective-permute-start(f32[64,1024]{1,0:T(8,128)S(1)} %get-tuple-element.89), channel_id=1, source_target_pairs={{1,0},{2,1},{3,2},{5,4},{6,5},{7,6},{9,8},{10,9},{11,10},{13,12},{... | collective-permute-start | bytes 786440 | tf_op jit(solution)/shard_map/ppermute | solution.py:625
  2.4 18.7 %collective-permute-start.2 = (f32[64,1024]{1,0:T(8,128)S(1)}, f32[64,1024]{1,0:T(8,128)S(1)}, u32[]{:S(2)}, u32[]{:S(2)}) collective-permute-start(f32[64,1024]{1,0:T(8,128)S(1)} %get-tuple-element.90), channel_id=1, source_target_pairs={{0,1},{1,2},{2,3},{4,5},{5,6},{6,7},{8,9},{9,10},{10,11},{12,13},{... | collective-permute-start | bytes 786440 | tf_op jit(solution)/shard_map/ppermute | solution.py:624
  9.7 11.3 %collective-permute-start = (f32[32,1024]{1,0:T(8,128)S(1)}, f32[32,1024]{1,0:T(8,128)S(1)}, u32[]{:S(2)}, u32[]{:S(2)}) collective-permute-start(f32[32,1024]{1,0:T(8,128)S(1)} %bitcast.15), channel_id=1, source_target_pairs={{0,4},{4,8},{8,12},{12,16},{16,20},{20,24},{24,28},{1,5},{5,9},{9,... | collective-permute-start | bytes 393224 | tf_op jit(solution)/shard_map/ppermute | solution.py:622
  11.2 9.8 %collective-permute-start.1 = (f32[32,1024]{1,0:T(8,128)S(1)}, f32[32,1024]{1,0:T(8,128)S(1)}, u32[]{:S(2)}, u32[]{:S(2)}) collective-permute-start(f32[32,1024]{1,0:T(8,128)S(1)} %bitcast.16), channel_id=1, source_target_pairs={{4,0},{8,4},{12,8},{16,12},{20,16},{24,20},{28,24},{5,1},{9,5},{13... | collective-permute-start | bytes 393224 | tf_op jit(solution)/shard_map/ppermute | solution.py:623
  14.8 2.2 %copy-start.2 = (f32[1024,1024]{1,0:T(8,128)S(1)}, f32[1024,1024]{1,0:T(8,128)}, u32[]{:S(2)}) copy-start(f32[1024,1024]{1,0:T(8,128)} %upiv_ref.1) | copy-start | bytes 12582916
  17.0 1.2 copy-start.5
  18.2 0.8 copy-start.6
  48.6 4.3 %collective-permute-start.4 = (f32[2,16,1024]{2,1,0:T(8,128)S(1)}, f32[2,16,1024]{2,1,0:T(8,128)S(1)}, u32[]{:S(2)}, u32[]{:S(2)}) collective-permute-start(f32[2,16,1024]{2,1,0:T(8,128)S(1)} %get-tuple-element.57), channel_id=1, source_target_pairs={{0,4},{4,0},{8,12},{12,8},{16,20},{20,16},{24,28},{28,24},{1,5},{5... | collective-permute-start | bytes 393224 | tf_op jit(solution)/shard_map/ppermute | solution.py:648
  53.5 9.1 %collective-permute-start.5 = (f32[16,1024]{1,0:T(8,128)S(1)}, f32[16,1024]{1,0:T(8,128)S(1)}, u32[]{:S(2)}, u32[]{:S(2)}) collective-permute-start(f32[16,1024]{1,0:T(8,128)S(1)} %get-tuple-element.58), channel_id=1, source_target_pairs={{0,8},{4,12},{8,16},{12,20},{16,24},{20,28},{24,0},{28,4},{1,9},{5... | collective-permute-start | bytes 196616 | tf_op jit(solution)/shard_map/ppermute | solution.py:657
  55.6 16.3 %collective-permute-start.9 = (f32[64,1024]{1,0:T(8,128)S(1)}, f32[64,1024]{1,0:T(8,128)S(1)}, u32[]{:S(2)}, u32[]{:S(2)}) collective-permute-start(f32[64,1024]{1,0:T(8,128)S(1)} %get-tuple-element.63), channel_id=1, source_target_pairs={{0,1},{1,2},{2,3},{3,0},{4,5},{5,6},{6,7},{7,4},{8,9},{9,10},{10,1... | collective-permute-start | bytes 786440 | tf_op jit(solution)/shard_map/ppermute | solution.py:647
  57.9 15.4 %collective-permute-start.10 = (f32[64,1024]{1,0:T(8,128)S(1)}, f32[64,1024]{1,0:T(8,128)S(1)}, u32[]{:S(2)}, u32[]{:S(2)}) collective-permute-start(f32[64,1024]{1,0:T(8,128)S(1)} %get-tuple-element.64), channel_id=1, source_target_pairs={{0,2},{1,3},{2,0},{3,1},{4,6},{5,7},{6,4},{7,5},{8,10},{9,11},{10,... | collective-permute-start | bytes 786440 | tf_op jit(solution)/shard_map/ppermute | solution.py:647
  57.9 15.4 %collective-permute-start.11 = (f32[64,1024]{1,0:T(8,128)S(1)}, f32[64,1024]{1,0:T(8,128)S(1)}, u32[]{:S(2)}, u32[]{:S(2)}) collective-permute-start(f32[64,1024]{1,0:T(8,128)S(1)} %get-tuple-element.65), channel_id=1, source_target_pairs={{0,3},{1,0},{2,1},{3,2},{4,7},{5,4},{6,5},{7,6},{8,11},{9,8},{10,9... | collective-permute-start | bytes 786440 | tf_op jit(solution)/shard_map/ppermute | solution.py:647
  60.0 6.4 %collective-permute-start.6 = (f32[16,1024]{1,0:T(8,128)S(1)}, f32[16,1024]{1,0:T(8,128)S(1)}, u32[]{:S(2)}, u32[]{:S(2)}) collective-permute-start(f32[16,1024]{1,0:T(8,128)S(1)} %get-tuple-element.59), channel_id=1, source_target_pairs={{0,16},{4,20},{8,24},{12,28},{16,0},{20,4},{24,8},{28,12},{1,17},{... | collective-permute-start | bytes 196616 | tf_op jit(solution)/shard_map/ppermute | solution.py:657
  62.6 4.3 %collective-permute-start.7 = (f32[16,1024]{1,0:T(8,128)S(1)}, f32[16,1024]{1,0:T(8,128)S(1)}, u32[]{:S(2)}, u32[]{:S(2)}) collective-permute-start(f32[16,1024]{1,0:T(8,128)S(1)} %get-tuple-element.60), channel_id=1, source_target_pairs={{0,24},{4,28},{8,0},{12,4},{16,8},{20,12},{24,16},{28,20},{1,25},{... | collective-permute-start | bytes 196616 | tf_op jit(solution)/shard_map/ppermute | solution.py:657
  67.7 1.4 collective-permute-start.8
  69.8 4.6 %collective-permute-start.12 = (f32[2,1024]{1,0:T(2,128)S(1)}, f32[2,1024]{1,0:T(2,128)S(1)}, u32[]{:S(2)}, u32[]{:S(2)}) collective-permute-start(f32[2,1024]{1,0:T(2,128)S(1)} %get-tuple-element.66), channel_id=1, source_target_pairs={{0,1},{1,2},{2,3},{3,0},{4,5},{5,6},{6,7},{7,4},{8,9},{9,10},{10,1... | collective-permute-start | bytes 24584 | tf_op jit(solution)/shard_map/ppermute | solution.py:675
  70.0 4.5 %collective-permute-start.13 = (f32[2,1024]{1,0:T(2,128)S(1)}, f32[2,1024]{1,0:T(2,128)S(1)}, u32[]{:S(2)}, u32[]{:S(2)}) collective-permute-start(f32[2,1024]{1,0:T(2,128)S(1)} %get-tuple-element.67), channel_id=1, source_target_pairs={{0,2},{1,3},{2,0},{3,1},{4,6},{5,7},{6,4},{7,5},{8,10},{9,11},{10,... | collective-permute-start | bytes 24584 | tf_op jit(solution)/shard_map/ppermute | solution.py:675
  71.9 3.7 %collective-permute-start.14 = (f32[2,1024]{1,0:T(2,128)S(1)}, f32[2,1024]{1,0:T(2,128)S(1)}, u32[]{:S(2)}, u32[]{:S(2)}) collective-permute-start(f32[2,1024]{1,0:T(2,128)S(1)} %get-tuple-element.68), channel_id=1, source_target_pairs={{0,3},{1,0},{2,1},{3,2},{4,7},{5,4},{6,5},{7,6},{8,11},{9,8},{10,9... | collective-permute-start | bytes 24584 | tf_op jit(solution)/shard_map/ppermute | solution.py:675
  75.5 3.4 %copy-start.3 = (f32[32,64,1024]{2,1,0:T(8,128)S(1)}, f32[32,64,1024]{2,1,0:T(8,128)}, u32[]{:S(2)}) copy-start(f32[32,64,1024]{2,1,0:T(8,128)} %get-tuple-element.54.t_ref) | copy-start | bytes 25165828
  89.0 3.4 %copy-start = (f32[32,64,1024]{2,1,0:T(8,128)}, f32[32,64,1024]{2,1,0:T(8,128)S(1)}, u32[]{:S(2)}) copy-start(f32[32,64,1024]{2,1,0:T(8,128)S(1)} %get-tuple-element.69.u_ref.below_ref.above_ref) | copy-start | bytes 25165828
  92.4 50.8 %copy-start.1 = (f32[32,64,1024]{2,1,0:T(8,128)S(1)}, f32[32,64,1024]{2,1,0:T(8,128)}, u32[]{:S(2)}) copy-start(f32[32,64,1024]{2,1,0:T(8,128)} %copy-done) | copy-start | bytes 25165828
  120.1 1.3 collective-permute-start.15
  122.1 7.6 %collective-permute-start.16 = (f32[16,1024]{1,0:T(8,128)S(1)}, f32[16,1024]{1,0:T(8,128)S(1)}, u32[]{:S(2)}, u32[]{:S(2)}) collective-permute-start(f32[16,1024]{1,0:T(8,128)S(1)} %get-tuple-element.78), channel_id=1, source_target_pairs={{0,8},{4,12},{8,16},{12,20},{16,24},{20,28},{24,0},{28,4},{1,9},{5... | collective-permute-start | bytes 196616 | tf_op jit(solution)/shard_map/ppermute | solution.py:657
  122.9 16.7 %collective-permute-start.20 = (f32[64,1024]{1,0:T(8,128)S(1)}, f32[64,1024]{1,0:T(8,128)S(1)}, u32[]{:S(2)}, u32[]{:S(2)}) collective-permute-start(f32[64,1024]{1,0:T(8,128)S(1)} %get-tuple-element.83), channel_id=1, source_target_pairs={{0,1},{1,2},{2,3},{3,0},{4,5},{5,6},{6,7},{7,4},{8,9},{9,10},{10,1... | collective-permute-start | bytes 786440 | tf_op jit(solution)/shard_map/ppermute | solution.py:647
  125.3 15.7 %collective-permute-start.21 = (f32[64,1024]{1,0:T(8,128)S(1)}, f32[64,1024]{1,0:T(8,128)S(1)}, u32[]{:S(2)}, u32[]{:S(2)}) collective-permute-start(f32[64,1024]{1,0:T(8,128)S(1)} %get-tuple-element.84), channel_id=1, source_target_pairs={{0,2},{1,3},{2,0},{3,1},{4,6},{5,7},{6,4},{7,5},{8,10},{9,11},{10,... | collective-permute-start | bytes 786440 | tf_op jit(solution)/shard_map/ppermute | solution.py:647
  125.8 15.2 %collective-permute-start.22 = (f32[64,1024]{1,0:T(8,128)S(1)}, f32[64,1024]{1,0:T(8,128)S(1)}, u32[]{:S(2)}, u32[]{:S(2)}) collective-permute-start(f32[64,1024]{1,0:T(8,128)S(1)} %get-tuple-element.85), channel_id=1, source_target_pairs={{0,3},{1,0},{2,1},{3,2},{4,7},{5,4},{6,5},{7,6},{8,11},{9,8},{10,9... | collective-permute-start | bytes 786440 | tf_op jit(solution)/shard_map/ppermute | solution.py:647
  126.7 6.4 %collective-permute-start.17 = (f32[16,1024]{1,0:T(8,128)S(1)}, f32[16,1024]{1,0:T(8,128)S(1)}, u32[]{:S(2)}, u32[]{:S(2)}) collective-permute-start(f32[16,1024]{1,0:T(8,128)S(1)} %get-tuple-element.79), channel_id=1, source_target_pairs={{0,16},{4,20},{8,24},{12,28},{16,0},{20,4},{24,8},{28,12},{1,17},{... | collective-permute-start | bytes 196616 | tf_op jit(solution)/shard_map/ppermute | solution.py:657
  129.7 4.3 %collective-permute-start.18 = (f32[16,1024]{1,0:T(8,128)S(1)}, f32[16,1024]{1,0:T(8,128)S(1)}, u32[]{:S(2)}, u32[]{:S(2)}) collective-permute-start(f32[16,1024]{1,0:T(8,128)S(1)} %get-tuple-element.80), channel_id=1, source_target_pairs={{0,24},{4,28},{8,0},{12,4},{16,8},{20,12},{24,16},{28,20},{1,25},{... | collective-permute-start | bytes 196616 | tf_op jit(solution)/shard_map/ppermute | solution.py:657
  134.7 1.4 collective-permute-start.19
  136.9 4.6 %collective-permute-start.23 = (f32[2,1024]{1,0:T(2,128)S(1)}, f32[2,1024]{1,0:T(2,128)S(1)}, u32[]{:S(2)}, u32[]{:S(2)}) collective-permute-start(f32[2,1024]{1,0:T(2,128)S(1)} %get-tuple-element.86), channel_id=1, source_target_pairs={{0,1},{1,2},{2,3},{3,0},{4,5},{5,6},{6,7},{7,4},{8,9},{9,10},{10,1... | collective-permute-start | bytes 24584 | tf_op jit(solution)/shard_map/ppermute | solution.py:675
  138.0 3.7 %collective-permute-start.24 = (f32[2,1024]{1,0:T(2,128)S(1)}, f32[2,1024]{1,0:T(2,128)S(1)}, u32[]{:S(2)}, u32[]{:S(2)}) collective-permute-start(f32[2,1024]{1,0:T(2,128)S(1)} %get-tuple-element.87), channel_id=1, source_target_pairs={{0,2},{1,3},{2,0},{3,1},{4,6},{5,7},{6,4},{7,5},{8,10},{9,11},{10,... | collective-permute-start | bytes 24584 | tf_op jit(solution)/shard_map/ppermute | solution.py:675
  139.6 3.7 %collective-permute-start.25 = (f32[2,1024]{1,0:T(2,128)S(1)}, f32[2,1024]{1,0:T(2,128)S(1)}, u32[]{:S(2)}, u32[]{:S(2)}) collective-permute-start(f32[2,1024]{1,0:T(2,128)S(1)} %get-tuple-element.88), channel_id=1, source_target_pairs={{0,3},{1,0},{2,1},{3,2},{4,7},{5,4},{6,5},{7,6},{8,11},{9,8},{10,9... | collective-permute-start | bytes 24584 | tf_op jit(solution)/shard_map/ppermute | solution.py:675
  143.2 3.4 %copy-start.4 = (f32[32,64,1024]{2,1,0:T(8,128)S(1)}, f32[32,64,1024]{2,1,0:T(8,128)}, u32[]{:S(2)}) copy-start(f32[32,64,1024]{2,1,0:T(8,128)} %get-tuple-element.74.t_ref) | copy-start | bytes 25165828

commit v3 on v2

--- a/solution.py
+++ b/solution.py
@@ -14,10 +14,13 @@
 SUB = 8
 XB = 256
 ZB = 8
+VL1 = 30
+VL2 = 20
 
 DIAG, UP, DOWN, SUM_UP, SUM_DOWN, COND, MISC, CHIPS, LINES = range(9)
 TABLE_ROWS = 16
 Z_LOW, Z_HIGH, Y_LOW, Y_HIGH, MIX, KEEP, GIVE = 0, 1, 2, 3, 4, 8, 12
+LARGE = 2**20
 FAR = 64
 
 f32 = jnp.float32
@@ -34,6 +37,9 @@
     return jnp.concatenate([ref[rows]] * (nx // LANES), axis=1)
 
 
+VMEM_WHOLE = pl.BlockSpec(memory_space=pltpu.VMEM)
+
+
 def full(a):
     return pl.BlockSpec(a.shape, lambda *_: (0,) * len(a.shape))
 
@@ -44,6 +50,22 @@
 
 def call(kernel, out_shape, operands, **kw):
     limit = kw.pop("vmem", 16)
+    large = kw.pop("large", LARGE)
+    resident = kw.pop("resident", ())
+    operands = [
+        pltpu.with_memory_space_constraint(a, pltpu.HBM)
+        if a.size >= large and s is not VMEM_WHOLE
+        else a
+        for a, s in zip(operands, kw["in_specs"])
+    ]
+    out_shape = [
+        pltpu.VMEM(a.shape, a.dtype)
+        if i in resident
+        else pltpu.HBM(a.shape, a.dtype)
+        if a.size >= large
+        else a
+        for i, a in enumerate(out_shape)
+    ]
     return pl.pallas_call(
         kernel,
         out_shape=out_shape,
@@ -265,26 +287,38 @@
             full(shape(2 * rows, 2 * rows)),
             full(shape(TABLE_ROWS, LANES)),
         ],
+        large=2**14,
         name="tables",
     )
 
 
 def explicit_kernel(
-    ids_ref, scal_ref, u_ref, below_ref, above_ref, o_ref, ylo_ref, yhi_ref,
-    zlo_ref, zhi_ref, cx_ref, wide_ref, ay_ref, axh_ref, axl_ref, xlo_ref, xhi_ref,
-    t_ref, edge_ref, mine_ref, theirs_ref, *rest, nz,
+    ids_ref, scal_ref, *rest, nz, resident,
 ):
+    if resident:
+        u_ref, *rest = rest
+    else:
+        u_ref, below_ref, above_ref, *rest = rest
+    o_ref, ylo_ref, yhi_ref, zlo_ref, zhi_ref, cx_ref, wide_ref, *rest = rest
+    ay_ref, axh_ref, axl_ref, xlo_ref, xhi_ref, *rest = rest
+    t_ref, edge_ref, mine_ref, theirs_ref, *rest = rest
     pays = rest[: nz - 1]
     rhs_ref, line_ref, sy_ref, sz_ref, low_ref, high_ref = rest[nz - 1 :]
     step = pl.program_id(0)
     steps = pl.num_programs(0)
-    zb, rows, nx = u_ref.shape
+    zb, rows, nx = o_ref.shape
     tiles = rows // SUB
     blocks = nx // XB
+    base_z = step * zb if resident else 0
     sub = lax.broadcasted_iota(jnp.int32, (SUB, nx), 0)
 
-    low_ref[...] = jnp.where(step > 0, below_ref[0], zlo_ref[...])
-    high_ref[...] = jnp.where(step < steps - 1, above_ref[0], zhi_ref[...])
+    if resident:
+        under = u_ref[jnp.maximum(base_z - 1, 0)]
+        over = u_ref[jnp.minimum(base_z + zb, steps * zb - 1)]
+    else:
+        under, over = below_ref[0], above_ref[0]
+    low_ref[...] = jnp.where(step > 0, under, zlo_ref[...])
+    high_ref[...] = jnp.where(step < steps - 1, over, zhi_ref[...])
 
     def plane(z, below, above):
         zz = step * zb + z
@@ -292,12 +326,12 @@
         c_up = scal_ref[COND, zz + 1]
         cx = jnp.broadcast_to(cx_ref[...], (SUB, nx))
         before = jnp.broadcast_to(ylo_ref[pl.ds(zz, 1), :], (SUB, nx))
-        current = u_ref[z, :SUB, :]
+        current = u_ref[base_z + z, :SUB, :]
         down_roll = pltpu.roll(current, 1, 0)
         for r in range(tiles):
             own = slice(r * SUB, (r + 1) * SUB)
             if r + 1 < tiles:
-                following = u_ref[z, (r + 1) * SUB : (r + 2) * SUB, :]
+                following = u_ref[base_z + z, (r + 1) * SUB : (r + 2) * SUB, :]
                 up_next = pltpu.roll(following, SUB - 1, 0)
                 down_next = pltpu.roll(following, 1, 0)
             else:
@@ -319,14 +353,18 @@
             current = following
             down_roll = down_next
 
-    plane(0, lambda own: low_ref[own, :], lambda own: u_ref[1, own, :])
+    plane(0, lambda own: low_ref[own, :], lambda own: u_ref[base_z + 1, own, :])
 
     def inner(z, carry):
-        plane(z, lambda own: u_ref[z - 1, own, :], lambda own: u_ref[z + 1, own, :])
+        plane(
+            z,
+            lambda own: u_ref[base_z + z - 1, own, :],
+            lambda own: u_ref[base_z + z + 1, own, :],
+        )
         return carry
 
     lax.fori_loop(1, zb - 1, inner, 0)
-    plane(zb - 1, lambda own: u_ref[zb - 2, own, :], lambda own: high_ref[own, :])
+    plane(zb - 1, lambda own: u_ref[base_z + zb - 2, own, :], lambda own: high_ref[own, :])
 
     dot = functools.partial(jnp.dot, preferred_element_type=f32)
     for e in range(blocks):
@@ -372,7 +410,7 @@
         both = jnp.concatenate([high, low], axis=0)
         result = dot(ay_ref[...], both)
         value = result[:rows] + result[rows:]
-        t_ref[z] = value
+        t_ref[zz] = value
         first, final = value[:1], value[rows - 1 :]
         sy_ref[0, pl.ds(z, 1), :] = final
         sy_ref[1, pl.ds(z, 1), :] = first
@@ -382,7 +420,7 @@
         sz_ref[1] = sz_ref[1] + scal_ref[SUM_DOWN, zz] * value
         return carry
 
-    lax.fori_loop(0, zb, solve, 0)
+    lax.fori_loop(0, zb, solve, 0, unroll=True)
 
     half = mine_ref.shape[1]
     part = (step * zb) // half
@@ -404,7 +442,7 @@
             pays[k - 1][...] = jnp.where(higher, sz_ref[0], sz_ref[1])
 
 
-def explicit(ids, scal, u, o, halos, tabs, cx):
+def explicit(ids, scal, u, o, halos, tabs, cx, resident):
     depth, rows, nx = u.shape
     axh, axl, xlo, xhi, wide, mat = tabs
     nz = lax.axis_size("gz")
@@ -424,12 +462,15 @@
         shape(2, half, nx),
     ] + [shape(rows, nx)] * (nz - 1)
     return call(
-        functools.partial(explicit_kernel, nz=nz),
+        functools.partial(explicit_kernel, nz=nz, resident=resident),
         outs,
-        (ids, scal, u, u, u, o, *rest),
+        (ids, scal, *([u] if resident else [u, u, u]), o, *rest),
         grid=(steps,),
-        in_specs=[smem(), smem(), field, below, above, field, *map(full, rest)],
-        out_specs=[field, pl.BlockSpec((zb, SUB, nx), lambda s: (s, 0, 0))]
+        in_specs=[smem(), smem()]
+        + ([VMEM_WHOLE] if resident else [field, below, above])
+        + [field, *map(full, rest)],
+        resident=(0,),
+        out_specs=[VMEM_WHOLE, pl.BlockSpec((zb, SUB, nx), lambda s: (s, 0, 0))]
         + [full(a) for a in outs[2:]],
         scratch_shapes=[
             pltpu.VMEM((zb * rows, nx), f32),
@@ -439,7 +480,7 @@
             pltpu.VMEM((rows, nx), f32),
             pltpu.VMEM((rows, nx), f32),
         ],
-        vmem=48,
+        vmem=VL1,
         name="explicit",
     )
 
@@ -494,7 +535,7 @@
 
 def update_kernel(
     ids_ref, scal_ref, t_ref, u_ref, edge_ref, keep_ref, back_ref, wide_ref,
-    ylo_ref, yhi_ref, zlo_ref, zhi_ref, *rest, nz, final,
+    ylo_ref, yhi_ref, zlo_ref, zhi_ref, *rest, nz, final, resident,
 ):
     gots, corners, rest = rest[: nz - 1], rest[nz - 1 : 2 * nz - 2], rest[2 * nz - 2 :]
     if final:
@@ -546,15 +587,18 @@
         below = lax.fori_loop(0, depth, backward, scal(MISC, Z_HIGH) * high, unroll=4)
         return low + below, high + above
 
+    u_own = own if resident else slice(None)
+    out_own = slice(None) if final else own
+
     def first(z, s):
-        out_ref[z] = u_ref[z] + s
+        out_ref[z, out_own, :] = u_ref[z, u_own, :] + s
 
     def second(z, b):
-        out_ref[z] = out_ref[z] + b
+        out_ref[z, out_own, :] = out_ref[z, out_own, :] + b
 
     @pl.when(r < tiles)
     def _():
-        below, above = solve(lambda got: got[own, :], lambda z: t_ref[z], first, second)
+        below, above = solve(lambda got: got[own, :], lambda z: t_ref[z, own, :], first, second)
         if not final:
             nzlo_ref[...] = zlo_ref[...] + below
             nzhi_ref[...] = zhi_ref[...] + above
@@ -583,7 +627,7 @@
             solve(ends, lambda z: edge_ref[z], keep_sum, put)
 
 
-def update(ids, scal, t, u, edge, keep, back, wide, halos, gots, corners, final):
+def update(ids, scal, t, u, edge, keep, back, wide, halos, gots, corners, final, resident):
     depth, rows, nx = u.shape
     nz = lax.axis_size("gz")
     tiles = rows // SUB
@@ -592,25 +636,26 @@
     field = pl.BlockSpec((depth, SUB, nx), lambda r: (0, clamp(r), 0))
     tile = pl.BlockSpec((SUB, nx), lambda r: (clamp(r), 0))
     outs = [shape(depth, rows, nx)]
-    out_specs = [field]
+    out_specs = [field if final else VMEM_WHOLE]
     scratch = [pltpu.VMEM((depth, SUB, nx), f32), pltpu.VMEM((2, depth, nx), f32)]
     if not final:
         outs += [shape(depth, nx)] * 2 + [shape(rows, nx)] * 2
         out_specs += [full(ylo), full(yhi), tile, tile]
         scratch += [pltpu.VMEM((depth, SUB, nx), f32)]
     return call(
-        functools.partial(update_kernel, nz=nz, final=final),
+        functools.partial(update_kernel, nz=nz, final=final, resident=resident),
         outs,
         (ids, scal, t, u, edge, keep, back, wide, ylo, yhi, zlo, zhi, *gots, *corners),
         grid=(tiles if final else tiles + 1,),
         in_specs=[
-            smem(), smem(), field, field, full(edge), full(keep), full(back), full(wide),
+            smem(), smem(), VMEM_WHOLE, VMEM_WHOLE if resident else field, full(edge), full(keep), full(back), full(wide),
             full(ylo), full(yhi), tile, tile,
             *map(full, gots), *map(full, corners),
         ],
         out_specs=out_specs,
         scratch_shapes=scratch,
-        vmem=32,
+        resident=() if final else (0,),
+        vmem=VL2,
         name="update",
     )
 
@@ -641,7 +686,9 @@
     u = phase_field
     for step in range(STEPS):
         final = step == STEPS - 1
-        t, edge, mine, theirs, *pays = explicit(ids, scal, u, others, halos, tabs, cx)
+        t, edge, mine, theirs, *pays = explicit(
+            ids, scal, u, others, halos, tabs, cx, step > 0
+        )
         gots = []
         for k in range(1, nz):
             gots.append(lax.ppermute(pays[k - 1], "gz", cyclic(nz, k)))
@@ -674,7 +721,8 @@
         )
         corners = [lax.ppermute(pays[k - 1], "gz", cyclic(nz, k)) for k in range(1, nz)]
         out = update(
-            ids, scal, t, u, edge, keep, back, wide, halos, gots, corners, final
+            ids, scal, t, u, edge, keep, back, wide, halos, gots, corners,
+            final, step > 0,
         )
         u, halos = out[0], out[1:]
     return u

time: 156 us -> 135 us (0.87)
  local copies, waits for them, and re-layouts: 19.5 us -> 8.82 us
  Pallas kernels: 80 us -> 69.6 us
    unnamed x16, local copies, waits for them, and re-layouts: 14.5 us -> 3.81 us
    pallas_call x11, Pallas kernels: 80 us -> 69.6 us  [call(): pl.pallas_call(kernel, out_shape=out_shape, compiler_params=pltpu.Compile...]
  transfers between devices with their start and end apart: 26 -> 26, of which waited for: 13 -> 13; matrix products, arithmetic and copies ran while one was open for 3% -> 3% of each run, Pallas kernels for 3% -> 6%
where the time goes in v3:
time: 135 us; the launch traced here: 134 us
  Pallas kernels  69.6 us (52%)
  starting transfers between devices  38.9 us (29%)
  waiting for transfers between devices  16.5 us (12%)
  local copies, waits for them, and re-layouts  8.82 us (7%)
    pallas_call x11, Pallas kernels, call(): pl.pallas_call(kernel, out_shape=out_shape, compiler_params=pltpu.Compile...  69.6 us
    ppermute x6, starting transfers between devices, body(): lax.ppermute(pays[k - 1], 'gy', cyclic(ny, k, 2))  9.83 us
    ppermute x6, starting transfers between devices, body(): gots.append(lax.ppermute(pays[k - 1], 'gz', cyclic(nz, k)))  8.31 us
    ppermute x6, starting transfers between devices, body(): lax.ppermute(pays[k - 1], 'gz', cyclic(nz, k))  7.58 us
    ppermute x6, waiting for transfers between devices, body(): lax.ppermute(pays[k - 1], 'gy', cyclic(ny, k, 2))  7.08 us
    ppermute x1, starting transfers between devices, halo(): zlo = lax.ppermute(u[-1], 'gz', up(nz))  5.52 us
    ppermute x6, waiting for transfers between devices, body(): lax.ppermute(pays[k - 1], 'gz', cyclic(nz, k))  4.42 us
    unnamed x16, local copies, waits for them, and re-layouts  3.81 us
  transfers between devices with their start and end apart: 26, of which 13 were waited for; matrix products, arithmetic and copies ran while one was open for 3% of the time, Pallas kernels for 6%

profile of v3, /device:TPU:0, one launch (start us, length us, event | category | flops | bytes accessed | tf_op | source)
XLA Modules:
  0.0 134.2 jit_solution(3796805667633068286)
XLA Ops:
  0.0 1.1 slice_bitcast_fusion
  1.1 1.3 collective-permute-start.3
  2.4 5.5 %collective-permute-start.2 = (f32[64,1024]{1,0:T(8,128)S(1)}, f32[64,1024]{1,0:T(8,128)S(1)}, u32[]{:S(2)}, u32[]{:S(2)}) collective-permute-start(f32[64,1024]{1,0:T(8,128)S(1)} %get-tuple-element.90), channel_id=1, source_target_pairs={{0,1},{1,2},{2,3},{4,5},{5,6},{6,7},{8,9},{9,10},{10,11},{12,13},{... | collective-permute-start | bytes 786440 | tf_op jit(solution)/shard_map/ppermute | solution.py:669
  7.9 1.8 %fusion = (f32[32,1,1024]{2,1,0:T(1,128)S(1)}, f32[32,1,1024]{2,1,0:T(1,128)S(1)}) fusion(f32[32,64,1024]{2,1,0:T(8,128)} %u_ref.1), kind=kLoop, calls=%fused_computation.5 | loop fusion | bytes 524288 | tf_op jit(solution)/shard_map/slice | solution.py:668
  9.7 1.5 %collective-permute-start = (f32[32,1024]{1,0:T(8,128)S(1)}, f32[32,1024]{1,0:T(8,128)S(1)}, u32[]{:S(2)}, u32[]{:S(2)}) collective-permute-start(f32[32,1024]{1,0:T(8,128)S(1)} %bitcast.15), channel_id=1, source_target_pairs={{0,4},{4,8},{8,12},{12,16},{16,20},{20,24},{24,28},{1,5},{5,9},{9,... | collective-permute-start | bytes 393224 | tf_op jit(solution)/shard_map/ppermute | solution.py:667
  11.2 1.3 collective-permute-start.1
  12.5 0.7 pad.13
  13.2 0.7 pad.14
  13.9 0.8 pad.12
  14.7 0.1 pad_add_fusion.ids_ref
  14.8 4.9 %tables.1 = (bf16[4,256,256]{2,1,0:T(8,128)(2,1)}, bf16[4,256,256]{2,1,0:T(8,128)(2,1)}, f32[1,1024]{1,0:T(1,128)S(1)}, f32[1,1024]{1,0:T(1,128)S(1)}, f32[4,72,...) custom-call(s32[2]{0:T(128)S(1)} %pad_add_fusion.ids_ref, f32[1024,1024]{1,0:T(8,128)} %upiv_ref.1, ...), custom_call_target="tpu_custom_call" | custom-call | tf_op jit(solution)/shard_map/tables/pallas_call | solution.py:69
  19.6 0.0 collective-permute-done.rest_4_.ylo_ref
  19.7 0.0 collective-permute-done.2.rest_6_.zlo_ref
  19.7 0.9 copy-done
  20.6 1.0 copy-done.1
  21.6 1.0 copy-done.3
  22.7 0.8 copy-done.5
  23.4 21.7 %explicit.2 = (f32[32,64,1024]{2,1,0:T(8,128)S(1)}, f32[32,8,1024]{2,1,0:T(8,128)S(1)}, f32[2,16,1024]{2,1,0:T(8,128)S(1)}, f32[2,16,1024]{2,1,0:T(8,128)S(1)}, ...) custom-call(s32[2]{0:T(128)S(1)} %pad_add_fusion.ids_ref, ...), custom_call_target="tpu_custom_call" | custom-call | tf_op jit(solution)/shard_map/explicit/pallas_call | solution.py:69
  45.2 3.4 %collective-permute-start.4 = (f32[2,16,1024]{2,1,0:T(8,128)S(1)}, f32[2,16,1024]{2,1,0:T(8,128)S(1)}, u32[]{:S(2)}, u32[]{:S(2)}) collective-permute-start(f32[2,16,1024]{2,1,0:T(8,128)S(1)} %get-tuple-element.57), channel_id=1, source_target_pairs={{0,4},{4,0},{8,12},{12,8},{16,20},{20,16},{24,28},{28,24},{1,5},{5... | collective-permute-start | bytes 393224 | tf_op jit(solution)/shard_map/ppermute | solution.py:695
  48.5 1.0 collective-permute-done.4.other_ref
  49.5 0.7 chip.2
  50.2 2.0 %collective-permute-start.5 = (f32[16,1024]{1,0:T(8,128)S(1)}, f32[16,1024]{1,0:T(8,128)S(1)}, u32[]{:S(2)}, u32[]{:S(2)}) collective-permute-start(f32[16,1024]{1,0:T(8,128)S(1)} %get-tuple-element.58), channel_id=1, source_target_pairs={{0,8},{4,12},{8,16},{12,20},{16,24},{20,28},{24,0},{28,4},{1,9},{5... | collective-permute-start | bytes 196616 | tf_op jit(solution)/shard_map/ppermute | solution.py:704
  52.3 2.4 %collective-permute-start.9 = (f32[64,1024]{1,0:T(8,128)S(1)}, f32[64,1024]{1,0:T(8,128)S(1)}, u32[]{:S(2)}, u32[]{:S(2)}) collective-permute-start(f32[64,1024]{1,0:T(8,128)S(1)} %get-tuple-element.63), channel_id=1, source_target_pairs={{0,1},{1,2},{2,3},{3,0},{4,5},{5,6},{6,7},{7,4},{8,9},{9,10},{10,1... | collective-permute-start | bytes 786440 | tf_op jit(solution)/shard_map/ppermute | solution.py:694
  54.6 0.0 collective-permute-start.10
  54.6 2.1 %collective-permute-start.11 = (f32[64,1024]{1,0:T(8,128)S(1)}, f32[64,1024]{1,0:T(8,128)S(1)}, u32[]{:S(2)}, u32[]{:S(2)}) collective-permute-start(f32[64,1024]{1,0:T(8,128)S(1)} %get-tuple-element.65), channel_id=1, source_target_pairs={{0,3},{1,0},{2,1},{3,2},{4,7},{5,4},{6,5},{7,6},{8,11},{9,8},{10,9... | collective-permute-start | bytes 786440 | tf_op jit(solution)/shard_map/ppermute | solution.py:694
  56.7 2.6 %collective-permute-start.6 = (f32[16,1024]{1,0:T(8,128)S(1)}, f32[16,1024]{1,0:T(8,128)S(1)}, u32[]{:S(2)}, u32[]{:S(2)}) collective-permute-start(f32[16,1024]{1,0:T(8,128)S(1)} %get-tuple-element.59), channel_id=1, source_target_pairs={{0,16},{4,20},{8,24},{12,28},{16,0},{20,4},{24,8},{28,12},{1,17},{... | collective-permute-start | bytes 196616 | tf_op jit(solution)/shard_map/ppermute | solution.py:704
  59.3 1.3 %collective-permute-start.7 = (f32[16,1024]{1,0:T(8,128)S(1)}, f32[16,1024]{1,0:T(8,128)S(1)}, u32[]{:S(2)}, u32[]{:S(2)}) collective-permute-start(f32[16,1024]{1,0:T(8,128)S(1)} %get-tuple-element.60), channel_id=1, source_target_pairs={{0,24},{4,28},{8,0},{12,4},{16,8},{20,12},{24,16},{28,20},{1,25},{... | collective-permute-start | bytes 196616 | tf_op jit(solution)/shard_map/ppermute | solution.py:704
  60.6 2.5 %collective-permute-done.6.rest_1_ = f32[16,1024]{1,0:T(8,128)S(1)} collective-permute-done((f32[16,1024]{1,0:T(8,128)S(1)}, f32[16,1024]{1,0:T(8,128)S(1)}, u32[]{:S(2)}, u32[]{:S(2)}) %collective-permute-start.6) | collective-permute-done | bytes 65568 | tf_op jit(solution)/shard_map/ppermute | solution.py:704
  63.1 0.5 collective-permute-done.7.rest_2_
  63.6 0.7 share.2
  64.4 0.1 collective-permute-start.8
  64.4 1.3 collective-permute-done.8.back_ref
  65.8 0.8 corner.2
  66.5 0.2 collective-permute-start.12
  66.7 1.9 %collective-permute-start.13 = (f32[2,1024]{1,0:T(2,128)S(1)}, f32[2,1024]{1,0:T(2,128)S(1)}, u32[]{:S(2)}, u32[]{:S(2)}) collective-permute-start(f32[2,1024]{1,0:T(2,128)S(1)} %get-tuple-element.67), channel_id=1, source_target_pairs={{0,2},{1,3},{2,0},{3,1},{4,6},{5,7},{6,4},{7,5},{8,10},{9,11},{10,... | collective-permute-start | bytes 24584 | tf_op jit(solution)/shard_map/ppermute | solution.py:722
  68.6 0.0 collective-permute-done.9.rest_0_
  68.6 1.4 %collective-permute-start.14 = (f32[2,1024]{1,0:T(2,128)S(1)}, f32[2,1024]{1,0:T(2,128)S(1)}, u32[]{:S(2)}, u32[]{:S(2)}) collective-permute-start(f32[2,1024]{1,0:T(2,128)S(1)} %get-tuple-element.68), channel_id=1, source_target_pairs={{0,3},{1,0},{2,1},{3,2},{4,7},{5,4},{6,5},{7,6},{8,11},{9,8},{10,9... | collective-permute-start | bytes 24584 | tf_op jit(solution)/shard_map/ppermute | solution.py:722
  70.0 0.0 collective-permute-done.10.rest_1_
  70.0 1.1 collective-permute-done.12.rest_3_
  71.1 1.1 collective-permute-done.14.rest_5_
  72.2 9.6 %update.2 = (f32[32,64,1024]{2,1,0:T(8,128)S(1)}, f32[32,1024]{1,0:T(8,128)S(1)}, f32[32,1024]{1,0:T(8,128)S(1)}, f32[64,1024]{1,0:T(8,128)S(1)}, f32[64,1024]{1,0:T(8,128)S(1)}) custom-call(s32[2]{0:T(128)S(1)} %pad_add_fusion.ids_ref, f32[16,128]{1,0:T(8,128)S(1)} %get-tuple-element.47.scal_ref, f32[32,64,1024]{2,1,0:T(8,128)S(1)} %get-tuple-element.54.t_ref, ...), custom_call_target="tpu_custom_call" | custom-call | tf_op jit(solution)/shard_map/update/pallas_call | solution.py:69
  81.9 21.3 %explicit.3 = (f32[32,64,1024]{2,1,0:T(8,128)S(1)}, f32[32,8,1024]{2,1,0:T(8,128)S(1)}, f32[2,16,1024]{2,1,0:T(8,128)S(1)}, f32[2,16,1024]{2,1,0:T(8,128)S(1)}, ...) custom-call(s32[2]{0:T(128)S(1)} %pad_add_fusion.ids_ref, ...), custom_call_target="tpu_custom_call" | custom-call | tf_op jit(solution)/shard_map/explicit/pallas_call | solution.py:69
  103.1 0.1 collective-permute-start.15
  103.2 1.3 collective-permute-done.15.other_ref
  104.6 0.7 chip.3
  105.3 0.7 collective-permute-start.16
  106.0 2.4 %collective-permute-start.20 = (f32[64,1024]{1,0:T(8,128)S(1)}, f32[64,1024]{1,0:T(8,128)S(1)}, u32[]{:S(2)}, u32[]{:S(2)}) collective-permute-start(f32[64,1024]{1,0:T(8,128)S(1)} %get-tuple-element.83), channel_id=1, source_target_pairs={{0,1},{1,2},{2,3},{3,0},{4,5},{5,6},{6,7},{7,4},{8,9},{9,10},{10,1... | collective-permute-start | bytes 786440 | tf_op jit(solution)/shard_map/ppermute | solution.py:694
  108.4 0.5 collective-permute-start.21
  108.9 1.0 collective-permute-start.22
  109.9 3.0 %collective-permute-start.17 = (f32[16,1024]{1,0:T(8,128)S(1)}, f32[16,1024]{1,0:T(8,128)S(1)}, u32[]{:S(2)}, u32[]{:S(2)}) collective-permute-start(f32[16,1024]{1,0:T(8,128)S(1)} %get-tuple-element.79), channel_id=1, source_target_pairs={{0,16},{4,20},{8,24},{12,28},{16,0},{20,4},{24,8},{28,12},{1,17},{... | collective-permute-start | bytes 196616 | tf_op jit(solution)/shard_map/ppermute | solution.py:704
  112.8 0.2 collective-permute-start.18
  113.0 3.3 %collective-permute-done.17.rest_1_ = f32[16,1024]{1,0:T(8,128)S(1)} collective-permute-done((f32[16,1024]{1,0:T(8,128)S(1)}, f32[16,1024]{1,0:T(8,128)S(1)}, u32[]{:S(2)}, u32[]{:S(2)}) %collective-permute-start.17) | collective-permute-done | bytes 65568 | tf_op jit(solution)/shard_map/ppermute | solution.py:704
  116.3 0.8 collective-permute-done.18.rest_2_
  117.1 0.7 share.3
  117.8 0.1 collective-permute-start.19
  117.9 1.3 collective-permute-done.19.back_ref
  119.2 0.8 corner.3
  120.0 1.2 collective-permute-start.23
  121.2 1.5 %collective-permute-start.24 = (f32[2,1024]{1,0:T(2,128)S(1)}, f32[2,1024]{1,0:T(2,128)S(1)}, u32[]{:S(2)}, u32[]{:S(2)}) collective-permute-start(f32[2,1024]{1,0:T(2,128)S(1)} %get-tuple-element.87), channel_id=1, source_target_pairs={{0,2},{1,3},{2,0},{3,1},{4,6},{5,7},{6,4},{7,5},{8,10},{9,11},{10,... | collective-permute-start | bytes 24584 | tf_op jit(solution)/shard_map/ppermute | solution.py:722
  122.7 1.4 %collective-permute-start.25 = (f32[2,1024]{1,0:T(2,128)S(1)}, f32[2,1024]{1,0:T(2,128)S(1)}, u32[]{:S(2)}, u32[]{:S(2)}) collective-permute-start(f32[2,1024]{1,0:T(2,128)S(1)} %get-tuple-element.88), channel_id=1, source_target_pairs={{0,3},{1,0},{2,1},{3,2},{4,7},{5,4},{6,5},{7,6},{8,11},{9,8},{10,9... | collective-permute-start | bytes 24584 | tf_op jit(solution)/shard_map/ppermute | solution.py:722
  124.1 0.5 collective-permute-done.23.rest_3_
  124.6 0.2 collective-permute-done.24.rest_4_
  124.8 1.5 %collective-permute-done.25.rest_5_ = f32[2,1024]{1,0:T(2,128)S(1)} collective-permute-done((f32[2,1024]{1,0:T(2,128)S(1)}, f32[2,1024]{1,0:T(2,128)S(1)}, u32[]{:S(2)}, u32[]{:S(2)}) %collective-permute-start.25) | collective-permute-done | bytes 8224 | tf_op jit(solution)/shard_map/ppermute | solution.py:722
  126.3 7.8 %update.3 = f32[32,64,1024]{2,1,0:T(8,128)} custom-call(s32[2]{0:T(128)S(1)} %pad_add_fusion.ids_ref, f32[16,128]{1,0:T(8,128)S(1)} %get-tuple-element.47.scal_ref, f32[32,64,1024]{2,1,0:T(8,128)S(1)} %get-tuple-element.74.t_ref, f32[32,64,1024]{2,1,0:T(8,128)S(1)} %get-tuple-element.69.rest_0_.u_ref, f32[32,8,1024]{2,1,0:T(8,128)S(1)} %get-tuple-element.75.edge_ref, ...), custom_call_target="tpu_custom_call" | custom-call | tf_op jit(solution)/shard_map/update/pallas_call | solution.py:69
  (23 shorter events, 0.1 us)
Async XLA Ops:
  1.1 18.6 %collective-permute-start.3 = (f32[64,1024]{1,0:T(8,128)S(1)}, f32[64,1024]{1,0:T(8,128)S(1)}, u32[]{:S(2)}, u32[]{:S(2)}) collective-permute-start(f32[64,1024]{1,0:T(8,128)S(1)} %get-tuple-element.89), channel_id=1, source_target_pairs={{1,0},{2,1},{3,2},{5,4},{6,5},{7,6},{9,8},{10,9},{11,10},{13,12},{... | collective-permute-start | bytes 786440 | tf_op jit(solution)/shard_map/ppermute | solution.py:670
  2.4 17.3 %collective-permute-start.2 = (f32[64,1024]{1,0:T(8,128)S(1)}, f32[64,1024]{1,0:T(8,128)S(1)}, u32[]{:S(2)}, u32[]{:S(2)}) collective-permute-start(f32[64,1024]{1,0:T(8,128)S(1)} %get-tuple-element.90), channel_id=1, source_target_pairs={{0,1},{1,2},{2,3},{4,5},{5,6},{6,7},{8,9},{9,10},{10,11},{12,13},{... | collective-permute-start | bytes 786440 | tf_op jit(solution)/shard_map/ppermute | solution.py:669
  9.7 10.0 %collective-permute-start = (f32[32,1024]{1,0:T(8,128)S(1)}, f32[32,1024]{1,0:T(8,128)S(1)}, u32[]{:S(2)}, u32[]{:S(2)}) collective-permute-start(f32[32,1024]{1,0:T(8,128)S(1)} %bitcast.15), channel_id=1, source_target_pairs={{0,4},{4,8},{8,12},{12,16},{16,20},{20,24},{24,28},{1,5},{5,9},{9,... | collective-permute-start | bytes 393224 | tf_op jit(solution)/shard_map/ppermute | solution.py:667
  11.2 8.5 %collective-permute-start.1 = (f32[32,1024]{1,0:T(8,128)S(1)}, f32[32,1024]{1,0:T(8,128)S(1)}, u32[]{:S(2)}, u32[]{:S(2)}) collective-permute-start(f32[32,1024]{1,0:T(8,128)S(1)} %bitcast.16), channel_id=1, source_target_pairs={{4,0},{8,4},{12,8},{16,12},{20,16},{24,20},{28,24},{5,1},{9,5},{13... | collective-permute-start | bytes 393224 | tf_op jit(solution)/shard_map/ppermute | solution.py:668
  19.7 0.9 copy-start
  20.6 1.0 copy-start.1
  21.6 1.0 copy-start.3
  22.7 0.8 copy-start.5
  45.2 4.3 %collective-permute-start.4 = (f32[2,16,1024]{2,1,0:T(8,128)S(1)}, f32[2,16,1024]{2,1,0:T(8,128)S(1)}, u32[]{:S(2)}, u32[]{:S(2)}) collective-permute-start(f32[2,16,1024]{2,1,0:T(8,128)S(1)} %get-tuple-element.57), channel_id=1, source_target_pairs={{0,4},{4,0},{8,12},{12,8},{16,20},{20,16},{24,28},{28,24},{1,5},{5... | collective-permute-start | bytes 393224 | tf_op jit(solution)/shard_map/ppermute | solution.py:695
  50.2 9.1 %collective-permute-start.5 = (f32[16,1024]{1,0:T(8,128)S(1)}, f32[16,1024]{1,0:T(8,128)S(1)}, u32[]{:S(2)}, u32[]{:S(2)}) collective-permute-start(f32[16,1024]{1,0:T(8,128)S(1)} %get-tuple-element.58), channel_id=1, source_target_pairs={{0,8},{4,12},{8,16},{12,20},{16,24},{20,28},{24,0},{28,4},{1,9},{5... | collective-permute-start | bytes 196616 | tf_op jit(solution)/shard_map/ppermute | solution.py:704
  52.3 16.3 %collective-permute-start.9 = (f32[64,1024]{1,0:T(8,128)S(1)}, f32[64,1024]{1,0:T(8,128)S(1)}, u32[]{:S(2)}, u32[]{:S(2)}) collective-permute-start(f32[64,1024]{1,0:T(8,128)S(1)} %get-tuple-element.63), channel_id=1, source_target_pairs={{0,1},{1,2},{2,3},{3,0},{4,5},{5,6},{6,7},{7,4},{8,9},{9,10},{10,1... | collective-permute-start | bytes 786440 | tf_op jit(solution)/shard_map/ppermute | solution.py:694
  54.6 15.4 %collective-permute-start.10 = (f32[64,1024]{1,0:T(8,128)S(1)}, f32[64,1024]{1,0:T(8,128)S(1)}, u32[]{:S(2)}, u32[]{:S(2)}) collective-permute-start(f32[64,1024]{1,0:T(8,128)S(1)} %get-tuple-element.64), channel_id=1, source_target_pairs={{0,2},{1,3},{2,0},{3,1},{4,6},{5,7},{6,4},{7,5},{8,10},{9,11},{10,... | collective-permute-start | bytes 786440 | tf_op jit(solution)/shard_map/ppermute | solution.py:694
  54.6 15.4 %collective-permute-start.11 = (f32[64,1024]{1,0:T(8,128)S(1)}, f32[64,1024]{1,0:T(8,128)S(1)}, u32[]{:S(2)}, u32[]{:S(2)}) collective-permute-start(f32[64,1024]{1,0:T(8,128)S(1)} %get-tuple-element.65), channel_id=1, source_target_pairs={{0,3},{1,0},{2,1},{3,2},{4,7},{5,4},{6,5},{7,6},{8,11},{9,8},{10,9... | collective-permute-start | bytes 786440 | tf_op jit(solution)/shard_map/ppermute | solution.py:694
  56.7 6.4 %collective-permute-start.6 = (f32[16,1024]{1,0:T(8,128)S(1)}, f32[16,1024]{1,0:T(8,128)S(1)}, u32[]{:S(2)}, u32[]{:S(2)}) collective-permute-start(f32[16,1024]{1,0:T(8,128)S(1)} %get-tuple-element.59), channel_id=1, source_target_pairs={{0,16},{4,20},{8,24},{12,28},{16,0},{20,4},{24,8},{28,12},{1,17},{... | collective-permute-start | bytes 196616 | tf_op jit(solution)/shard_map/ppermute | solution.py:704
  59.3 4.3 %collective-permute-start.7 = (f32[16,1024]{1,0:T(8,128)S(1)}, f32[16,1024]{1,0:T(8,128)S(1)}, u32[]{:S(2)}, u32[]{:S(2)}) collective-permute-start(f32[16,1024]{1,0:T(8,128)S(1)} %get-tuple-element.60), channel_id=1, source_target_pairs={{0,24},{4,28},{8,0},{12,4},{16,8},{20,12},{24,16},{28,20},{1,25},{... | collective-permute-start | bytes 196616 | tf_op jit(solution)/shard_map/ppermute | solution.py:704
  64.4 1.4 %collective-permute-start.8 = (f32[2,16,1024]{2,1,0:T(8,128)S(1)}, f32[2,16,1024]{2,1,0:T(8,128)S(1)}, u32[]{:S(2)}, u32[]{:S(2)}) collective-permute-start(f32[2,16,1024]{2,1,0:T(8,128)S(1)} %get-tuple-element.62), channel_id=1, source_target_pairs={{0,4},{4,0},{8,12},{12,8},{16,20},{20,16},{24,28},{28,24},{1,5},{5... | collective-permute-start | bytes 393224 | tf_op jit(solution)/shard_map/ppermute | solution.py:714
  66.5 4.6 %collective-permute-start.12 = (f32[2,1024]{1,0:T(2,128)S(1)}, f32[2,1024]{1,0:T(2,128)S(1)}, u32[]{:S(2)}, u32[]{:S(2)}) collective-permute-start(f32[2,1024]{1,0:T(2,128)S(1)} %get-tuple-element.66), channel_id=1, source_target_pairs={{0,1},{1,2},{2,3},{3,0},{4,5},{5,6},{6,7},{7,4},{8,9},{9,10},{10,1... | collective-permute-start | bytes 24584 | tf_op jit(solution)/shard_map/ppermute | solution.py:722
  66.7 4.5 %collective-permute-start.13 = (f32[2,1024]{1,0:T(2,128)S(1)}, f32[2,1024]{1,0:T(2,128)S(1)}, u32[]{:S(2)}, u32[]{:S(2)}) collective-permute-start(f32[2,1024]{1,0:T(2,128)S(1)} %get-tuple-element.67), channel_id=1, source_target_pairs={{0,2},{1,3},{2,0},{3,1},{4,6},{5,7},{6,4},{7,5},{8,10},{9,11},{10,... | collective-permute-start | bytes 24584 | tf_op jit(solution)/shard_map/ppermute | solution.py:722
  68.6 3.7 %collective-permute-start.14 = (f32[2,1024]{1,0:T(2,128)S(1)}, f32[2,1024]{1,0:T(2,128)S(1)}, u32[]{:S(2)}, u32[]{:S(2)}) collective-permute-start(f32[2,1024]{1,0:T(2,128)S(1)} %get-tuple-element.68), channel_id=1, source_target_pairs={{0,3},{1,0},{2,1},{3,2},{4,7},{5,4},{6,5},{7,6},{8,11},{9,8},{10,9... | collective-permute-start | bytes 24584 | tf_op jit(solution)/shard_map/ppermute | solution.py:722
  72.2 9.6 %copy-start.2 = (bf16[4,256,256]{2,1,0:T(8,128)(2,1)S(1)}, bf16[4,256,256]{2,1,0:T(8,128)(2,1)}, u32[]{:S(2)}) copy-start(bf16[4,256,256]{2,1,0:T(8,128)(2,1)} %get-tuple-element.50.rest_11_.rest_9_) | copy-start | bytes 1572868
  72.2 9.6 %copy-start.4 = (bf16[4,256,256]{2,1,0:T(8,128)(2,1)S(1)}, bf16[4,256,256]{2,1,0:T(8,128)(2,1)}, u32[]{:S(2)}) copy-start(bf16[4,256,256]{2,1,0:T(8,128)(2,1)} %get-tuple-element.51.rest_12_.rest_10_) | copy-start | bytes 1572868
  72.2 9.6 %copy-start.6 = (bf16[128,128]{1,0:T(8,128)(2,1)S(1)}, bf16[128,128]{1,0:T(8,128)(2,1)}, u32[]{:S(2)}) copy-start(bf16[128,128]{1,0:T(8,128)(2,1)} %get-tuple-element.49.rest_10_.rest_8_) | copy-start | bytes 98308
  103.1 1.4 %collective-permute-start.15 = (f32[2,16,1024]{2,1,0:T(8,128)S(1)}, f32[2,16,1024]{2,1,0:T(8,128)S(1)}, u32[]{:S(2)}, u32[]{:S(2)}) collective-permute-start(f32[2,16,1024]{2,1,0:T(8,128)S(1)} %get-tuple-element.77), channel_id=1, source_target_pairs={{0,4},{4,0},{8,12},{12,8},{16,20},{20,16},{24,28},{28,24},{1,5},{5... | collective-permute-start | bytes 393224 | tf_op jit(solution)/shard_map/ppermute | solution.py:695
  105.3 7.6 %collective-permute-start.16 = (f32[16,1024]{1,0:T(8,128)S(1)}, f32[16,1024]{1,0:T(8,128)S(1)}, u32[]{:S(2)}, u32[]{:S(2)}) collective-permute-start(f32[16,1024]{1,0:T(8,128)S(1)} %get-tuple-element.78), channel_id=1, source_target_pairs={{0,8},{4,12},{8,16},{12,20},{16,24},{20,28},{24,0},{28,4},{1,9},{5... | collective-permute-start | bytes 196616 | tf_op jit(solution)/shard_map/ppermute | solution.py:704
  106.0 16.7 %collective-permute-start.20 = (f32[64,1024]{1,0:T(8,128)S(1)}, f32[64,1024]{1,0:T(8,128)S(1)}, u32[]{:S(2)}, u32[]{:S(2)}) collective-permute-start(f32[64,1024]{1,0:T(8,128)S(1)} %get-tuple-element.83), channel_id=1, source_target_pairs={{0,1},{1,2},{2,3},{3,0},{4,5},{5,6},{6,7},{7,4},{8,9},{9,10},{10,1... | collective-permute-start | bytes 786440 | tf_op jit(solution)/shard_map/ppermute | solution.py:694
  108.4 15.7 %collective-permute-start.21 = (f32[64,1024]{1,0:T(8,128)S(1)}, f32[64,1024]{1,0:T(8,128)S(1)}, u32[]{:S(2)}, u32[]{:S(2)}) collective-permute-start(f32[64,1024]{1,0:T(8,128)S(1)} %get-tuple-element.84), channel_id=1, source_target_pairs={{0,2},{1,3},{2,0},{3,1},{4,6},{5,7},{6,4},{7,5},{8,10},{9,11},{10,... | collective-permute-start | bytes 786440 | tf_op jit(solution)/shard_map/ppermute | solution.py:694
  108.9 15.2 %collective-permute-start.22 = (f32[64,1024]{1,0:T(8,128)S(1)}, f32[64,1024]{1,0:T(8,128)S(1)}, u32[]{:S(2)}, u32[]{:S(2)}) collective-permute-start(f32[64,1024]{1,0:T(8,128)S(1)} %get-tuple-element.85), channel_id=1, source_target_pairs={{0,3},{1,0},{2,1},{3,2},{4,7},{5,4},{6,5},{7,6},{8,11},{9,8},{10,9... | collective-permute-start | bytes 786440 | tf_op jit(solution)/shard_map/ppermute | solution.py:694
  109.9 6.4 %collective-permute-start.17 = (f32[16,1024]{1,0:T(8,128)S(1)}, f32[16,1024]{1,0:T(8,128)S(1)}, u32[]{:S(2)}, u32[]{:S(2)}) collective-permute-start(f32[16,1024]{1,0:T(8,128)S(1)} %get-tuple-element.79), channel_id=1, source_target_pairs={{0,16},{4,20},{8,24},{12,28},{16,0},{20,4},{24,8},{28,12},{1,17},{... | collective-permute-start | bytes 196616 | tf_op jit(solution)/shard_map/ppermute | solution.py:704
  112.8 4.3 %collective-permute-start.18 = (f32[16,1024]{1,0:T(8,128)S(1)}, f32[16,1024]{1,0:T(8,128)S(1)}, u32[]{:S(2)}, u32[]{:S(2)}) collective-permute-start(f32[16,1024]{1,0:T(8,128)S(1)} %get-tuple-element.80), channel_id=1, source_target_pairs={{0,24},{4,28},{8,0},{12,4},{16,8},{20,12},{24,16},{28,20},{1,25},{... | collective-permute-start | bytes 196616 | tf_op jit(solution)/shard_map/ppermute | solution.py:704
  117.8 1.4 %collective-permute-start.19 = (f32[2,16,1024]{2,1,0:T(8,128)S(1)}, f32[2,16,1024]{2,1,0:T(8,128)S(1)}, u32[]{:S(2)}, u32[]{:S(2)}) collective-permute-start(f32[2,16,1024]{2,1,0:T(8,128)S(1)} %get-tuple-element.82), channel_id=1, source_target_pairs={{0,4},{4,0},{8,12},{12,8},{16,20},{20,16},{24,28},{28,24},{1,5},{5... | collective-permute-start | bytes 393224 | tf_op jit(solution)/shard_map/ppermute | solution.py:714
  120.0 4.6 %collective-permute-start.23 = (f32[2,1024]{1,0:T(2,128)S(1)}, f32[2,1024]{1,0:T(2,128)S(1)}, u32[]{:S(2)}, u32[]{:S(2)}) collective-permute-start(f32[2,1024]{1,0:T(2,128)S(1)} %get-tuple-element.86), channel_id=1, source_target_pairs={{0,1},{1,2},{2,3},{3,0},{4,5},{5,6},{6,7},{7,4},{8,9},{9,10},{10,1... | collective-permute-start | bytes 24584 | tf_op jit(solution)/shard_map/ppermute | solution.py:722
  121.2 3.7 %collective-permute-start.24 = (f32[2,1024]{1,0:T(2,128)S(1)}, f32[2,1024]{1,0:T(2,128)S(1)}, u32[]{:S(2)}, u32[]{:S(2)}) collective-permute-start(f32[2,1024]{1,0:T(2,128)S(1)} %get-tuple-element.87), channel_id=1, source_target_pairs={{0,2},{1,3},{2,0},{3,1},{4,6},{5,7},{6,4},{7,5},{8,10},{9,11},{10,... | collective-permute-start | bytes 24584 | tf_op jit(solution)/shard_map/ppermute | solution.py:722
  122.7 3.7 %collective-permute-start.25 = (f32[2,1024]{1,0:T(2,128)S(1)}, f32[2,1024]{1,0:T(2,128)S(1)}, u32[]{:S(2)}, u32[]{:S(2)}) collective-permute-start(f32[2,1024]{1,0:T(2,128)S(1)} %get-tuple-element.88), channel_id=1, source_target_pairs={{0,3},{1,0},{2,1},{3,2},{4,7},{5,4},{6,5},{7,6},{8,11},{9,8},{10,9... | collective-permute-start | bytes 24584 | tf_op jit(solution)/shard_map/ppermute | solution.py:722

commit v4 on v3

--- a/solution.py
+++ b/solution.py
@@ -14,6 +14,7 @@
 SUB = 8
 XB = 256
 ZB = 8
+PAIR = 2
 VL1 = 30
 VL2 = 20
 
@@ -111,19 +112,21 @@
 
 def tables_kernel(
     ids_ref, ax_ref, lower_ref, lpiv_ref, upper_ref, upiv_ref, ay_ref, az_ref,
-    cy_ref, cz_ref,
+    cond_ref,
     axh_ref, axl_ref, xlo_ref, xhi_ref, wide_ref, mat_ref, scal_ref,
-    *, rows, depth, ny, nz,
+    *, rows, depth, ny, nz, widths,
 ):
+    nx, wy, wz = widths
     e = pl.program_id(0)
     last = pl.num_programs(0) - 1
     high, low = split(ax_ref[...].T)
-    axh_ref[0] = high
-    axl_ref[0] = low
+    axh_ref[e] = high
+    axl_ref[e] = low
+    cols = pl.ds(pl.multiple_of(e * XB, XB), XB)
     from_low = lower_ref[...].T[LANES - 1 :] / lpiv_ref[SUB - 1 :, LANES - 1 :]
     from_high = upper_ref[...].T[:1] / upiv_ref[:1, :1]
-    xlo_ref[...] = jnp.where(e > 0, from_low, 0.0)
-    xhi_ref[...] = jnp.where(e < last, from_high, 0.0)
+    xlo_ref[:, cols] = jnp.where(e > 0, from_low, 0.0)
+    xhi_ref[:, cols] = jnp.where(e < last, from_high, 0.0)
 
     @pl.when(e == 0)
     def _():
@@ -151,7 +154,7 @@
         )
         wide_ref[0] = jnp.broadcast_to(lo, (rows + SUB, LANES))
         wide_ref[1] = jnp.broadcast_to(hi, (rows + SUB, LANES))
-        cy = pltpu.roll(cy_ref[...], lax.rem(cy_ref.shape[1] - y0, cy_ref.shape[1]), 1)
+        cy = pltpu.roll(cond_ref[:, nx : nx + wy], lax.rem(wy - y0, wy), 1)
         cy = jnp.broadcast_to(cy[:, :LANES], (LANES, LANES)).T
         wide_ref[2] = cy[1 : rows + 1 + SUB]
         wide_ref[3] = cy[: rows + SUB]
@@ -177,7 +180,7 @@
         row(DOWN, pick(-1) / diag)
         row(SUM_UP, zs[SUB + depth - 1 : SUB + depth])
         row(SUM_DOWN, zs[SUB : SUB + 1])
-        cz = pltpu.roll(cz_ref[...], lax.rem(cz_ref.shape[1] - z0, cz_ref.shape[1]), 1)
+        cz = pltpu.roll(cond_ref[:, nx + wy :], lax.rem(wz - z0, wz), 1)
         row(COND, cz)
 
         lane = lax.broadcasted_iota(jnp.int32, (1, LANES), 1)
@@ -243,19 +246,18 @@
         fill(LINES, values)
 
 
-def tables(ids, inverse_x, inverse_y, inverse_z, cond_y, cond_z, rows, depth):
+def tables(ids, inverse_x, inverse_y, inverse_z, conds, widths, rows, depth):
     nx = inverse_x.shape[0]
     blocks = nx // XB
     ny, nz = lax.axis_size("gy"), lax.axis_size("gz")
     q, s = XB // LANES, XB // SUB
-    round_up = lambda n: -(-n // LANES) * LANES
-    cy = jnp.pad(cond_y, (1, round_up(cond_y.shape[0] + 2 + LANES) - cond_y.shape[0] - 1))[None]
-    cz = jnp.pad(cond_z, (1, round_up(cond_z.shape[0] + 2 + LANES) - cond_z.shape[0] - 1))[None]
     column = lambda at: pl.BlockSpec((XB, LANES), lambda e: (e, at(e)))
     low = lambda e: jnp.maximum(q * e - 1, 0)
     top = lambda e: jnp.minimum(q * e + q, q * blocks - 1)
     return call(
-        functools.partial(tables_kernel, rows=rows, depth=depth, ny=ny, nz=nz),
+        functools.partial(
+            tables_kernel, rows=rows, depth=depth, ny=ny, nz=nz, widths=widths
+        ),
         [
             shape(blocks, XB, XB, dtype=bf16),
             shape(blocks, XB, XB, dtype=bf16),
@@ -265,7 +267,7 @@
             shape(2 * rows, 2 * rows, dtype=bf16),
             shape(TABLE_ROWS, LANES),
         ],
-        (ids, inverse_x, inverse_x, inverse_x, inverse_x, inverse_x, inverse_y, inverse_z, cy, cz),
+        (ids, inverse_x, inverse_x, inverse_x, inverse_x, inverse_x, inverse_y, inverse_z, conds),
         grid=(blocks,),
         in_specs=[
             smem(),
@@ -276,17 +278,13 @@
             pl.BlockSpec(
                 (SUB, LANES), lambda e: (jnp.minimum(s * e + s, s * blocks - 1), top(e))
             ),
-            full(inverse_y), full(inverse_z), full(cy), full(cz),
+            full(inverse_y), full(inverse_z), full(conds),
         ],
         out_specs=[
-            pl.BlockSpec((1, XB, XB), lambda e: (e, 0, 0)),
-            pl.BlockSpec((1, XB, XB), lambda e: (e, 0, 0)),
-            pl.BlockSpec((1, XB), lambda e: (0, e)),
-            pl.BlockSpec((1, XB), lambda e: (0, e)),
-            full(shape(4, rows + SUB, LANES)),
-            full(shape(2 * rows, 2 * rows)),
+            *[VMEM_WHOLE] * 6,
             full(shape(TABLE_ROWS, LANES)),
         ],
+        resident=range(6),
         large=2**14,
         name="tables",
     )
@@ -298,12 +296,14 @@
     if resident:
         u_ref, *rest = rest
     else:
-        u_ref, below_ref, above_ref, *rest = rest
+        u_ref, above_ref, *rest = rest
     o_ref, ylo_ref, yhi_ref, zlo_ref, zhi_ref, cx_ref, wide_ref, *rest = rest
     ay_ref, axh_ref, axl_ref, xlo_ref, xhi_ref, *rest = rest
     t_ref, edge_ref, mine_ref, theirs_ref, *rest = rest
     pays = rest[: nz - 1]
-    rhs_ref, line_ref, sy_ref, sz_ref, low_ref, high_ref = rest[nz - 1 :]
+    even_ref, odd_ref, line_ref, other_ref, sy_ref, sz_ref, high_ref, flux_ref = rest[
+        nz - 1 :
+    ]
     step = pl.program_id(0)
     steps = pl.num_programs(0)
     zb, rows, nx = o_ref.shape
@@ -311,132 +311,118 @@
     blocks = nx // XB
     base_z = step * zb if resident else 0
     sub = lax.broadcasted_iota(jnp.int32, (SUB, nx), 0)
-
-    if resident:
-        under = u_ref[jnp.maximum(base_z - 1, 0)]
-        over = u_ref[jnp.minimum(base_z + zb, steps * zb - 1)]
-    else:
-        under, over = below_ref[0], above_ref[0]
-    low_ref[...] = jnp.where(step > 0, under, zlo_ref[...])
+    dot = functools.partial(jnp.dot, preferred_element_type=f32)
+
+    over = u_ref[jnp.minimum(base_z + zb, steps * zb - 1)] if resident else above_ref[0]
     high_ref[...] = jnp.where(step < steps - 1, over, zhi_ref[...])
 
-    def plane(z, below, above):
+    @pl.when(step == 0)
+    def _():
+        sz_ref[...] = jnp.zeros_like(sz_ref)
+        odd_ref[...] = jnp.zeros_like(odd_ref)
+        flux_ref[...] = (u_ref[0] - zlo_ref[...]) * scal_ref[COND, 0]
+
+    def plane(z, out_ref):
         zz = step * zb + z
-        c_dn = scal_ref[COND, zz]
         c_up = scal_ref[COND, zz + 1]
-        cx = jnp.broadcast_to(cx_ref[...], (SUB, nx))
-        before = jnp.broadcast_to(ylo_ref[pl.ds(zz, 1), :], (SUB, nx))
-        current = u_ref[base_z + z, :SUB, :]
-        down_roll = pltpu.roll(current, 1, 0)
+        cx = jnp.broadcast_to(cx_ref[:, :nx], (SUB, nx))
+
+        def get(r):
+            return u_ref[base_z + z, r * SUB : (r + 1) * SUB, :]
+
+        current = get(0)
+        first = current[:1] - ylo_ref[pl.ds(zz, 1), :]
+        first = first * wide_rows(wide_ref, (3, slice(0, 1)), nx)
+        before = jnp.broadcast_to(first, (SUB, nx))
         for r in range(tiles):
             own = slice(r * SUB, (r + 1) * SUB)
+            c = current
             if r + 1 < tiles:
-                following = u_ref[base_z + z, (r + 1) * SUB : (r + 2) * SUB, :]
-                up_next = pltpu.roll(following, SUB - 1, 0)
-                down_next = pltpu.roll(following, 1, 0)
+                current = get(r + 1)
+                up_next = pltpu.roll(current, SUB - 1, 0)
             else:
-                following = down_next = None
                 up_next = jnp.broadcast_to(yhi_ref[pl.ds(zz, 1), :], (SUB, nx))
-            c = current
-            down = jnp.where(sub == 0, before, down_roll)
             up = jnp.where(sub == SUB - 1, up_next, pltpu.roll(c, SUB - 1, 0))
             fx = (pltpu.roll(c, nx - 1, 1) - c) * cx
             total = fx - pltpu.roll(fx, 1, 1)
-            cup = wide_rows(wide_ref, (2, own), nx)
-            cdn = wide_rows(wide_ref, (3, own), nx)
-            total = total + ((up - c) * cup - (c - down) * cdn)
-            total = total + ((above(own) - c) * c_up - (c - below(own)) * c_dn)
+            fy = (up - c) * wide_rows(wide_ref, (2, own), nx)
+            rolled = pltpu.roll(fy, 1, 0)
+            total = total + (fy - jnp.where(sub == 0, before, rolled))
+            before = rolled
+            above = high_ref[own, :] if z == zb - 1 else u_ref[base_z + z + 1, own, :]
+            fz = (above - c) * c_up
+            total = total + (fz - flux_ref[own, :])
+            flux_ref[own, :] = fz
             o = o_ref[z, own, :]
             total = total + (REACTION * c) * (1.0 - c * c - 2.0 * o)
-            rhs_ref[pl.ds(pl.multiple_of(z * rows + r * SUB, SUB), SUB), :] = total
-            before = down_roll
-            current = following
-            down_roll = down_next
-
-    plane(0, lambda own: low_ref[own, :], lambda own: u_ref[base_z + 1, own, :])
-
-    def inner(z, carry):
-        plane(
-            z,
-            lambda own: u_ref[base_z + z - 1, own, :],
-            lambda own: u_ref[base_z + z + 1, own, :],
-        )
-        return carry
-
-    lax.fori_loop(1, zb - 1, inner, 0)
-    plane(zb - 1, lambda own: u_ref[base_z + zb - 2, own, :], lambda own: high_ref[own, :])
-
-    dot = functools.partial(jnp.dot, preferred_element_type=f32)
-    for e in range(blocks):
-        cols = slice(e * XB, (e + 1) * XB)
-        high, low = split(rhs_ref[:, cols])
-        line_ref[:, cols] = (
-            dot(high, axh_ref[e]) + dot(low, axh_ref[e]) + dot(high, axl_ref[e])
-        )
-    lows = [None]
-    for e in range(blocks - 1):
-        at = slice((e + 1) * XB - 1, (e + 1) * XB)
-        end = line_ref[:, at]
-        if lows[e] is not None:
-            end = end + lows[e] * xlo_ref[:, at]
-        lows.append(end)
-    highs = [None] * blocks
-    for e in reversed(range(1, blocks)):
-        at = slice(e * XB, e * XB + 1)
-        end = line_ref[:, at]
-        if highs[e] is not None:
-            end = end + highs[e] * xhi_ref[:, at]
-        highs[e - 1] = end
-    for e in range(blocks):
-        cols = slice(e * XB, (e + 1) * XB)
-        value = line_ref[:, cols]
-        if lows[e] is not None:
-            value = value + lows[e] * xlo_ref[:, cols]
-        if highs[e] is not None:
-            value = value + highs[e] * xhi_ref[:, cols]
-        line_ref[:, cols] = value
-
-    @pl.when(step == 0)
-    def _():
-        sz_ref[...] = jnp.zeros_like(sz_ref)
+            at = (z % PAIR) * rows + r * SUB
+            out_ref[at : at + SUB, :] = total
 
     y_low = scal_ref[MISC, Y_LOW]
     y_high = scal_ref[MISC, Y_HIGH]
 
-    def solve(z, carry):
-        zz = step * zb + z
-        base = pl.multiple_of(z * rows, rows)
-        high, low = split(line_ref[pl.ds(base, rows), :])
-        both = jnp.concatenate([high, low], axis=0)
-        result = dot(ay_ref[...], both)
-        value = result[:rows] + result[rows:]
-        t_ref[zz] = value
-        first, final = value[:1], value[rows - 1 :]
-        sy_ref[0, pl.ds(z, 1), :] = final
-        sy_ref[1, pl.ds(z, 1), :] = first
-        edge_ref[z, 0:1, :] = y_low * first
-        edge_ref[z, 1:2, :] = y_high * final
-        sz_ref[0] = sz_ref[0] + scal_ref[SUM_UP, zz] * value
-        sz_ref[1] = sz_ref[1] + scal_ref[SUM_DOWN, zz] * value
-        return carry
-
-    lax.fori_loop(0, zb, solve, 0, unroll=True)
-
-    half = mine_ref.shape[1]
-    part = (step * zb) // half
-    at = pl.ds(pl.multiple_of(step * zb - part * half, SUB), zb)
-    core = lax.rem(ids_ref[0], 2)
-
-    @pl.when(part == core)
-    def _():
-        mine_ref[:, at, :] = sy_ref[...]
-
-    @pl.when(part != core)
-    def _():
-        theirs_ref[:, at, :] = sy_ref[...]
+    def solves(first, in_ref, x_ref):
+        for e in range(blocks):
+            cols = slice(e * XB, (e + 1) * XB)
+            high, low = split(in_ref[:, cols])
+            x_ref[:, cols] = (
+                dot(high, axh_ref[e]) + dot(low, axh_ref[e]) + dot(high, axl_ref[e])
+            )
+        lows = [None]
+        for e in range(blocks - 1):
+            at = slice((e + 1) * XB - 1, (e + 1) * XB)
+            end = x_ref[:, at]
+            if lows[e] is not None:
+                end = end + lows[e] * xlo_ref[:, at]
+            lows.append(end)
+        highs = [None] * blocks
+        for e in reversed(range(1, blocks)):
+            at = slice(e * XB, e * XB + 1)
+            end = x_ref[:, at]
+            if highs[e] is not None:
+                end = end + highs[e] * xhi_ref[:, at]
+            highs[e - 1] = end
+        for e in range(blocks):
+            cols = slice(e * XB, (e + 1) * XB)
+            up_sum = sz_ref[0, :, cols]
+            down_sum = sz_ref[1, :, cols]
+            for i in range(PAIR):
+                zz = jnp.maximum(first + i, 0)
+                here = slice(i * rows, (i + 1) * rows)
+                value = x_ref[here, cols]
+                if lows[e] is not None:
+                    value = value + lows[e][here] * xlo_ref[:, cols]
+                if highs[e] is not None:
+                    value = value + highs[e][here] * xhi_ref[:, cols]
+                high, low = split(value)
+                result = dot(ay_ref[...], jnp.concatenate([high, low], axis=0))
+                value = result[:rows] + result[rows:]
+                t_ref[zz, :, cols] = value
+                bottom, top = value[:1], value[rows - 1 :]
+                sy_ref[0, pl.ds(zz, 1), cols] = top
+                sy_ref[1, pl.ds(zz, 1), cols] = bottom
+                edge_ref[zz, 0:1, cols] = y_low * bottom
+                edge_ref[zz, 1:2, cols] = y_high * top
+                up_sum = up_sum + scal_ref[SUM_UP, zz] * value
+                down_sum = down_sum + scal_ref[SUM_DOWN, zz] * value
+            sz_ref[0, :, cols] = up_sum
+            sz_ref[1, :, cols] = down_sum
+
+    parity = [(even_ref, line_ref), (odd_ref, other_ref)]
+    for k in range(zb // PAIR):
+        for i in range(PAIR):
+            plane(k * PAIR + i, parity[k % 2][0])
+        solves(step * zb + (k - 1) * PAIR, *parity[(k - 1) % 2])
 
     @pl.when(step == steps - 1)
     def _():
+        solves(step * zb + zb - PAIR, *parity[(zb // PAIR - 1) % 2])
+        half = mine_ref.shape[1]
+        core = lax.rem(ids_ref[0], 2)
+        near = pl.multiple_of(core * half, SUB)
+        far = pl.multiple_of((1 - core) * half, SUB)
+        mine_ref[...] = sy_ref[:, pl.ds(near, half), :]
+        theirs_ref[...] = sy_ref[:, pl.ds(far, half), :]
         for k in range(1, nz):
             higher = ids_ref[1] + k < nz
             pays[k - 1][...] = jnp.where(higher, sz_ref[0], sz_ref[1])
@@ -450,7 +436,6 @@
     steps = depth // zb
     half = depth // 2
     field = pl.BlockSpec((zb, rows, nx), lambda s: (s, 0, 0))
-    below = pl.BlockSpec((1, rows, nx), lambda s: (jnp.maximum(s * zb - 1, 0), 0, 0))
     above = pl.BlockSpec(
         (1, rows, nx), lambda s: (jnp.minimum(s * zb + zb, depth - 1), 0, 0)
     )
@@ -464,18 +449,16 @@
     return call(
         functools.partial(explicit_kernel, nz=nz, resident=resident),
         outs,
-        (ids, scal, *([u] if resident else [u, u, u]), o, *rest),
+        (ids, scal, *([u] if resident else [u, u]), o, *rest),
         grid=(steps,),
         in_specs=[smem(), smem()]
-        + ([VMEM_WHOLE] if resident else [field, below, above])
-        + [field, *map(full, rest)],
-        resident=(0,),
-        out_specs=[VMEM_WHOLE, pl.BlockSpec((zb, SUB, nx), lambda s: (s, 0, 0))]
-        + [full(a) for a in outs[2:]],
-        scratch_shapes=[
-            pltpu.VMEM((zb * rows, nx), f32),
-            pltpu.VMEM((zb * rows, nx), f32),
-            pltpu.VMEM((2, zb, nx), f32),
+        + ([VMEM_WHOLE] if resident else [field, above])
+        + [field, *map(full, halos), full(cx), *[VMEM_WHOLE] * 6],
+        resident=(0, 1),
+        out_specs=[VMEM_WHOLE, VMEM_WHOLE] + [full(a) for a in outs[2:]],
+        scratch_shapes=[pltpu.VMEM((PAIR * rows, nx), f32)] * 4
+        + [
+            pltpu.VMEM((2, depth, nx), f32),
             pltpu.VMEM((2, rows, nx), f32),
             pltpu.VMEM((rows, nx), f32),
             pltpu.VMEM((rows, nx), f32),
@@ -648,7 +631,7 @@
         (ids, scal, t, u, edge, keep, back, wide, ylo, yhi, zlo, zhi, *gots, *corners),
         grid=(tiles if final else tiles + 1,),
         in_specs=[
-            smem(), smem(), VMEM_WHOLE, VMEM_WHOLE if resident else field, full(edge), full(keep), full(back), full(wide),
+            smem(), smem(), VMEM_WHOLE, VMEM_WHOLE if resident else field, VMEM_WHOLE, full(keep), full(back), full(wide),
             full(ylo), full(yhi), tile, tile,
             *map(full, gots), *map(full, corners),
         ],
@@ -677,11 +660,20 @@
     half = depth // 2
     ids = jnp.stack([lax.axis_index("gy"), lax.axis_index("gz")])
     halos = halo(phase_field)
+    room = lambda n: -(-(n + 3 + LANES) // LANES) * LANES
+    wy, wz = room(cond_y.shape[0]), room(cond_z.shape[0])
+    conds = jnp.concatenate(
+        [
+            jnp.pad(cond_x, (0, 1)),
+            jnp.pad(cond_y, (1, wy - 1 - cond_y.shape[0])),
+            jnp.pad(cond_z, (1, wz - 1 - cond_z.shape[0])),
+        ]
+    )[None]
     *tabs, scal = tables(
-        ids, inverse_x, inverse_y, inverse_z, cond_y, cond_z, rows, depth
+        ids, inverse_x, inverse_y, inverse_z, conds, (nx, wy, wz), rows, depth
     )
     wide = tabs[4]
-    cx = jnp.pad(cond_x, (0, 1))[None]
+    cx = conds
     swap = [(i, i ^ 1) for i in range(ny)]
     u = phase_field
     for step in range(STEPS):

time: 135 us -> 130 us (0.963)
  local copies, waits for them, and re-layouts: 8.82 us -> 2.89 us
    unnamed x16 -> x2, local copies, waits for them, and re-layouts: 3.81 us -> 0.05 us
    pad x3 -> x0, local copies, waits for them, and re-layouts: 2.18 us -> none  [the longest x1 0.75 us: tables(): jnp.pad(cond_y, (1, round_up(cond_y.shape[0] + 2 + LANES) - cond_y.shape[...]
  transfers between devices with their start and end apart: 26 -> 26, of which waited for: 13 -> 13; matrix products, arithmetic and copies ran while one was open for 3% -> 2% of each run, Pallas kernels for 6% -> 5%
where the time goes in v4:
time: 130 us; the launch traced here: 129 us
  Pallas kernels  69.7 us (54%)
  starting transfers between devices  38.9 us (30%)
  waiting for transfers between devices  16.5 us (13%)
  local copies, waits for them, and re-layouts  2.89 us (2%)
    pallas_call x11, Pallas kernels, call(): pl.pallas_call(kernel, out_shape=out_shape, compiler_params=pltpu.Compile...  69.7 us
    ppermute x6, starting transfers between devices, body(): lax.ppermute(pays[k - 1], 'gy', cyclic(ny, k, 2))  9.86 us
    ppermute x6, starting transfers between devices, body(): gots.append(lax.ppermute(pays[k - 1], 'gz', cyclic(nz, k)))  8.32 us
    ppermute x6, starting transfers between devices, body(): lax.ppermute(pays[k - 1], 'gz', cyclic(nz, k))  7.55 us
    ppermute x6, waiting for transfers between devices, body(): lax.ppermute(pays[k - 1], 'gy', cyclic(ny, k, 2))  7.08 us
    ppermute x1, starting transfers between devices, halo(): zlo = lax.ppermute(u[-1], 'gz', up(nz))  5.52 us
    ppermute x6, waiting for transfers between devices, body(): lax.ppermute(pays[k - 1], 'gz', cyclic(nz, k))  4.44 us
    ppermute x2, starting transfers between devices, body(): other = lax.ppermute(theirs, 'gy', swap)  3.41 us
  transfers between devices with their start and end apart: 26, of which 13 were waited for; matrix products, arithmetic and copies ran while one was open for 2% of the time, Pallas kernels for 5%

profile of v4, /device:TPU:0, one launch (start us, length us, event | category | flops | bytes accessed | tf_op | source)
XLA Modules:
  0.0 129.1 jit_solution(8773216843347822817)
XLA Ops:
  0.0 1.1 slice_bitcast_fusion
  1.1 1.3 %collective-permute-start.3 = (f32[64,1024]{1,0:T(8,128)S(1)}, f32[64,1024]{1,0:T(8,128)S(1)}, u32[]{:S(2)}, u32[]{:S(2)}) collective-permute-start(f32[64,1024]{1,0:T(8,128)S(1)} %get-tuple-element.89), channel_id=1, source_target_pairs={{1,0},{2,1},{3,2},{5,4},{6,5},{7,6},{9,8},{10,9},{11,10},{13,12},{... | collective-permute-start | bytes 786440 | tf_op jit(solution)/shard_map/ppermute | solution.py:653
  2.4 5.5 %collective-permute-start.2 = (f32[64,1024]{1,0:T(8,128)S(1)}, f32[64,1024]{1,0:T(8,128)S(1)}, u32[]{:S(2)}, u32[]{:S(2)}) collective-permute-start(f32[64,1024]{1,0:T(8,128)S(1)} %get-tuple-element.90), channel_id=1, source_target_pairs={{0,1},{1,2},{2,3},{4,5},{5,6},{6,7},{8,9},{9,10},{10,11},{12,13},{... | collective-permute-start | bytes 786440 | tf_op jit(solution)/shard_map/ppermute | solution.py:652
  7.9 1.8 %fusion.1 = (f32[32,1,1024]{2,1,0:T(1,128)S(1)}, f32[32,1,1024]{2,1,0:T(1,128)S(1)}) fusion(f32[32,64,1024]{2,1,0:T(8,128)} %u_ref.1), kind=kLoop, calls=%fused_computation.12 | loop fusion | bytes 524288 | tf_op jit(solution)/shard_map/slice | solution.py:651
  9.7 1.5 %collective-permute-start = (f32[32,1024]{1,0:T(8,128)S(1)}, f32[32,1024]{1,0:T(8,128)S(1)}, u32[]{:S(2)}, u32[]{:S(2)}) collective-permute-start(f32[32,1024]{1,0:T(8,128)S(1)} %bitcast.12), channel_id=1, source_target_pairs={{0,4},{4,8},{8,12},{12,16},{16,20},{20,24},{24,28},{1,5},{5,9},{9,... | collective-permute-start | bytes 393224 | tf_op jit(solution)/shard_map/ppermute | solution.py:650
  11.2 1.3 %collective-permute-start.1 = (f32[32,1024]{1,0:T(8,128)S(1)}, f32[32,1024]{1,0:T(8,128)S(1)}, u32[]{:S(2)}, u32[]{:S(2)}) collective-permute-start(f32[32,1024]{1,0:T(8,128)S(1)} %bitcast.13), channel_id=1, source_target_pairs={{4,0},{8,4},{12,8},{16,12},{20,16},{24,20},{28,24},{5,1},{9,5},{13... | collective-permute-start | bytes 393224 | tf_op jit(solution)/shard_map/ppermute | solution.py:651
  12.5 0.8 select_maximum_fusion
  13.3 0.1 pad_add_fusion.ids_ref
  13.4 3.8 %tables.1 = (bf16[4,256,256]{2,1,0:T(8,128)(2,1)S(1)}, bf16[4,256,256]{2,1,0:T(8,128)(2,1)S(1)}, f32[1,1024]{1,0:T(1,128)S(1)}, f32[1,1024]{1,0:T(1,128)S(1)}, f...) custom-call(s32[2]{0:T(128)S(1)} %pad_add_fusion.ids_ref, f32[1024,1024]{1,0:T(8,128)} %upiv_ref.1, ...), custom_call_target="tpu_custom_call" | custom-call | tf_op jit(solution)/shard_map/tables/pallas_call | solution.py:70
  17.2 0.0 collective-permute-done.rest_3_.ylo_ref
  17.2 0.0 collective-permute-done.1.rest_4_.yhi_ref
  17.2 0.0 collective-permute-done.3.rest_6_.zhi_ref
  17.2 0.0 collective-permute-done.2.rest_5_.zlo_ref
  17.2 22.5 %explicit.2 = (f32[32,64,1024]{2,1,0:T(8,128)S(1)}, f32[32,8,1024]{2,1,0:T(8,128)S(1)}, f32[2,16,1024]{2,1,0:T(8,128)S(1)}, f32[2,16,1024]{2,1,0:T(8,128)S(1)}, ...) custom-call(s32[2]{0:T(128)S(1)} %pad_add_fusion.ids_ref, ...), custom_call_target="tpu_custom_call" | custom-call | tf_op jit(solution)/shard_map/explicit/pallas_call | solution.py:70
  39.7 3.3 %collective-permute-start.4 = (f32[2,16,1024]{2,1,0:T(8,128)S(1)}, f32[2,16,1024]{2,1,0:T(8,128)S(1)}, u32[]{:S(2)}, u32[]{:S(2)}) collective-permute-start(f32[2,16,1024]{2,1,0:T(8,128)S(1)} %get-tuple-element.57), channel_id=1, source_target_pairs={{0,4},{4,0},{8,12},{12,8},{16,20},{20,16},{24,28},{28,24},{1,5},{5... | collective-permute-start | bytes 393224 | tf_op jit(solution)/shard_map/ppermute | solution.py:687
  43.0 1.0 collective-permute-done.4.other_ref
  44.0 0.7 chip.2
  44.7 2.0 %collective-permute-start.5 = (f32[16,1024]{1,0:T(8,128)S(1)}, f32[16,1024]{1,0:T(8,128)S(1)}, u32[]{:S(2)}, u32[]{:S(2)}) collective-permute-start(f32[16,1024]{1,0:T(8,128)S(1)} %get-tuple-element.58), channel_id=1, source_target_pairs={{0,8},{4,12},{8,16},{12,20},{16,24},{20,28},{24,0},{28,4},{1,9},{5... | collective-permute-start | bytes 196616 | tf_op jit(solution)/shard_map/ppermute | solution.py:696
  46.7 2.4 %collective-permute-start.9 = (f32[64,1024]{1,0:T(8,128)S(1)}, f32[64,1024]{1,0:T(8,128)S(1)}, u32[]{:S(2)}, u32[]{:S(2)}) collective-permute-start(f32[64,1024]{1,0:T(8,128)S(1)} %get-tuple-element.63), channel_id=1, source_target_pairs={{0,1},{1,2},{2,3},{3,0},{4,5},{5,6},{6,7},{7,4},{8,9},{9,10},{10,1... | collective-permute-start | bytes 786440 | tf_op jit(solution)/shard_map/ppermute | solution.py:686
  49.1 0.0 collective-permute-start.10
  49.1 2.1 %collective-permute-start.11 = (f32[64,1024]{1,0:T(8,128)S(1)}, f32[64,1024]{1,0:T(8,128)S(1)}, u32[]{:S(2)}, u32[]{:S(2)}) collective-permute-start(f32[64,1024]{1,0:T(8,128)S(1)} %get-tuple-element.65), channel_id=1, source_target_pairs={{0,3},{1,0},{2,1},{3,2},{4,7},{5,4},{6,5},{7,6},{8,11},{9,8},{10,9... | collective-permute-start | bytes 786440 | tf_op jit(solution)/shard_map/ppermute | solution.py:686
  51.2 2.6 %collective-permute-start.6 = (f32[16,1024]{1,0:T(8,128)S(1)}, f32[16,1024]{1,0:T(8,128)S(1)}, u32[]{:S(2)}, u32[]{:S(2)}) collective-permute-start(f32[16,1024]{1,0:T(8,128)S(1)} %get-tuple-element.59), channel_id=1, source_target_pairs={{0,16},{4,20},{8,24},{12,28},{16,0},{20,4},{24,8},{28,12},{1,17},{... | collective-permute-start | bytes 196616 | tf_op jit(solution)/shard_map/ppermute | solution.py:696
  53.8 0.0 collective-permute-done.5.rest_0_
  53.8 1.3 %collective-permute-start.7 = (f32[16,1024]{1,0:T(8,128)S(1)}, f32[16,1024]{1,0:T(8,128)S(1)}, u32[]{:S(2)}, u32[]{:S(2)}) collective-permute-start(f32[16,1024]{1,0:T(8,128)S(1)} %get-tuple-element.60), channel_id=1, source_target_pairs={{0,24},{4,28},{8,0},{12,4},{16,8},{20,12},{24,16},{28,20},{1,25},{... | collective-permute-start | bytes 196616 | tf_op jit(solution)/shard_map/ppermute | solution.py:696
  55.1 2.5 %collective-permute-done.6.rest_1_ = f32[16,1024]{1,0:T(8,128)S(1)} collective-permute-done((f32[16,1024]{1,0:T(8,128)S(1)}, f32[16,1024]{1,0:T(8,128)S(1)}, u32[]{:S(2)}, u32[]{:S(2)}) %collective-permute-start.6) | collective-permute-done | bytes 65568 | tf_op jit(solution)/shard_map/ppermute | solution.py:696
  57.6 0.5 collective-permute-done.7.rest_2_
  58.1 0.7 share.2
  58.8 0.1 collective-permute-start.8
  58.9 1.3 %collective-permute-done.8.back_ref = f32[2,16,1024]{2,1,0:T(8,128)S(1)} collective-permute-done((f32[2,16,1024]{2,1,0:T(8,128)S(1)}, f32[2,16,1024]{2,1,0:T(8,128)S(1)}, u32[]{:S(2)}, u32[]{:S(2)}) %collective-permute-start.8) | collective-permute-done | bytes 131104 | tf_op jit(solution)/shard_map/ppermute | solution.py:706
  60.3 0.8 corner.2
  61.0 0.1 collective-permute-start.12
  61.2 1.9 %collective-permute-start.13 = (f32[2,1024]{1,0:T(2,128)S(1)}, f32[2,1024]{1,0:T(2,128)S(1)}, u32[]{:S(2)}, u32[]{:S(2)}) collective-permute-start(f32[2,1024]{1,0:T(2,128)S(1)} %get-tuple-element.67), channel_id=1, source_target_pairs={{0,2},{1,3},{2,0},{3,1},{4,6},{5,7},{6,4},{7,5},{8,10},{9,11},{10,... | collective-permute-start | bytes 24584 | tf_op jit(solution)/shard_map/ppermute | solution.py:714
  63.1 0.0 collective-permute-done.9.rest_0_
  63.1 1.5 %collective-permute-start.14 = (f32[2,1024]{1,0:T(2,128)S(1)}, f32[2,1024]{1,0:T(2,128)S(1)}, u32[]{:S(2)}, u32[]{:S(2)}) collective-permute-start(f32[2,1024]{1,0:T(2,128)S(1)} %get-tuple-element.68), channel_id=1, source_target_pairs={{0,3},{1,0},{2,1},{3,2},{4,7},{5,4},{6,5},{7,6},{8,11},{9,8},{10,9... | collective-permute-start | bytes 24584 | tf_op jit(solution)/shard_map/ppermute | solution.py:714
  64.5 0.0 collective-permute-done.10.rest_1_
  64.5 0.0 collective-permute-done.11.rest_2_
  64.5 1.1 collective-permute-done.12.rest_3_
  65.6 0.0 collective-permute-done.13.rest_4_
  65.6 1.1 collective-permute-done.14.rest_5_
  66.7 9.5 %update.2 = (f32[32,64,1024]{2,1,0:T(8,128)S(1)}, f32[32,1024]{1,0:T(8,128)S(1)}, f32[32,1024]{1,0:T(8,128)S(1)}, f32[64,1024]{1,0:T(8,128)S(1)}, f32[64,1024]{1,0:T(8,128)S(1)}) custom-call(s32[2]{0:T(128)S(1)} %pad_add_fusion.ids_ref, f32[16,128]{1,0:T(8,128)S(1)} %get-tuple-element.47.scal_ref, f32[32,64,1024]{2,1,0:T(8,128)S(1)} %get-tuple-element.54.t_ref, ...), custom_call_target="tpu_custom_call" | custom-call | tf_op jit(solution)/shard_map/update/pallas_call | solution.py:70
  76.2 21.8 %explicit.3 = (f32[32,64,1024]{2,1,0:T(8,128)S(1)}, f32[32,8,1024]{2,1,0:T(8,128)S(1)}, f32[2,16,1024]{2,1,0:T(8,128)S(1)}, f32[2,16,1024]{2,1,0:T(8,128)S(1)}, ...) custom-call(s32[2]{0:T(128)S(1)} %pad_add_fusion.ids_ref, ...), custom_call_target="tpu_custom_call" | custom-call | tf_op jit(solution)/shard_map/explicit/pallas_call | solution.py:70
  98.0 0.1 collective-permute-start.15
  98.1 1.3 %collective-permute-done.15.other_ref = f32[2,16,1024]{2,1,0:T(8,128)S(1)} collective-permute-done((f32[2,16,1024]{2,1,0:T(8,128)S(1)}, f32[2,16,1024]{2,1,0:T(8,128)S(1)}, u32[]{:S(2)}, u32[]{:S(2)}) %collective-permute-start.15) | collective-permute-done | bytes 131104 | tf_op jit(solution)/shard_map/ppermute | solution.py:687
  99.5 0.7 chip.3
  100.2 0.7 collective-permute-start.16
  100.9 2.4 %collective-permute-start.20 = (f32[64,1024]{1,0:T(8,128)S(1)}, f32[64,1024]{1,0:T(8,128)S(1)}, u32[]{:S(2)}, u32[]{:S(2)}) collective-permute-start(f32[64,1024]{1,0:T(8,128)S(1)} %get-tuple-element.83), channel_id=1, source_target_pairs={{0,1},{1,2},{2,3},{3,0},{4,5},{5,6},{6,7},{7,4},{8,9},{9,10},{10,1... | collective-permute-start | bytes 786440 | tf_op jit(solution)/shard_map/ppermute | solution.py:686
  103.3 0.5 collective-permute-start.21
  103.8 1.0 collective-permute-start.22
  104.8 3.0 %collective-permute-start.17 = (f32[16,1024]{1,0:T(8,128)S(1)}, f32[16,1024]{1,0:T(8,128)S(1)}, u32[]{:S(2)}, u32[]{:S(2)}) collective-permute-start(f32[16,1024]{1,0:T(8,128)S(1)} %get-tuple-element.79), channel_id=1, source_target_pairs={{0,16},{4,20},{8,24},{12,28},{16,0},{20,4},{24,8},{28,12},{1,17},{... | collective-permute-start | bytes 196616 | tf_op jit(solution)/shard_map/ppermute | solution.py:696
  107.8 0.0 collective-permute-done.16.rest_0_
  107.8 0.2 collective-permute-start.18
  107.9 3.3 %collective-permute-done.17.rest_1_ = f32[16,1024]{1,0:T(8,128)S(1)} collective-permute-done((f32[16,1024]{1,0:T(8,128)S(1)}, f32[16,1024]{1,0:T(8,128)S(1)}, u32[]{:S(2)}, u32[]{:S(2)}) %collective-permute-start.17) | collective-permute-done | bytes 65568 | tf_op jit(solution)/shard_map/ppermute | solution.py:696
  111.2 0.8 collective-permute-done.18.rest_2_
  112.0 0.7 share.3
  112.8 0.1 collective-permute-start.19
  112.8 1.3 %collective-permute-done.19.back_ref = f32[2,16,1024]{2,1,0:T(8,128)S(1)} collective-permute-done((f32[2,16,1024]{2,1,0:T(8,128)S(1)}, f32[2,16,1024]{2,1,0:T(8,128)S(1)}, u32[]{:S(2)}, u32[]{:S(2)}) %collective-permute-start.19) | collective-permute-done | bytes 131104 | tf_op jit(solution)/shard_map/ppermute | solution.py:706
  114.2 0.8 corner.3
  114.9 1.2 collective-permute-start.23
  116.1 1.5 %collective-permute-start.24 = (f32[2,1024]{1,0:T(2,128)S(1)}, f32[2,1024]{1,0:T(2,128)S(1)}, u32[]{:S(2)}, u32[]{:S(2)}) collective-permute-start(f32[2,1024]{1,0:T(2,128)S(1)} %get-tuple-element.87), channel_id=1, source_target_pairs={{0,2},{1,3},{2,0},{3,1},{4,6},{5,7},{6,4},{7,5},{8,10},{9,11},{10,... | collective-permute-start | bytes 24584 | tf_op jit(solution)/shard_map/ppermute | solution.py:714
  117.6 1.4 %collective-permute-start.25 = (f32[2,1024]{1,0:T(2,128)S(1)}, f32[2,1024]{1,0:T(2,128)S(1)}, u32[]{:S(2)}, u32[]{:S(2)}) collective-permute-start(f32[2,1024]{1,0:T(2,128)S(1)} %get-tuple-element.88), channel_id=1, source_target_pairs={{0,3},{1,0},{2,1},{3,2},{4,7},{5,4},{6,5},{7,6},{8,11},{9,8},{10,9... | collective-permute-start | bytes 24584 | tf_op jit(solution)/shard_map/ppermute | solution.py:714
  119.0 0.5 collective-permute-done.23.rest_3_
  119.5 0.2 collective-permute-done.24.rest_4_
  119.8 1.5 %collective-permute-done.25.rest_5_ = f32[2,1024]{1,0:T(2,128)S(1)} collective-permute-done((f32[2,1024]{1,0:T(2,128)S(1)}, f32[2,1024]{1,0:T(2,128)S(1)}, u32[]{:S(2)}, u32[]{:S(2)}) %collective-permute-start.25) | collective-permute-done | bytes 8224 | tf_op jit(solution)/shard_map/ppermute | solution.py:714
  121.3 7.8 %update.3 = f32[32,64,1024]{2,1,0:T(8,128)} custom-call(s32[2]{0:T(128)S(1)} %pad_add_fusion.ids_ref, f32[16,128]{1,0:T(8,128)S(1)} %get-tuple-element.47.scal_ref, f32[32,64,1024]{2,1,0:T(8,128)S(1)} %get-tuple-element.74.t_ref, f32[32,64,1024]{2,1,0:T(8,128)S(1)} %get-tuple-element.69.rest_0_.u_ref, f32[32,8,1024]{2,1,0:T(8,128)S(1)} %get-tuple-element.75.edge_ref, ...), custom_call_target="tpu_custom_call" | custom-call | tf_op jit(solution)/shard_map/update/pallas_call | solution.py:70
  (6 shorter events, 0.1 us)
Async XLA Ops:
  1.1 16.1 %collective-permute-start.3 = (f32[64,1024]{1,0:T(8,128)S(1)}, f32[64,1024]{1,0:T(8,128)S(1)}, u32[]{:S(2)}, u32[]{:S(2)}) collective-permute-start(f32[64,1024]{1,0:T(8,128)S(1)} %get-tuple-element.89), channel_id=1, source_target_pairs={{1,0},{2,1},{3,2},{5,4},{6,5},{7,6},{9,8},{10,9},{11,10},{13,12},{... | collective-permute-start | bytes 786440 | tf_op jit(solution)/shard_map/ppermute | solution.py:653
  2.4 14.8 %collective-permute-start.2 = (f32[64,1024]{1,0:T(8,128)S(1)}, f32[64,1024]{1,0:T(8,128)S(1)}, u32[]{:S(2)}, u32[]{:S(2)}) collective-permute-start(f32[64,1024]{1,0:T(8,128)S(1)} %get-tuple-element.90), channel_id=1, source_target_pairs={{0,1},{1,2},{2,3},{4,5},{5,6},{6,7},{8,9},{9,10},{10,11},{12,13},{... | collective-permute-start | bytes 786440 | tf_op jit(solution)/shard_map/ppermute | solution.py:652
  9.7 7.5 %collective-permute-start = (f32[32,1024]{1,0:T(8,128)S(1)}, f32[32,1024]{1,0:T(8,128)S(1)}, u32[]{:S(2)}, u32[]{:S(2)}) collective-permute-start(f32[32,1024]{1,0:T(8,128)S(1)} %bitcast.12), channel_id=1, source_target_pairs={{0,4},{4,8},{8,12},{12,16},{16,20},{20,24},{24,28},{1,5},{5,9},{9,... | collective-permute-start | bytes 393224 | tf_op jit(solution)/shard_map/ppermute | solution.py:650
  11.2 6.0 %collective-permute-start.1 = (f32[32,1024]{1,0:T(8,128)S(1)}, f32[32,1024]{1,0:T(8,128)S(1)}, u32[]{:S(2)}, u32[]{:S(2)}) collective-permute-start(f32[32,1024]{1,0:T(8,128)S(1)} %bitcast.13), channel_id=1, source_target_pairs={{4,0},{8,4},{12,8},{16,12},{20,16},{24,20},{28,24},{5,1},{9,5},{13... | collective-permute-start | bytes 393224 | tf_op jit(solution)/shard_map/ppermute | solution.py:651
  39.7 4.3 %collective-permute-start.4 = (f32[2,16,1024]{2,1,0:T(8,128)S(1)}, f32[2,16,1024]{2,1,0:T(8,128)S(1)}, u32[]{:S(2)}, u32[]{:S(2)}) collective-permute-start(f32[2,16,1024]{2,1,0:T(8,128)S(1)} %get-tuple-element.57), channel_id=1, source_target_pairs={{0,4},{4,0},{8,12},{12,8},{16,20},{20,16},{24,28},{28,24},{1,5},{5... | collective-permute-start | bytes 393224 | tf_op jit(solution)/shard_map/ppermute | solution.py:687
  44.7 9.1 %collective-permute-start.5 = (f32[16,1024]{1,0:T(8,128)S(1)}, f32[16,1024]{1,0:T(8,128)S(1)}, u32[]{:S(2)}, u32[]{:S(2)}) collective-permute-start(f32[16,1024]{1,0:T(8,128)S(1)} %get-tuple-element.58), channel_id=1, source_target_pairs={{0,8},{4,12},{8,16},{12,20},{16,24},{20,28},{24,0},{28,4},{1,9},{5... | collective-permute-start | bytes 196616 | tf_op jit(solution)/shard_map/ppermute | solution.py:696
  46.7 16.3 %collective-permute-start.9 = (f32[64,1024]{1,0:T(8,128)S(1)}, f32[64,1024]{1,0:T(8,128)S(1)}, u32[]{:S(2)}, u32[]{:S(2)}) collective-permute-start(f32[64,1024]{1,0:T(8,128)S(1)} %get-tuple-element.63), channel_id=1, source_target_pairs={{0,1},{1,2},{2,3},{3,0},{4,5},{5,6},{6,7},{7,4},{8,9},{9,10},{10,1... | collective-permute-start | bytes 786440 | tf_op jit(solution)/shard_map/ppermute | solution.py:686
  49.1 15.4 %collective-permute-start.10 = (f32[64,1024]{1,0:T(8,128)S(1)}, f32[64,1024]{1,0:T(8,128)S(1)}, u32[]{:S(2)}, u32[]{:S(2)}) collective-permute-start(f32[64,1024]{1,0:T(8,128)S(1)} %get-tuple-element.64), channel_id=1, source_target_pairs={{0,2},{1,3},{2,0},{3,1},{4,6},{5,7},{6,4},{7,5},{8,10},{9,11},{10,... | collective-permute-start | bytes 786440 | tf_op jit(solution)/shard_map/ppermute | solution.py:686
  49.1 15.4 %collective-permute-start.11 = (f32[64,1024]{1,0:T(8,128)S(1)}, f32[64,1024]{1,0:T(8,128)S(1)}, u32[]{:S(2)}, u32[]{:S(2)}) collective-permute-start(f32[64,1024]{1,0:T(8,128)S(1)} %get-tuple-element.65), channel_id=1, source_target_pairs={{0,3},{1,0},{2,1},{3,2},{4,7},{5,4},{6,5},{7,6},{8,11},{9,8},{10,9... | collective-permute-start | bytes 786440 | tf_op jit(solution)/shard_map/ppermute | solution.py:686
  51.2 6.5 %collective-permute-start.6 = (f32[16,1024]{1,0:T(8,128)S(1)}, f32[16,1024]{1,0:T(8,128)S(1)}, u32[]{:S(2)}, u32[]{:S(2)}) collective-permute-start(f32[16,1024]{1,0:T(8,128)S(1)} %get-tuple-element.59), channel_id=1, source_target_pairs={{0,16},{4,20},{8,24},{12,28},{16,0},{20,4},{24,8},{28,12},{1,17},{... | collective-permute-start | bytes 196616 | tf_op jit(solution)/shard_map/ppermute | solution.py:696
  53.8 4.3 %collective-permute-start.7 = (f32[16,1024]{1,0:T(8,128)S(1)}, f32[16,1024]{1,0:T(8,128)S(1)}, u32[]{:S(2)}, u32[]{:S(2)}) collective-permute-start(f32[16,1024]{1,0:T(8,128)S(1)} %get-tuple-element.60), channel_id=1, source_target_pairs={{0,24},{4,28},{8,0},{12,4},{16,8},{20,12},{24,16},{28,20},{1,25},{... | collective-permute-start | bytes 196616 | tf_op jit(solution)/shard_map/ppermute | solution.py:696
  58.8 1.4 %collective-permute-start.8 = (f32[2,16,1024]{2,1,0:T(8,128)S(1)}, f32[2,16,1024]{2,1,0:T(8,128)S(1)}, u32[]{:S(2)}, u32[]{:S(2)}) collective-permute-start(f32[2,16,1024]{2,1,0:T(8,128)S(1)} %get-tuple-element.62), channel_id=1, source_target_pairs={{0,4},{4,0},{8,12},{12,8},{16,20},{20,16},{24,28},{28,24},{1,5},{5... | collective-permute-start | bytes 393224 | tf_op jit(solution)/shard_map/ppermute | solution.py:706
  61.0 4.6 %collective-permute-start.12 = (f32[2,1024]{1,0:T(2,128)S(1)}, f32[2,1024]{1,0:T(2,128)S(1)}, u32[]{:S(2)}, u32[]{:S(2)}) collective-permute-start(f32[2,1024]{1,0:T(2,128)S(1)} %get-tuple-element.66), channel_id=1, source_target_pairs={{0,1},{1,2},{2,3},{3,0},{4,5},{5,6},{6,7},{7,4},{8,9},{9,10},{10,1... | collective-permute-start | bytes 24584 | tf_op jit(solution)/shard_map/ppermute | solution.py:714
  61.2 4.5 %collective-permute-start.13 = (f32[2,1024]{1,0:T(2,128)S(1)}, f32[2,1024]{1,0:T(2,128)S(1)}, u32[]{:S(2)}, u32[]{:S(2)}) collective-permute-start(f32[2,1024]{1,0:T(2,128)S(1)} %get-tuple-element.67), channel_id=1, source_target_pairs={{0,2},{1,3},{2,0},{3,1},{4,6},{5,7},{6,4},{7,5},{8,10},{9,11},{10,... | collective-permute-start | bytes 24584 | tf_op jit(solution)/shard_map/ppermute | solution.py:714
  63.1 3.7 %collective-permute-start.14 = (f32[2,1024]{1,0:T(2,128)S(1)}, f32[2,1024]{1,0:T(2,128)S(1)}, u32[]{:S(2)}, u32[]{:S(2)}) collective-permute-start(f32[2,1024]{1,0:T(2,128)S(1)} %get-tuple-element.68), channel_id=1, source_target_pairs={{0,3},{1,0},{2,1},{3,2},{4,7},{5,4},{6,5},{7,6},{8,11},{9,8},{10,9... | collective-permute-start | bytes 24584 | tf_op jit(solution)/shard_map/ppermute | solution.py:714
  98.0 1.4 %collective-permute-start.15 = (f32[2,16,1024]{2,1,0:T(8,128)S(1)}, f32[2,16,1024]{2,1,0:T(8,128)S(1)}, u32[]{:S(2)}, u32[]{:S(2)}) collective-permute-start(f32[2,16,1024]{2,1,0:T(8,128)S(1)} %get-tuple-element.77), channel_id=1, source_target_pairs={{0,4},{4,0},{8,12},{12,8},{16,20},{20,16},{24,28},{28,24},{1,5},{5... | collective-permute-start | bytes 393224 | tf_op jit(solution)/shard_map/ppermute | solution.py:687
  100.2 7.6 %collective-permute-start.16 = (f32[16,1024]{1,0:T(8,128)S(1)}, f32[16,1024]{1,0:T(8,128)S(1)}, u32[]{:S(2)}, u32[]{:S(2)}) collective-permute-start(f32[16,1024]{1,0:T(8,128)S(1)} %get-tuple-element.78), channel_id=1, source_target_pairs={{0,8},{4,12},{8,16},{12,20},{16,24},{20,28},{24,0},{28,4},{1,9},{5... | collective-permute-start | bytes 196616 | tf_op jit(solution)/shard_map/ppermute | solution.py:696
  100.9 16.7 %collective-permute-start.20 = (f32[64,1024]{1,0:T(8,128)S(1)}, f32[64,1024]{1,0:T(8,128)S(1)}, u32[]{:S(2)}, u32[]{:S(2)}) collective-permute-start(f32[64,1024]{1,0:T(8,128)S(1)} %get-tuple-element.83), channel_id=1, source_target_pairs={{0,1},{1,2},{2,3},{3,0},{4,5},{5,6},{6,7},{7,4},{8,9},{9,10},{10,1... | collective-permute-start | bytes 786440 | tf_op jit(solution)/shard_map/ppermute | solution.py:686
  103.3 15.7 %collective-permute-start.21 = (f32[64,1024]{1,0:T(8,128)S(1)}, f32[64,1024]{1,0:T(8,128)S(1)}, u32[]{:S(2)}, u32[]{:S(2)}) collective-permute-start(f32[64,1024]{1,0:T(8,128)S(1)} %get-tuple-element.84), channel_id=1, source_target_pairs={{0,2},{1,3},{2,0},{3,1},{4,6},{5,7},{6,4},{7,5},{8,10},{9,11},{10,... | collective-permute-start | bytes 786440 | tf_op jit(solution)/shard_map/ppermute | solution.py:686
  103.8 15.2 %collective-permute-start.22 = (f32[64,1024]{1,0:T(8,128)S(1)}, f32[64,1024]{1,0:T(8,128)S(1)}, u32[]{:S(2)}, u32[]{:S(2)}) collective-permute-start(f32[64,1024]{1,0:T(8,128)S(1)} %get-tuple-element.85), channel_id=1, source_target_pairs={{0,3},{1,0},{2,1},{3,2},{4,7},{5,4},{6,5},{7,6},{8,11},{9,8},{10,9... | collective-permute-start | bytes 786440 | tf_op jit(solution)/shard_map/ppermute | solution.py:686
  104.8 6.5 %collective-permute-start.17 = (f32[16,1024]{1,0:T(8,128)S(1)}, f32[16,1024]{1,0:T(8,128)S(1)}, u32[]{:S(2)}, u32[]{:S(2)}) collective-permute-start(f32[16,1024]{1,0:T(8,128)S(1)} %get-tuple-element.79), channel_id=1, source_target_pairs={{0,16},{4,20},{8,24},{12,28},{16,0},{20,4},{24,8},{28,12},{1,17},{... | collective-permute-start | bytes 196616 | tf_op jit(solution)/shard_map/ppermute | solution.py:696
  107.8 4.3 %collective-permute-start.18 = (f32[16,1024]{1,0:T(8,128)S(1)}, f32[16,1024]{1,0:T(8,128)S(1)}, u32[]{:S(2)}, u32[]{:S(2)}) collective-permute-start(f32[16,1024]{1,0:T(8,128)S(1)} %get-tuple-element.80), channel_id=1, source_target_pairs={{0,24},{4,28},{8,0},{12,4},{16,8},{20,12},{24,16},{28,20},{1,25},{... | collective-permute-start | bytes 196616 | tf_op jit(solution)/shard_map/ppermute | solution.py:696
  112.8 1.4 %collective-permute-start.19 = (f32[2,16,1024]{2,1,0:T(8,128)S(1)}, f32[2,16,1024]{2,1,0:T(8,128)S(1)}, u32[]{:S(2)}, u32[]{:S(2)}) collective-permute-start(f32[2,16,1024]{2,1,0:T(8,128)S(1)} %get-tuple-element.82), channel_id=1, source_target_pairs={{0,4},{4,0},{8,12},{12,8},{16,20},{20,16},{24,28},{28,24},{1,5},{5... | collective-permute-start | bytes 393224 | tf_op jit(solution)/shard_map/ppermute | solution.py:706
  114.9 4.6 %collective-permute-start.23 = (f32[2,1024]{1,0:T(2,128)S(1)}, f32[2,1024]{1,0:T(2,128)S(1)}, u32[]{:S(2)}, u32[]{:S(2)}) collective-permute-start(f32[2,1024]{1,0:T(2,128)S(1)} %get-tuple-element.86), channel_id=1, source_target_pairs={{0,1},{1,2},{2,3},{3,0},{4,5},{5,6},{6,7},{7,4},{8,9},{9,10},{10,1... | collective-permute-start | bytes 24584 | tf_op jit(solution)/shard_map/ppermute | solution.py:714
  116.1 3.7 %collective-permute-start.24 = (f32[2,1024]{1,0:T(2,128)S(1)}, f32[2,1024]{1,0:T(2,128)S(1)}, u32[]{:S(2)}, u32[]{:S(2)}) collective-permute-start(f32[2,1024]{1,0:T(2,128)S(1)} %get-tuple-element.87), channel_id=1, source_target_pairs={{0,2},{1,3},{2,0},{3,1},{4,6},{5,7},{6,4},{7,5},{8,10},{9,11},{10,... | collective-permute-start | bytes 24584 | tf_op jit(solution)/shard_map/ppermute | solution.py:714
  117.6 3.7 %collective-permute-start.25 = (f32[2,1024]{1,0:T(2,128)S(1)}, f32[2,1024]{1,0:T(2,128)S(1)}, u32[]{:S(2)}, u32[]{:S(2)}) collective-permute-start(f32[2,1024]{1,0:T(2,128)S(1)} %get-tuple-element.88), channel_id=1, source_target_pairs={{0,3},{1,0},{2,1},{3,2},{4,7},{5,4},{6,5},{7,6},{8,11},{9,8},{10,9... | collective-permute-start | bytes 24584 | tf_op jit(solution)/shard_map/ppermute | solution.py:714
